TPU v7x, 32 devices: a whole 2x2x4 slice. The times are simulated.
32 devices in a mesh: mem: 4 (over y, x), tile: 8 (over z, core).
Axes of the slice: x: 2, y: 2, z: 4, core: 2. Of those that a mesh axis runs over, the one named last changes fastest.
Arguments:
- perturbations: bfloat16 [3, 256, 128, 256], P(None, 'mem', 'tile'), may hold values from -0.375 to 0.375
- control: float32 [256, 128, 256], P('mem', 'tile'), may hold values from -15 to 15
- innovation: float32 [3, 128, 256], P(None, 'tile'), may hold values from -6 to 6
- obs_weight: float32 [3, 128, 256], P(None, 'tile'), may hold values from 2 to 32
- diffusion: float32 [128, 256], P('tile'), may hold values from 0.04 to 0.18
- advection: float32 [128, 256], P('tile'), may hold values from 0.08 to 0.3
- upwind: int32 [128, 256], P('tile'), may hold values from 0 to 1
Outputs:
- gradient: float32 [256, 128, 256], P('mem', 'tile')
- hessian_product: float32 [256, 128, 256], P('mem', 'tile')
- step_length: float32 [], replicated
All inputs are finite; a program needn't handle non-finite values.
Results may differ from a plain program's by a relative error of at most 0.0003.
Values sent between devices are 32-bit elements; how exact they have to be, the bound alone decides.
No kernel may reach another device: no remote copies, remote signals or barrier semaphores. Data moves between devices by JAX's collectives and lax.ppermute only.
A program may use at most 64 MiB of HBM per device.

v0:
```python
import jax
import jax.numpy as jnp
from jax import lax
from jax.sharding import PartitionSpec as P

SWEEPS = 4


def extended_2(block, sides, width):
    for axis, dim in sides:
        count = lax.axis_size(axis)
        forward = [(i, i + 1) for i in range(count - 1)]
        backward = [(target, source) for source, target in forward]
        low = lax.ppermute(
            lax.slice_in_dim(block, block.shape[dim] - width, None, axis=dim), axis, forward
        )
        high = lax.ppermute(lax.slice_in_dim(block, 0, width, axis=dim), axis, backward)
        block = jnp.concatenate([low, block, high], axis=dim)
    return block


def column_pad(values):
    return jnp.pad(values, ((0, 0), (0, 0), (1, 1)))


def forward_core(extended, kappa_rows, advect_rows, upper_rows):
    center = extended[:, 1:-1]
    below = extended[:, 2:]
    above = extended[:, :-2]
    padded = column_pad(center)
    spread = below + above + padded[:, :, 2:] + padded[:, :, :-2] - 4.0 * center
    upwind_value = jnp.where(upper_rows, below, above)
    return center + kappa_rows * spread - advect_rows * (center - upwind_value)


def adjoint_core(center, carried, weighted_ext, lower_ext, upper_ext):
    weighted = weighted_ext[:, 1:-1]
    padded = column_pad(weighted)
    spread = (
        weighted_ext[:, 2:]
        + weighted_ext[:, :-2]
        + padded[:, :, 2:]
        + padded[:, :, :-2]
        - 4.0 * weighted
    )
    returned = lower_ext[:, 2:] + upper_ext[:, :-2]
    return center + spread - carried + returned


def shards(perturbations, control, innovation, obs_weight, diffusion, advection, upwind):
    row_count = control.shape[1]
    upper = upwind == 1
    stacked_coeff = jnp.stack([diffusion, advection, upper.astype(jnp.float32)])
    coefficients = extended_2(stacked_coeff, (("tile", 1),), SWEEPS)
    kappa_wide = coefficients[0]
    advect_wide = coefficients[1]
    upper_wide = coefficients[2] > 0.5
    global_rows = (
        lax.axis_index("tile") * row_count
        + jnp.arange(row_count + 2 * SWEEPS, dtype=jnp.int32)
        - SWEEPS
    )
    inside = ((global_rows >= 0) & (global_rows < row_count * lax.axis_size("tile"))).astype(
        jnp.float32
    )[:, None]

    def localise(values):
        extended = extended_2(values, (("tile", 1),), SWEEPS)
        for repeat in range(SWEEPS):
            first_row = repeat + 1
            last_row = row_count + 2 * SWEEPS - repeat - 1
            extended = (
                forward_core(
                    extended,
                    kappa_wide[first_row:last_row],
                    advect_wide[first_row:last_row],
                    upper_wide[first_row:last_row],
                )
                * inside[first_row:last_row]
            )
        return extended

    def localise_adjoint(values):
        extended = extended_2(values, (("tile", 1),), SWEEPS)
        for repeat in range(SWEEPS):
            last_row = row_count + 2 * SWEEPS - repeat
            upper_part = upper_wide[repeat:last_row]
            carried = advect_wide[repeat:last_row] * extended
            weighted = kappa_wide[repeat:last_row] * extended
            lower_ext = jnp.where(upper_part, 0.0, carried)
            upper_ext = jnp.where(upper_part, carried, 0.0)
            extended = (
                adjoint_core(extended[:, 1:-1], carried[:, 1:-1], weighted, lower_ext, upper_ext)
                * inside[repeat + 1 : last_row - 1]
            )
        return extended

    def project(values):
        return jnp.sum(perturbations.astype(jnp.float32) * values[None], axis=1)

    def pull_back(weights_time):
        return jnp.sum(perturbations.astype(jnp.float32) * weights_time[:, None], axis=0)

    def misfit_of(partial_value, subtract):
        total = lax.psum(partial_value, "mem")
        if subtract:
            whole_misfit = obs_weight * (total - innovation)
        else:
            whole_misfit = obs_weight * total
        local_term = jnp.where(lax.axis_index("mem") == 0, jnp.sum(total * whole_misfit), 0.0)
        return (whole_misfit, local_term)

    misfit, unused_term = misfit_of(project(localise(control)), True)
    gradient = control + localise_adjoint(pull_back(misfit))
    weighted_image, curvature_term = misfit_of(project(localise(gradient)), False)
    hessian_product = gradient + localise_adjoint(pull_back(weighted_image))
    squares, obs_total = lax.psum((jnp.sum(gradient * gradient), curvature_term), ("mem", "tile"))
    return (gradient, hessian_product, squares / (squares + obs_total))


def solution(mesh):
    return jax.shard_map(
        shards,
        mesh=mesh,
        in_specs=(
            P(None, "mem", "tile", None),
            P("mem", "tile", None),
            P(None, "tile", None),
            P(None, "tile", None),
            P("tile", None),
            P("tile", None),
            P("tile", None),
        ),
        out_specs=(P("mem", "tile", None), P("mem", "tile", None), P()),
        check_vma=False,
    )
```

profile of v0, /device:TPU:0, one launch (start us, length us, event | category | flops | bytes accessed | tf_op | source)
XLA Modules:
  0.0 154.4 jit_solution(899908008557257718)
XLA Ops:
  2.2 2.4 %collective-permute-start.2 = (f32[3,4,256]{2,1,0:T(4,128)S(1)}, f32[3,4,256]{2,1,0:T(4,128)S(1)}, u32[]{:S(2)}, u32[]{:S(2)}) collective-permute-start(f32[3,4,256]{2,1,0:T(4,128)S(1)} %get-tuple-element.43), channel_id=1, source_target_pairs={{0,1},{1,2},{2,3},{3,4},{4,5},{5,6},{6,7},{8,9},{9,10},{10,11},{11... | collective-permute-start | bytes 36872 | tf_op jit(solution)/shard_map/ppermute | solution.py:14
  4.6 1.3 collective-permute-start.3
  5.9 1.3 fusion.136
  7.2 5.2 %collective-permute-start = (f32[64,4,256]{2,1,0:T(4,128)S(1)}, f32[64,4,256]{2,1,0:T(4,128)S(1)}, u32[]{:S(2)}, u32[]{:S(2)}) collective-permute-start(f32[64,4,256]{2,1,0:T(4,128)S(1)} %get-tuple-element.33), channel_id=1, source_target_pairs={{0,1},{1,2},{2,3},{3,4},{4,5},{5,6},{6,7},{8,9},{9,10},{10,11},{11... | collective-permute-start | bytes 786440 | tf_op jit(solution)/shard_map/ppermute | solution.py:14
  12.4 1.3 collective-permute-start.1
  15.0 2.1 %collective-permute-done.1 = f32[64,4,256]{2,1,0:T(4,128)S(1)} collective-permute-done((f32[64,4,256]{2,1,0:T(4,128)S(1)}, f32[64,4,256]{2,1,0:T(4,128)S(1)}, u32[]{:S(2)}, u32[]{:S(2)}) %collective-permute-start.1) | collective-permute-done | bytes 262176 | tf_op jit(solution)/shard_map/ppermute | solution.py:17
  17.5 1.5 fusion.10
  19.2 1.5 fusion.17
  20.9 1.5 fusion.24
  24.9 16.7 %psum.28 = f32[3,16,256]{2,1,0:T(8,128)S(1)} all-reduce(f32[3,16,256]{2,1,0:T(8,128)S(1)} %fusion), channel_id=1, replica_groups=mesh['mem'=4,'tile'=8] {'mem'}, use_global_device_ids=true, to_apply=%region_1.2 | all-reduce | flops 12288 | bytes 98304 | tf_op jit(solution)/shard_map/psum | solution.py:105
  42.1 3.2 %collective-permute-start.4 = (f32[64,4,256]{2,1,0:T(4,128)S(1)}, f32[64,4,256]{2,1,0:T(4,128)S(1)}, u32[]{:S(2)}, u32[]{:S(2)}) collective-permute-start(f32[64,4,256]{2,1,0:T(4,128)S(1)} %get-tuple-element.31), channel_id=1, source_target_pairs={{0,1},{1,2},{2,3},{3,4},{4,5},{5,6},{6,7},{8,9},{9,10},{10,11},{11... | collective-permute-start | bytes 786440 | tf_op jit(solution)/shard_map/ppermute | solution.py:14
  45.3 1.5 collective-permute-start.5
  46.9 4.8 %collective-permute-done.5 = f32[64,4,256]{2,1,0:T(4,128)S(1)} collective-permute-done((f32[64,4,256]{2,1,0:T(4,128)S(1)}, f32[64,4,256]{2,1,0:T(4,128)S(1)}, u32[]{:S(2)}, u32[]{:S(2)}) %collective-permute-start.5) | collective-permute-done | bytes 262176 | tf_op jit(solution)/shard_map/ppermute | solution.py:17
  52.2 1.4 broadcast_multiply_fusion.13
  53.9 1.4 broadcast_multiply_fusion.9
  55.5 1.4 broadcast_multiply_fusion.5
  58.2 1.8 %multiply_reduce_fusion = (f32[]{:T(128)}, f32[64,16,256]{2,1,0:T(8,128)S(1)}) fusion(f32[64,16,256]{2,1,0:T(8,128)S(1)} %copy-done.3, f32[16]{0:T(128)S(1)} %slice.537, f32[64,18,256]{2,1,0:T(8,128)S(1)} %get-tuple-element.15, pred[16,256]{1,0:T(8,128)(4,1)S(1)} %get-tuple-element.46, pred[16,256]{1,0:T(8,128)(4,1)S(1)} %get-tuple-element.45, ...), kind=kLoop, calls=%fused_computation.190 | loop fusion | flops 3932159 | bytes 9445444 | tf_op jit(solution)/shard_map/reduce_sum | solution.py:117
  60.1 6.7 %collective-permute-start.6 = (f32[64,4,256]{2,1,0:T(4,128)S(1)}, f32[64,4,256]{2,1,0:T(4,128)S(1)}, u32[]{:S(2)}, u32[]{:S(2)}) collective-permute-start(f32[64,4,256]{2,1,0:T(4,128)S(1)} %get-tuple-element.29), channel_id=1, source_target_pairs={{0,1},{1,2},{2,3},{3,4},{4,5},{5,6},{6,7},{8,9},{9,10},{10,11},{11... | collective-permute-start | bytes 786440 | tf_op jit(solution)/shard_map/ppermute | solution.py:14
  66.8 1.5 collective-permute-start.7
  68.3 1.9 %collective-permute-done.7 = f32[64,4,256]{2,1,0:T(4,128)S(1)} collective-permute-done((f32[64,4,256]{2,1,0:T(4,128)S(1)}, f32[64,4,256]{2,1,0:T(4,128)S(1)}, u32[]{:S(2)}, u32[]{:S(2)}) %collective-permute-start.7) | collective-permute-done | bytes 262176 | tf_op jit(solution)/shard_map/ppermute | solution.py:17
  70.6 1.5 fusion.52
  72.3 1.5 fusion.59
  74.0 1.5 fusion.66
  77.0 14.5 %psum.29 = f32[3,16,256]{2,1,0:T(8,128)S(1)} all-reduce(f32[3,16,256]{2,1,0:T(8,128)S(1)} %fusion.2), channel_id=1, replica_groups=mesh['mem'=4,'tile'=8] {'mem'}, use_global_device_ids=true, to_apply=%region_4.5 | all-reduce | flops 12288 | bytes 98304 | tf_op jit(solution)/shard_map/psum | solution.py:105
  93.6 2.5 %collective-permute-start.8 = (f32[64,4,256]{2,1,0:T(4,128)S(1)}, f32[64,4,256]{2,1,0:T(4,128)S(1)}, u32[]{:S(2)}, u32[]{:S(2)}) collective-permute-start(f32[64,4,256]{2,1,0:T(4,128)S(1)} %get-tuple-element.27), channel_id=1, source_target_pairs={{0,1},{1,2},{2,3},{3,4},{4,5},{5,6},{6,7},{8,9},{9,10},{10,11},{11... | collective-permute-start | bytes 786440 | tf_op jit(solution)/shard_map/ppermute | solution.py:14
  96.1 1.3 collective-permute-start.9
  98.0 44.5 %all-reduce.16 = (f32[]{:T(128)}, f32[]{:T(128)}) all-reduce(f32[]{:T(128)} %get-tuple-element.7, f32[]{:T(128)S(6)} %select_n.112), channel_id=1, replica_groups=mesh['mem'=4,'tile'=8] {'mem','tile'}, use_global_device_ids=true, to_apply=%region_7.8 | all-reduce | flops 2 | bytes 16 | tf_op jit(solution)/shard_map/psum | solution.py:117
  144.5 1.6 %pad_maximum_fusion.3 = (f32[64,24,256]{2,1,0:T(8,128)S(1)}, f32[64,24,256]{2,1,0:T(8,128)S(1)}, f32[64,24,256]{2,1,0:T(8,128)S(1)}) fusion(f32[64,4,256]{2,1,0:T(4,128)S(1)} %collective-permute-done.9, f32[64,16,256]{2,1,0:T(8,128)} %copy-done.4, f32[64,4,256]{2,1,0:T(4,128)S(1)} %collective-permute-done.8, f32[24,256]{1,0:T(8,128)S(1)} %get-tuple-element.35, ...), kind=kLoop, calls=%fused_computation.151 | loop fusion | flops 1572864 | bytes 6340608 | tf_op jit(solution)/shard_map/concatenate | solution.py:18
  146.3 1.4 broadcast_multiply_fusion.12
  147.9 1.4 broadcast_multiply_fusion.8
  149.5 1.4 broadcast_multiply_fusion.4
  151.2 2.1 %fusion.123 = f32[64,16,256]{2,1,0:T(8,128)} fusion(f32[64,16,256]{2,1,0:T(8,128)S(1)} %get-tuple-element.8, f32[64,16,256]{2,1,0:T(8,128)S(1)} %slice.747, f32[64,18,256]{2,1,0:T(8,128)S(1)} %get-tuple-element.9, f32[64,18,256]{2,1,0:T(8,128)S(1)} %broadcast_multiply_fusion.6, f32[64,18,256]{2,1,0:T(8,128)S(1)} %get-tuple-element.10, f32[16]{0:T(128)S(1)} %slice.537, ...), kind=kLoop, calls=%fused_computation.181 | loop fusion | flops 3407872 | bytes 9445440 | tf_op jit(solution)/shard_map/add | solution.py:116
  (83 shorter events, 13.9 us)
Async XLA Ops:
  0.6 16.5 %copy-start.2 = (f32[64,16,256]{2,1,0:T(8,128)S(1)}, f32[64,16,256]{2,1,0:T(8,128)}, u32[]{:S(2)}) copy-start(f32[64,16,256]{2,1,0:T(8,128)} %param.8) | copy-start | bytes 3145732
  2.2 11.8 %collective-permute-start.2 = (f32[3,4,256]{2,1,0:T(4,128)S(1)}, f32[3,4,256]{2,1,0:T(4,128)S(1)}, u32[]{:S(2)}, u32[]{:S(2)}) collective-permute-start(f32[3,4,256]{2,1,0:T(4,128)S(1)} %get-tuple-element.43), channel_id=1, source_target_pairs={{0,1},{1,2},{2,3},{3,4},{4,5},{5,6},{6,7},{8,9},{9,10},{10,11},{11... | collective-permute-start | bytes 36872 | tf_op jit(solution)/shard_map/ppermute | solution.py:14
  4.6 9.4 %collective-permute-start.3 = (f32[3,4,256]{2,1,0:T(4,128)S(1)}, f32[3,4,256]{2,1,0:T(4,128)S(1)}, u32[]{:S(2)}, u32[]{:S(2)}) collective-permute-start(f32[3,4,256]{2,1,0:T(4,128)S(1)} %get-tuple-element.44), channel_id=1, source_target_pairs={{1,0},{2,1},{3,2},{4,3},{5,4},{6,5},{7,6},{9,8},{10,9},{11,10},{12... | collective-permute-start | bytes 36872 | tf_op jit(solution)/shard_map/ppermute | solution.py:17
  7.2 7.8 %collective-permute-start = (f32[64,4,256]{2,1,0:T(4,128)S(1)}, f32[64,4,256]{2,1,0:T(4,128)S(1)}, u32[]{:S(2)}, u32[]{:S(2)}) collective-permute-start(f32[64,4,256]{2,1,0:T(4,128)S(1)} %get-tuple-element.33), channel_id=1, source_target_pairs={{0,1},{1,2},{2,3},{3,4},{4,5},{5,6},{6,7},{8,9},{9,10},{10,11},{11... | collective-permute-start | bytes 786440 | tf_op jit(solution)/shard_map/ppermute | solution.py:14
  12.4 4.7 %collective-permute-start.1 = (f32[64,4,256]{2,1,0:T(4,128)S(1)}, f32[64,4,256]{2,1,0:T(4,128)S(1)}, u32[]{:S(2)}, u32[]{:S(2)}) collective-permute-start(f32[64,4,256]{2,1,0:T(4,128)S(1)} %get-tuple-element.34), channel_id=1, source_target_pairs={{1,0},{2,1},{3,2},{4,3},{5,4},{6,5},{7,6},{9,8},{10,9},{11,10},{12... | collective-permute-start | bytes 786440 | tf_op jit(solution)/shard_map/ppermute | solution.py:17
  22.4 0.7 copy-start.5
  22.4 0.7 copy-start.6
  23.2 1.4 copy-start
  24.6 17.1 %copy-start.7 = (f32[3,16,256]{2,1,0:T(8,128)S(1)}, f32[3,16,256]{2,1,0:T(8,128)}, u32[]{:S(2)}) copy-start(f32[3,16,256]{2,1,0:T(8,128)} %param.10) | copy-start | bytes 147460
  24.6 17.1 %copy-start.8 = (f32[3,16,256]{2,1,0:T(8,128)S(1)}, f32[3,16,256]{2,1,0:T(8,128)}, u32[]{:S(2)}) copy-start(f32[3,16,256]{2,1,0:T(8,128)} %param.9) | copy-start | bytes 147460
  42.1 4.8 %collective-permute-start.4 = (f32[64,4,256]{2,1,0:T(4,128)S(1)}, f32[64,4,256]{2,1,0:T(4,128)S(1)}, u32[]{:S(2)}, u32[]{:S(2)}) collective-permute-start(f32[64,4,256]{2,1,0:T(4,128)S(1)} %get-tuple-element.31), channel_id=1, source_target_pairs={{0,1},{1,2},{2,3},{3,4},{4,5},{5,6},{6,7},{8,9},{9,10},{10,11},{11... | collective-permute-start | bytes 786440 | tf_op jit(solution)/shard_map/ppermute | solution.py:14
  45.3 6.3 %collective-permute-start.5 = (f32[64,4,256]{2,1,0:T(4,128)S(1)}, f32[64,4,256]{2,1,0:T(4,128)S(1)}, u32[]{:S(2)}, u32[]{:S(2)}) collective-permute-start(f32[64,4,256]{2,1,0:T(4,128)S(1)} %get-tuple-element.32), channel_id=1, source_target_pairs={{1,0},{2,1},{3,2},{4,3},{5,4},{6,5},{7,6},{9,8},{10,9},{11,10},{12... | collective-permute-start | bytes 786440 | tf_op jit(solution)/shard_map/ppermute | solution.py:17
  57.0 1.2 copy-start.3
  60.0 91.2 %copy-start.1 = (f32[64,16,256]{2,1,0:T(8,128)}, f32[64,16,256]{2,1,0:T(8,128)S(1)}, u32[]{:S(2)}) copy-start(f32[64,16,256]{2,1,0:T(8,128)S(1)} %get-tuple-element.8) | copy-start | bytes 3145732
  60.1 8.2 %collective-permute-start.6 = (f32[64,4,256]{2,1,0:T(4,128)S(1)}, f32[64,4,256]{2,1,0:T(4,128)S(1)}, u32[]{:S(2)}, u32[]{:S(2)}) collective-permute-start(f32[64,4,256]{2,1,0:T(4,128)S(1)} %get-tuple-element.29), channel_id=1, source_target_pairs={{0,1},{1,2},{2,3},{3,4},{4,5},{5,6},{6,7},{8,9},{9,10},{10,11},{11... | collective-permute-start | bytes 786440 | tf_op jit(solution)/shard_map/ppermute | solution.py:14
  66.8 3.4 %collective-permute-start.7 = (f32[64,4,256]{2,1,0:T(4,128)S(1)}, f32[64,4,256]{2,1,0:T(4,128)S(1)}, u32[]{:S(2)}, u32[]{:S(2)}) collective-permute-start(f32[64,4,256]{2,1,0:T(4,128)S(1)} %get-tuple-element.30), channel_id=1, source_target_pairs={{1,0},{2,1},{3,2},{4,3},{5,4},{6,5},{7,6},{9,8},{10,9},{11,10},{12... | collective-permute-start | bytes 786440 | tf_op jit(solution)/shard_map/ppermute | solution.py:17
  92.6 1.0 copy-start.4
  93.6 50.8 %collective-permute-start.8 = (f32[64,4,256]{2,1,0:T(4,128)S(1)}, f32[64,4,256]{2,1,0:T(4,128)S(1)}, u32[]{:S(2)}, u32[]{:S(2)}) collective-permute-start(f32[64,4,256]{2,1,0:T(4,128)S(1)} %get-tuple-element.27), channel_id=1, source_target_pairs={{0,1},{1,2},{2,3},{3,4},{4,5},{5,6},{6,7},{8,9},{9,10},{10,11},{11... | collective-permute-start | bytes 786440 | tf_op jit(solution)/shard_map/ppermute | solution.py:14
  96.1 48.4 %collective-permute-start.9 = (f32[64,4,256]{2,1,0:T(4,128)S(1)}, f32[64,4,256]{2,1,0:T(4,128)S(1)}, u32[]{:S(2)}, u32[]{:S(2)}) collective-permute-start(f32[64,4,256]{2,1,0:T(4,128)S(1)} %get-tuple-element.28), channel_id=1, source_target_pairs={{1,0},{2,1},{3,2},{4,3},{5,4},{6,5},{7,6},{9,8},{10,9},{11,10},{12... | collective-permute-start | bytes 786440 | tf_op jit(solution)/shard_map/ppermute | solution.py:17
where the time goes:
time: 156 us; the launch traced here: 154 us
  blocking collectives  75.7 us (49%)
  other arithmetic  30.8 us (20%)
  starting transfers between devices  26.9 us (17%)
  waiting for transfers between devices  8.78 us (6%)
  local copies, waits for them, and re-layouts  7.32 us (5%)
  between operations  4.95 us (3%)
    psum x1, blocking collectives, shards(): lax.psum((jnp.sum(gradient * gradient), curvature_term), ('mem', 'tile'))  44.5 us
    psum x2, blocking collectives, misfit_of(): total = lax.psum(partial_value, 'mem')  31.2 us
    ppermute x5, starting transfers between devices, extended_2(): lax.ppermute(lax.slice_in_dim(block, block.shape[dim] - width, None, axis...  20 us
    mul x8, other arithmetic, localise(): forward_core(extended, kappa_wide[first_row:last_row], advect_wide[first_...  11.2 us
    ppermute x5, waiting for transfers between devices, extended_2(): lax.ppermute(lax.slice_in_dim(block, 0, width, axis=dim), axis, backward)  8.77 us
    mul x6, other arithmetic, localise_adjoint(): carried = advect_wide[repeat:last_row] * extended  8.22 us
    ppermute x5, starting transfers between devices, extended_2(): lax.ppermute(lax.slice_in_dim(block, 0, width, axis=dim), axis, backward)  6.86 us
    concatenate x5, other arithmetic, extended_2(): block = jnp.concatenate([low, block, high], axis=dim)  3.31 us
  transfers between devices with their start and end apart: 10, of which 3 were waited for; matrix products, arithmetic and copies ran while one was open for 2% of the time, Pallas kernels for 0%

commit v1 on v0

v1 whole, which is shorter than its diff:
```python
import jax
import jax.numpy as jnp
from jax import lax
from jax.sharding import PartitionSpec as P

SWEEPS = 4


def pairs_inner(count):
    return [(i, i ^ 1) for i in range(count) if (i ^ 1) < count]


def pairs_outer(count):
    partner = [(i, i + 1 if i % 2 else i - 1) for i in range(count)]
    return [(i, j) for i, j in partner if 0 <= j < count]


def halo(block, width, dim):
    count = lax.axis_size("tile")
    odd = lax.axis_index("tile") % 2 == 1
    top = lax.slice_in_dim(block, 0, width, axis=dim)
    bottom = lax.slice_in_dim(block, block.shape[dim] - width, None, axis=dim)
    outer = lax.ppermute(jnp.where(odd, bottom, top), "tile", pairs_outer(count))
    inner = lax.ppermute(jnp.where(odd, top, bottom), "tile", pairs_inner(count))
    return jnp.where(odd, inner, outer), jnp.where(odd, outer, inner)


def extended(block, width, dim):
    low, high = halo(block, width, dim)
    return jnp.concatenate([low, block, high], axis=dim)


def sum_over(value, axis):
    count = lax.axis_size(axis)
    power = count & (count - 1) == 0
    total = value
    for step in range(1, count):
        pairs = [(i, i ^ step if power else (i + step) % count) for i in range(count)]
        total = total + lax.ppermute(value, axis, pairs)
    return total


def sum_doubling(value, axis):
    count = lax.axis_size(axis)
    if count & (count - 1):
        return sum_over(value, axis)
    step = 1
    while step < count:
        value = value + lax.ppermute(value, axis, [(i, i ^ step) for i in range(count)])
        step *= 2
    return value


def column_pad(values):
    return jnp.pad(values, ((0, 0), (0, 0), (1, 1)))


def forward_core(extended, kappa_rows, advect_rows, upper_rows):
    center = extended[:, 1:-1]
    below = extended[:, 2:]
    above = extended[:, :-2]
    padded = column_pad(center)
    spread = below + above + padded[:, :, 2:] + padded[:, :, :-2] - 4.0 * center
    upwind_value = jnp.where(upper_rows, below, above)
    return center + kappa_rows * spread - advect_rows * (center - upwind_value)


def adjoint_core(center, carried, weighted_ext, lower_ext, upper_ext):
    weighted = weighted_ext[:, 1:-1]
    padded = column_pad(weighted)
    spread = (
        weighted_ext[:, 2:]
        + weighted_ext[:, :-2]
        + padded[:, :, 2:]
        + padded[:, :, :-2]
        - 4.0 * weighted
    )
    returned = lower_ext[:, 2:] + upper_ext[:, :-2]
    return center + spread - carried + returned


def shards(perturbations, control, innovation, obs_weight, diffusion, advection, upwind):
    row_count = control.shape[1]
    upper = upwind == 1
    stacked_coeff = jnp.stack([diffusion, advection, upper.astype(jnp.float32)])
    coefficients = extended(stacked_coeff, SWEEPS, 1)
    kappa_wide = coefficients[0]
    advect_wide = coefficients[1]
    upper_wide = coefficients[2] > 0.5
    global_rows = (
        lax.axis_index("tile") * row_count
        + jnp.arange(row_count + 2 * SWEEPS, dtype=jnp.int32)
        - SWEEPS
    )
    inside = ((global_rows >= 0) & (global_rows < row_count * lax.axis_size("tile"))).astype(
        jnp.float32
    )[:, None]

    def localise(values):
        wide = extended(values, SWEEPS, 1)
        for repeat in range(SWEEPS):
            first_row = repeat + 1
            last_row = row_count + 2 * SWEEPS - repeat - 1
            wide = (
                forward_core(
                    wide,
                    kappa_wide[first_row:last_row],
                    advect_wide[first_row:last_row],
                    upper_wide[first_row:last_row],
                )
                * inside[first_row:last_row]
            )
        return wide

    def localise_adjoint(values):
        wide = extended(values, SWEEPS, 1)
        for repeat in range(SWEEPS):
            last_row = row_count + 2 * SWEEPS - repeat
            upper_part = upper_wide[repeat:last_row]
            carried = advect_wide[repeat:last_row] * wide
            weighted = kappa_wide[repeat:last_row] * wide
            lower_ext = jnp.where(upper_part, 0.0, carried)
            upper_ext = jnp.where(upper_part, carried, 0.0)
            wide = (
                adjoint_core(wide[:, 1:-1], carried[:, 1:-1], weighted, lower_ext, upper_ext)
                * inside[repeat + 1 : last_row - 1]
            )
        return wide

    def project(values):
        return jnp.sum(perturbations.astype(jnp.float32) * values[None], axis=1)

    def pull_back(weights_time):
        return jnp.sum(perturbations.astype(jnp.float32) * weights_time[:, None], axis=0)

    increment = sum_over(project(localise(control)), "mem")
    misfit = obs_weight * (increment - innovation)
    gradient = control + localise_adjoint(pull_back(misfit))
    partial = project(localise(gradient))
    squares = jnp.sum(gradient * gradient, axis=(0, 1))
    times = partial.shape[0]
    flat = jnp.concatenate(
        [partial.reshape(times * row_count, -1), jnp.broadcast_to(squares / 8, (8,) + squares.shape)]
    )
    flat = sum_over(flat, "mem")
    image = flat[: times * row_count].reshape(partial.shape)
    weighted_image = obs_weight * image
    terms = image * weighted_image
    curve = terms.reshape(-1, 8, terms.shape[-1]).sum(0)
    both = sum_doubling(jnp.concatenate([flat[times * row_count :], curve]), "tile")
    square_sum = jnp.sum(both[:8])
    hessian_product = gradient + localise_adjoint(pull_back(weighted_image))
    return (gradient, hessian_product, square_sum / (square_sum + jnp.sum(both[8:])))


def solution(mesh):
    return jax.shard_map(
        shards,
        mesh=mesh,
        in_specs=(
            P(None, "mem", "tile", None),
            P("mem", "tile", None),
            P(None, "tile", None),
            P(None, "tile", None),
            P("tile", None),
            P("tile", None),
            P("tile", None),
        ),
        out_specs=(P("mem", "tile", None), P("mem", "tile", None), P()),
        check_vma=False,
    )
```

time: 156 us -> 96.8 us (0.62)
  blocking collectives: 75.7 us -> 0 us
  starting transfers between devices: 26.9 us -> 41.3 us
  waiting for transfers between devices: 8.78 us -> 13.6 us
    psum x3 -> x0, blocking collectives: 75.7 us -> none  [the longest x1 44.5 us: shards(): lax.psum((jnp.sum(gradient * gradient), curvature_term), ('mem', 'tile'))]
    ppermute x10 -> x19, starting transfers between devices: 26.9 us -> 41.3 us  [the longest x5 17 us: halo(): lax.ppermute(jnp.where(odd, top, bottom), 'tile', pairs_inner(count))]
    ppermute x10 -> x19, waiting for transfers between devices: 8.78 us -> 13.6 us  [the longest x6 6.65 us: sum_over(): total = total + lax.ppermute(value, axis, pairs)]
    select_n x0 -> x11, other arithmetic: none -> 2.5 us  [the longest x5 2.34 us: halo(): jnp.where(odd, top, bottom)]
    slice x4 -> x2, local copies, waits for them, and re-layouts: 1.57 us -> 0.01 us  [the longest x1 0.01 us: shards(): image = flat[:times * row_count].reshape(partial.shape)]
    concatenate x5 -> x7, other arithmetic: 3.31 us -> 2.11 us  [the longest x5 2.1 us: extended(): return jnp.concatenate([low, block, high], axis=dim)]
    mul x21 -> x22, other arithmetic: 20 us -> 20.1 us  [the longest x8 11.1 us: localise(): forward_core(wide, kappa_wide[first_row:last_row], advect_wide[first_row:...]
  transfers between devices with their start and end apart: 10 -> 19, of which waited for: 3 -> 9; matrix products, arithmetic and copies ran while one was open for 2% -> 4% of each run, Pallas kernels for 0% -> 0%
where the time goes in v1:
time: 96.8 us; the launch traced here: 96 us
  starting transfers between devices  41.3 us (43%)
  other arithmetic  31 us (32%)
  waiting for transfers between devices  13.6 us (14%)
  local copies, waits for them, and re-layouts  5.77 us (6%)
  between operations  4.33 us (4%)
    ppermute x5, starting transfers between devices, halo(): lax.ppermute(jnp.where(odd, top, bottom), 'tile', pairs_inner(count))  17 us
    ppermute x3, starting transfers between devices, sum_doubling(): lax.ppermute(value, axis, [(i, i ^ step) for i in range(count)])  13.1 us
    mul x8, other arithmetic, localise(): forward_core(wide, kappa_wide[first_row:last_row], advect_wide[first_row:...  11.1 us
    mul x6, other arithmetic, localise_adjoint(): carried = advect_wide[repeat:last_row] * wide  8.22 us
    ppermute x6, starting transfers between devices, sum_over(): total = total + lax.ppermute(value, axis, pairs)  7.11 us
    ppermute x6, waiting for transfers between devices, sum_over(): total = total + lax.ppermute(value, axis, pairs)  6.65 us
    ppermute x3, waiting for transfers between devices, sum_doubling(): lax.ppermute(value, axis, [(i, i ^ step) for i in range(count)])  6.37 us
    ppermute x5, starting transfers between devices, halo(): lax.ppermute(jnp.where(odd, bottom, top), 'tile', pairs_outer(count))  4.13 us
  transfers between devices with their start and end apart: 19, of which 9 were waited for; matrix products, arithmetic and copies ran while one was open for 4% of the time, Pallas kernels for 0%

profile of v1, /device:TPU:0, one launch (start us, length us, event | category | flops | bytes accessed | tf_op | source)
XLA Modules:
  0.0 96.0 jit_solution(1547735891534961170)
XLA Ops:
  2.9 4.5 %collective-permute-start.2 = (f32[3,4,256]{2,1,0:T(4,128)S(1)}, f32[3,4,256]{2,1,0:T(4,128)S(1)}, u32[]{:S(2)}, u32[]{:S(2)}) collective-permute-start(f32[3,4,256]{2,1,0:T(4,128)S(1)} %get-tuple-element.21), channel_id=1, source_target_pairs={{0,1},{1,0},{2,3},{3,2},{4,5},{5,4},{6,7},{7,6},{8,9},{9,8},{10,11... | collective-permute-start | bytes 36872 | tf_op jit(solution)/shard_map/ppermute | solution.py:24
  7.4 1.3 %slice_select_fusion.23 = (f32[64,4,256]{2,1,0:T(4,128)S(1)}, f32[64,4,256]{2,1,0:T(4,128)S(1)}) fusion(f32[64,16,256]{2,1,0:T(8,128)} %param.8, pred[]{:T(512)S(6)} %eq.19), kind=kLoop, calls=%fused_computation.214 | loop fusion | flops 131072 | bytes 1048577 | tf_op jit(solution)/shard_map/jit(_where)/select_n | solution.py:24
  11.2 1.5 %fusion.10 = f32[64,22,256]{2,1,0:T(8,128)S(1)} fusion(f32[64,22,256]{2,1,0:T(8,128)S(1)} %slice.654, f32[64,24,256]{2,1,0:T(8,128)S(1)} %pad_maximum_fusion, f32[22]{0:T(128)S(1)} %slice.521, f32[22,256]{1,0:T(8,128)S(1)} %get-tuple-element.53, f32[22,256]{1,0:T(8,128)S(1)} %get-tuple-element.52, pred[22,256]{1,0:T(8,128)(4,1)S(1)} %slice_bitcast_fusion.10), kind=kLoop, calls=%fused_computation.46 | loop fusion | flops 4325376 | bytes 5817944 | tf_op jit(solution)/shard_map/mul | solution.py:105
  12.9 1.5 %fusion.17 = f32[64,20,256]{2,1,0:T(8,128)S(1)} fusion(f32[64,20,256]{2,1,0:T(8,128)S(1)} %slice.661, f32[64,22,256]{2,1,0:T(8,128)S(1)} %fusion.10, f32[20]{0:T(128)S(1)} %slice.531, f32[20,256]{1,0:T(8,128)S(1)} %get-tuple-element.51, f32[20,256]{1,0:T(8,128)S(1)} %get-tuple-element.50, pred[20,256]{1,0:T(8,128)(4,1)S(1)} %slice_bitcast_fusion.9), kind=kLoop, calls=%fused_computation.53 | loop fusion | flops 3932160 | bytes 5289040 | tf_op jit(solution)/shard_map/mul | solution.py:105
  14.6 1.5 %fusion.24 = f32[64,18,256]{2,1,0:T(8,128)S(1)} fusion(f32[64,18,256]{2,1,0:T(8,128)S(1)} %slice.667, f32[64,20,256]{2,1,0:T(8,128)S(1)} %fusion.17, f32[18]{0:T(128)S(1)} %slice.541, f32[18,256]{1,0:T(8,128)S(1)} %get-tuple-element.49, f32[18,256]{1,0:T(8,128)S(1)} %get-tuple-element.48, pred[18,256]{1,0:T(8,128)(4,1)S(1)} %slice_bitcast_fusion.8), kind=kLoop, calls=%fused_computation.60 | loop fusion | flops 3538944 | bytes 4760136 | tf_op jit(solution)/shard_map/mul | solution.py:105
  18.6 2.5 %collective-permute-start.6 = (f32[3,16,256]{2,1,0:T(8,128)S(1)}, f32[3,16,256]{2,1,0:T(8,128)S(1)}, u32[]{:S(2)}, u32[]{:S(2)}) collective-permute-start(f32[3,16,256]{2,1,0:T(8,128)S(1)} %fusion), channel_id=1, source_target_pairs={{0,24},{8,16},{16,8},{24,0},{1,25},{9,17},{17,9},{25,1},{2,26},{10... | collective-permute-start | bytes 147464 | tf_op jit(solution)/shard_map/ppermute | solution.py:39
  22.2 1.5 %collective-permute-done.6 = f32[3,16,256]{2,1,0:T(8,128)S(1)} collective-permute-done((f32[3,16,256]{2,1,0:T(8,128)S(1)}, f32[3,16,256]{2,1,0:T(8,128)S(1)}, u32[]{:S(2)}, u32[]{:S(2)}) %collective-permute-start.6) | collective-permute-done | bytes 49184 | tf_op jit(solution)/shard_map/ppermute | solution.py:39
  23.7 1.5 %collective-permute-done.5 = f32[3,16,256]{2,1,0:T(8,128)S(1)} collective-permute-done((f32[3,16,256]{2,1,0:T(8,128)S(1)}, f32[3,16,256]{2,1,0:T(8,128)S(1)}, u32[]{:S(2)}, u32[]{:S(2)}) %collective-permute-start.5) | collective-permute-done | bytes 49184 | tf_op jit(solution)/shard_map/ppermute | solution.py:39
  26.2 4.6 %collective-permute-start.7 = (f32[64,4,256]{2,1,0:T(4,128)S(1)}, f32[64,4,256]{2,1,0:T(4,128)S(1)}, u32[]{:S(2)}, u32[]{:S(2)}) collective-permute-start(f32[64,4,256]{2,1,0:T(4,128)S(1)} %get-tuple-element.34), channel_id=1, source_target_pairs={{0,1},{1,0},{2,3},{3,2},{4,5},{5,4},{6,7},{7,6},{8,9},{9,8},{10,11... | collective-permute-start | bytes 786440 | tf_op jit(solution)/shard_map/ppermute | solution.py:24
  32.5 1.4 %broadcast_multiply_fusion.13 = (f32[64,22,256]{2,1,0:T(8,128)S(1)}, f32[64,22,256]{2,1,0:T(8,128)S(1)}) fusion(f32[22,256]{1,0:T(8,128)S(1)} %get-tuple-element.53, f32[22]{0:T(128)S(1)} %slice.521, f32[64,24,256]{2,1,0:T(8,128)S(1)} %get-tuple-element.29, pred[22,256]{1,0:T(8,128)(4,1)S(1)} %get-tuple-element.63, ...), kind=kLoop, calls=%fused_computation.204 | loop fusion | flops 4685824 | bytes 13010008 | tf_op jit(solution)/shard_map/mul | solution.py:120
  34.2 1.4 %broadcast_multiply_fusion.9 = (f32[64,20,256]{2,1,0:T(8,128)S(1)}, f32[64,20,256]{2,1,0:T(8,128)S(1)}) fusion(f32[20,256]{1,0:T(8,128)S(1)} %get-tuple-element.51, f32[20]{0:T(128)S(1)} %slice.531, f32[64,22,256]{2,1,0:T(8,128)S(1)} %get-tuple-element.19, pred[20,256]{1,0:T(8,128)(4,1)S(1)} %get-tuple-element.61, ...), kind=kLoop, calls=%fused_computation.200 | loop fusion | flops 4259840 | bytes 11827280 | tf_op jit(solution)/shard_map/mul | solution.py:120
  35.8 1.4 %broadcast_multiply_fusion.5 = (f32[64,18,256]{2,1,0:T(8,128)S(1)}, f32[64,18,256]{2,1,0:T(8,128)S(1)}) fusion(f32[18,256]{1,0:T(8,128)S(1)} %get-tuple-element.49, f32[18]{0:T(128)S(1)} %slice.541, f32[64,20,256]{2,1,0:T(8,128)S(1)} %get-tuple-element.17, pred[18,256]{1,0:T(8,128)(4,1)S(1)} %get-tuple-element.59, ...), kind=kLoop, calls=%fused_computation.196 | loop fusion | flops 3833856 | bytes 10644552 | tf_op jit(solution)/shard_map/mul | solution.py:120
  37.5 1.1 %copy-done.3 = f32[64,16,256]{2,1,0:T(8,128)S(1)} copy-done((f32[64,16,256]{2,1,0:T(8,128)S(1)}, f32[64,16,256]{2,1,0:T(8,128)}, u32[]{:S(2)}) %copy-start.3) | copy-done | bytes 1048600
  38.5 1.3 %multiply_reduce_fusion = (f32[256]{0:T(256)S(1)}, f32[64,16,256]{2,1,0:T(8,128)S(1)}) fusion(f32[64,16,256]{2,1,0:T(8,128)S(1)} %copy-done.3, f32[16]{0:T(128)S(1)} %slice.549, f32[64,18,256]{2,1,0:T(8,128)S(1)} %get-tuple-element.15, pred[16,256]{1,0:T(8,128)(4,1)S(1)} %get-tuple-element.57, pred[16,256]{1,0:T(8,128)(4,1)S(1)} %get-tuple-element.56, ...), kind=kLoop, calls=%fused_computation.190 | loop fusion | flops 3931904 | bytes 9446464 | tf_op jit(solution)/shard_map/reduce_sum | solution.py:140
  39.9 7.8 %collective-permute-start.9 = (f32[64,4,256]{2,1,0:T(4,128)S(1)}, f32[64,4,256]{2,1,0:T(4,128)S(1)}, u32[]{:S(2)}, u32[]{:S(2)}) collective-permute-start(f32[64,4,256]{2,1,0:T(4,128)S(1)} %get-tuple-element.32), channel_id=1, source_target_pairs={{0,1},{1,0},{2,3},{3,2},{4,5},{5,4},{6,7},{7,6},{8,9},{9,8},{10,11... | collective-permute-start | bytes 786440 | tf_op jit(solution)/shard_map/ppermute | solution.py:24
  49.3 1.5 %fusion.52 = f32[64,22,256]{2,1,0:T(8,128)S(1)} fusion(f32[64,22,256]{2,1,0:T(8,128)S(1)} %slice.719, f32[64,24,256]{2,1,0:T(8,128)S(1)} %pad_maximum_fusion.2, f32[22]{0:T(128)S(1)} %slice.521, f32[22,256]{1,0:T(8,128)S(1)} %get-tuple-element.53, f32[22,256]{1,0:T(8,128)S(1)} %get-tuple-element.52, pred[22,256]{1,0:T(8,128)(4,1)S(1)} %slice_bitcast_fusion.10), kind=kLoop, calls=%fused_computation.88 | loop fusion | flops 4325376 | bytes 5817944 | tf_op jit(solution)/shard_map/mul | solution.py:105
  51.0 1.5 %fusion.59 = f32[64,20,256]{2,1,0:T(8,128)S(1)} fusion(f32[64,20,256]{2,1,0:T(8,128)S(1)} %slice.722, f32[64,22,256]{2,1,0:T(8,128)S(1)} %fusion.52, f32[20]{0:T(128)S(1)} %slice.531, f32[20,256]{1,0:T(8,128)S(1)} %get-tuple-element.51, f32[20,256]{1,0:T(8,128)S(1)} %get-tuple-element.50, pred[20,256]{1,0:T(8,128)(4,1)S(1)} %slice_bitcast_fusion.9), kind=kLoop, calls=%fused_computation.95 | loop fusion | flops 3932160 | bytes 5289040 | tf_op jit(solution)/shard_map/mul | solution.py:105
  52.7 1.5 %fusion.66 = f32[64,18,256]{2,1,0:T(8,128)S(1)} fusion(f32[64,18,256]{2,1,0:T(8,128)S(1)} %slice.725, f32[64,20,256]{2,1,0:T(8,128)S(1)} %fusion.59, f32[18]{0:T(128)S(1)} %slice.541, f32[18,256]{1,0:T(8,128)S(1)} %get-tuple-element.49, f32[18,256]{1,0:T(8,128)S(1)} %get-tuple-element.48, pred[18,256]{1,0:T(8,128)(4,1)S(1)} %slice_bitcast_fusion.8), kind=kLoop, calls=%fused_computation.102 | loop fusion | flops 3538944 | bytes 4760136 | tf_op jit(solution)/shard_map/mul | solution.py:105
  54.4 1.0 %fusion.115 = f32[64,16,256]{2,1,0:T(8,128)S(1)} fusion(f32[64,16,256]{2,1,0:T(8,128)S(1)} %slice.728, f32[64,18,256]{2,1,0:T(8,128)S(1)} %fusion.66, f32[16]{0:T(128)S(1)} %slice.549, f32[16,256]{1,0:T(8,128)S(1)} %copy-done.6, f32[16,256]{1,0:T(8,128)S(1)} %copy-done.7, pred[16,256]{1,0:T(8,128)(4,1)S(1)} %slice_bitcast_fusion.11), kind=kLoop, calls=%fused_computation.173 | loop fusion | flops 3145728 | bytes 4231232 | tf_op jit(solution)/shard_map/mul | solution.py:105
  55.7 1.6 %collective-permute-start.12 = (f32[56,256]{1,0:T(8,128)S(1)}, f32[56,256]{1,0:T(8,128)S(1)}, u32[]{:S(2)}, u32[]{:S(2)}) collective-permute-start(f32[56,256]{1,0:T(8,128)S(1)} %pad_maximum_fusion.5), channel_id=1, source_target_pairs={{0,16},{8,24},{16,0},{24,8},{1,17},{9,25},{17,1},{25,9},{2,18},{10... | collective-permute-start | bytes 172040 | tf_op jit(solution)/shard_map/ppermute | solution.py:39
  57.9 1.4 %collective-permute-start.11 = (f32[56,256]{1,0:T(8,128)S(1)}, f32[56,256]{1,0:T(8,128)S(1)}, u32[]{:S(2)}, u32[]{:S(2)}) collective-permute-start(f32[56,256]{1,0:T(8,128)S(1)} %pad_maximum_fusion.5), channel_id=1, source_target_pairs={{0,8},{8,0},{16,24},{24,16},{1,9},{9,1},{17,25},{25,17},{2,10},{10... | collective-permute-start | bytes 172040 | tf_op jit(solution)/shard_map/ppermute | solution.py:39
  60.0 2.4 %collective-permute-done.13 = f32[56,256]{1,0:T(8,128)S(1)} collective-permute-done((f32[56,256]{1,0:T(8,128)S(1)}, f32[56,256]{1,0:T(8,128)S(1)}, u32[]{:S(2)}, u32[]{:S(2)}) %collective-permute-start.13) | collective-permute-done | bytes 57376 | tf_op jit(solution)/shard_map/ppermute | solution.py:39
  62.5 5.6 %collective-permute-start.16 = (f32[16,256]{1,0:T(8,128)S(1)}, f32[16,256]{1,0:T(8,128)S(1)}, u32[]{:S(2)}, u32[]{:S(2)}) collective-permute-start(f32[16,256]{1,0:T(8,128)S(1)} %pad_maximum_fusion.6), channel_id=1, source_target_pairs={{0,1},{1,0},{2,3},{3,2},{4,5},{5,4},{6,7},{7,6},{8,9},{9,8},{10,11... | collective-permute-start | bytes 49160 | tf_op jit(solution)/shard_map/ppermute | solution.py:49
  69.6 1.1 %collective-permute-start.15 = (f32[64,4,256]{2,1,0:T(4,128)S(1)}, f32[64,4,256]{2,1,0:T(4,128)S(1)}, u32[]{:S(2)}, u32[]{:S(2)}) collective-permute-start(f32[64,4,256]{2,1,0:T(4,128)S(1)} %get-tuple-element.31), channel_id=1, source_target_pairs={{1,2},{2,1},{3,4},{4,3},{5,6},{6,5},{9,10},{10,9},{11,12},{12,11},... | collective-permute-start | bytes 786440 | tf_op jit(solution)/shard_map/ppermute | solution.py:23
  70.7 4.8 %collective-permute-start.17 = (f32[16,256]{1,0:T(8,128)S(1)}, f32[16,256]{1,0:T(8,128)S(1)}, u32[]{:S(2)}, u32[]{:S(2)}) collective-permute-start(f32[16,256]{1,0:T(8,128)S(1)} %fusion.126), channel_id=1, source_target_pairs={{0,2},{1,3},{2,0},{3,1},{4,6},{5,7},{6,4},{7,5},{8,10},{9,11},{10,... | collective-permute-start | bytes 49160 | tf_op jit(solution)/shard_map/ppermute | solution.py:49
  75.5 4.3 %collective-permute-done.17 = f32[16,256]{1,0:T(8,128)S(1)} collective-permute-done((f32[16,256]{1,0:T(8,128)S(1)}, f32[16,256]{1,0:T(8,128)S(1)}, u32[]{:S(2)}, u32[]{:S(2)}) %collective-permute-start.17) | collective-permute-done | bytes 16416 | tf_op jit(solution)/shard_map/ppermute | solution.py:49
  79.9 2.6 %collective-permute-start.18 = (f32[16,256]{1,0:T(8,128)S(1)}, f32[16,256]{1,0:T(8,128)S(1)}, u32[]{:S(2)}, u32[]{:S(2)}) collective-permute-start(f32[16,256]{1,0:T(8,128)S(1)} %add.415), channel_id=1, source_target_pairs={{0,4},{1,5},{2,6},{3,7},{4,0},{5,1},{6,2},{7,3},{8,12},{9,13},{10,... | collective-permute-start | bytes 49160 | tf_op jit(solution)/shard_map/ppermute | solution.py:49
  82.5 2.0 %collective-permute-done.18 = f32[16,256]{1,0:T(8,128)S(1)} collective-permute-done((f32[16,256]{1,0:T(8,128)S(1)}, f32[16,256]{1,0:T(8,128)S(1)}, u32[]{:S(2)}, u32[]{:S(2)}) %collective-permute-start.18) | collective-permute-done | bytes 16416 | tf_op jit(solution)/shard_map/ppermute | solution.py:49
  87.7 1.4 %broadcast_multiply_fusion.12 = (f32[64,22,256]{2,1,0:T(8,128)S(1)}, f32[64,22,256]{2,1,0:T(8,128)S(1)}) fusion(f32[22,256]{1,0:T(8,128)S(1)} %get-tuple-element.53, f32[22]{0:T(128)S(1)} %slice.521, f32[64,24,256]{2,1,0:T(8,128)S(1)} %get-tuple-element.26, pred[22,256]{1,0:T(8,128)(4,1)S(1)} %get-tuple-element.63, ...), kind=kLoop, calls=%fused_computation.203 | loop fusion | flops 4685824 | bytes 13010008 | tf_op jit(solution)/shard_map/mul | solution.py:120
  89.3 1.4 %broadcast_multiply_fusion.8 = (f32[64,20,256]{2,1,0:T(8,128)S(1)}, f32[64,20,256]{2,1,0:T(8,128)S(1)}) fusion(f32[20,256]{1,0:T(8,128)S(1)} %get-tuple-element.51, f32[20]{0:T(128)S(1)} %slice.531, f32[64,22,256]{2,1,0:T(8,128)S(1)} %get-tuple-element.11, pred[20,256]{1,0:T(8,128)(4,1)S(1)} %get-tuple-element.61, ...), kind=kLoop, calls=%fused_computation.199 | loop fusion | flops 4259840 | bytes 11827280 | tf_op jit(solution)/shard_map/mul | solution.py:120
  91.0 1.4 %broadcast_multiply_fusion.4 = (f32[64,18,256]{2,1,0:T(8,128)S(1)}, f32[64,18,256]{2,1,0:T(8,128)S(1)}) fusion(f32[18,256]{1,0:T(8,128)S(1)} %get-tuple-element.49, f32[18]{0:T(128)S(1)} %slice.541, f32[64,20,256]{2,1,0:T(8,128)S(1)} %get-tuple-element.9, pred[18,256]{1,0:T(8,128)(4,1)S(1)} %get-tuple-element.59, pred[18,256]{1,0:T(8,128)(4,1)S(1)} %get-tuple-element.58, ...), kind=kLoop, calls=%fused_computation.195 | loop fusion | flops 3833856 | bytes 10644552 | tf_op jit(solution)/shard_map/mul | solution.py:120
  92.6 2.2 %fusion.123 = f32[64,16,256]{2,1,0:T(8,128)} fusion(f32[64,16,256]{2,1,0:T(8,128)S(1)} %get-tuple-element.14, f32[64,16,256]{2,1,0:T(8,128)S(1)} %slice.764, f32[64,18,256]{2,1,0:T(8,128)S(1)} %get-tuple-element.7, f32[64,18,256]{2,1,0:T(8,128)S(1)} %broadcast_multiply_fusion.6, f32[64,18,256]{2,1,0:T(8,128)S(1)} %get-tuple-element.8, f32[16]{0:T(128)S(1)} %slice.549, ...), kind=kLoop, calls=%fused_computation.181 | loop fusion | flops 3407872 | bytes 9445440 | tf_op jit(solution)/shard_map/add | solution.py:152
  (118 shorter events, 19.1 us)
Async XLA Ops:
  0.6 10.1 %copy-start.2 = (f32[64,16,256]{2,1,0:T(8,128)S(1)}, f32[64,16,256]{2,1,0:T(8,128)}, u32[]{:S(2)}) copy-start(f32[64,16,256]{2,1,0:T(8,128)} %param.8) | copy-start | bytes 3145732
  2.2 7.5 %collective-permute-start.3 = (f32[3,4,256]{2,1,0:T(4,128)S(1)}, f32[3,4,256]{2,1,0:T(4,128)S(1)}, u32[]{:S(2)}, u32[]{:S(2)}) collective-permute-start(f32[3,4,256]{2,1,0:T(4,128)S(1)} %broadcast_select_fusion.10), channel_id=1, source_target_pairs={{1,2},{2,1},{3,4},{4,3},{5,6},{6,5},{9,10},{10,9},{11,12},{12,11},... | collective-permute-start | bytes 36872 | tf_op jit(solution)/shard_map/ppermute | solution.py:23
  2.9 6.9 %collective-permute-start.2 = (f32[3,4,256]{2,1,0:T(4,128)S(1)}, f32[3,4,256]{2,1,0:T(4,128)S(1)}, u32[]{:S(2)}, u32[]{:S(2)}) collective-permute-start(f32[3,4,256]{2,1,0:T(4,128)S(1)} %get-tuple-element.21), channel_id=1, source_target_pairs={{0,1},{1,0},{2,3},{3,2},{4,5},{5,4},{6,7},{7,6},{8,9},{9,8},{10,11... | collective-permute-start | bytes 36872 | tf_op jit(solution)/shard_map/ppermute | solution.py:24
  8.7 2.0 %collective-permute-start = (f32[64,4,256]{2,1,0:T(4,128)S(1)}, f32[64,4,256]{2,1,0:T(4,128)S(1)}, u32[]{:S(2)}, u32[]{:S(2)}) collective-permute-start(f32[64,4,256]{2,1,0:T(4,128)S(1)} %get-tuple-element.36), channel_id=1, source_target_pairs={{0,1},{1,0},{2,3},{3,2},{4,5},{5,4},{6,7},{7,6},{8,9},{9,8},{10,11... | collective-permute-start | bytes 786440 | tf_op jit(solution)/shard_map/ppermute | solution.py:24
  8.8 2.0 %collective-permute-start.1 = (f32[64,4,256]{2,1,0:T(4,128)S(1)}, f32[64,4,256]{2,1,0:T(4,128)S(1)}, u32[]{:S(2)}, u32[]{:S(2)}) collective-permute-start(f32[64,4,256]{2,1,0:T(4,128)S(1)} %get-tuple-element.37), channel_id=1, source_target_pairs={{1,2},{2,1},{3,4},{4,3},{5,6},{6,5},{9,10},{10,9},{11,12},{12,11},... | collective-permute-start | bytes 786440 | tf_op jit(solution)/shard_map/ppermute | solution.py:23
  16.1 0.7 copy-start.6
  16.1 0.7 copy-start.7
  16.8 1.4 %copy-start = (bf16[3,64,16,256]{3,2,1,0:T(8,128)(2,1)S(1)}, bf16[3,64,16,256]{3,2,1,0:T(8,128)(2,1)}, u32[]{:S(2)}) copy-start(bf16[3,64,16,256]{3,2,1,0:T(8,128)(2,1)} %param.7) | copy-start | bytes 4718596
  18.2 7.5 %copy-start.8 = (f32[3,16,256]{2,1,0:T(8,128)S(1)}, f32[3,16,256]{2,1,0:T(8,128)}, u32[]{:S(2)}) copy-start(f32[3,16,256]{2,1,0:T(8,128)} %param.10) | copy-start | bytes 147460
  18.2 7.5 %copy-start.9 = (f32[3,16,256]{2,1,0:T(8,128)S(1)}, f32[3,16,256]{2,1,0:T(8,128)}, u32[]{:S(2)}) copy-start(f32[3,16,256]{2,1,0:T(8,128)} %param.9) | copy-start | bytes 147460
  18.6 5.1 %collective-permute-start.6 = (f32[3,16,256]{2,1,0:T(8,128)S(1)}, f32[3,16,256]{2,1,0:T(8,128)S(1)}, u32[]{:S(2)}, u32[]{:S(2)}) collective-permute-start(f32[3,16,256]{2,1,0:T(8,128)S(1)} %fusion), channel_id=1, source_target_pairs={{0,24},{8,16},{16,8},{24,0},{1,25},{9,17},{17,9},{25,1},{2,26},{10... | collective-permute-start | bytes 147464 | tf_op jit(solution)/shard_map/ppermute | solution.py:39
  21.1 4.1 %collective-permute-start.5 = (f32[3,16,256]{2,1,0:T(8,128)S(1)}, f32[3,16,256]{2,1,0:T(8,128)S(1)}, u32[]{:S(2)}, u32[]{:S(2)}) collective-permute-start(f32[3,16,256]{2,1,0:T(8,128)S(1)} %fusion), channel_id=1, source_target_pairs={{0,16},{8,24},{16,0},{24,8},{1,17},{9,25},{17,1},{25,9},{2,18},{10... | collective-permute-start | bytes 147464 | tf_op jit(solution)/shard_map/ppermute | solution.py:39
  21.6 4.1 %collective-permute-start.4 = (f32[3,16,256]{2,1,0:T(8,128)S(1)}, f32[3,16,256]{2,1,0:T(8,128)S(1)}, u32[]{:S(2)}, u32[]{:S(2)}) collective-permute-start(f32[3,16,256]{2,1,0:T(8,128)S(1)} %fusion), channel_id=1, source_target_pairs={{0,8},{8,0},{16,24},{24,16},{1,9},{9,1},{17,25},{25,17},{2,10},{10... | collective-permute-start | bytes 147464 | tf_op jit(solution)/shard_map/ppermute | solution.py:39
  26.2 5.7 %collective-permute-start.7 = (f32[64,4,256]{2,1,0:T(4,128)S(1)}, f32[64,4,256]{2,1,0:T(4,128)S(1)}, u32[]{:S(2)}, u32[]{:S(2)}) collective-permute-start(f32[64,4,256]{2,1,0:T(4,128)S(1)} %get-tuple-element.34), channel_id=1, source_target_pairs={{0,1},{1,0},{2,3},{3,2},{4,5},{5,4},{6,7},{7,6},{8,9},{9,8},{10,11... | collective-permute-start | bytes 786440 | tf_op jit(solution)/shard_map/ppermute | solution.py:24
  30.7 1.2 %collective-permute-start.8 = (f32[64,4,256]{2,1,0:T(4,128)S(1)}, f32[64,4,256]{2,1,0:T(4,128)S(1)}, u32[]{:S(2)}, u32[]{:S(2)}) collective-permute-start(f32[64,4,256]{2,1,0:T(4,128)S(1)} %get-tuple-element.35), channel_id=1, source_target_pairs={{1,2},{2,1},{3,4},{4,3},{5,6},{6,5},{9,10},{10,9},{11,12},{12,11},... | collective-permute-start | bytes 786440 | tf_op jit(solution)/shard_map/ppermute | solution.py:23
  37.3 1.2 %copy-start.3 = (f32[64,16,256]{2,1,0:T(8,128)S(1)}, f32[64,16,256]{2,1,0:T(8,128)}, u32[]{:S(2)}) copy-start(f32[64,16,256]{2,1,0:T(8,128)} %param.8) | copy-start | bytes 3145732
  39.8 52.8 %copy-start.1 = (f32[64,16,256]{2,1,0:T(8,128)}, f32[64,16,256]{2,1,0:T(8,128)S(1)}, u32[]{:S(2)}) copy-start(f32[64,16,256]{2,1,0:T(8,128)S(1)} %get-tuple-element.14) | copy-start | bytes 3145732
  39.9 8.9 %collective-permute-start.9 = (f32[64,4,256]{2,1,0:T(4,128)S(1)}, f32[64,4,256]{2,1,0:T(4,128)S(1)}, u32[]{:S(2)}, u32[]{:S(2)}) collective-permute-start(f32[64,4,256]{2,1,0:T(4,128)S(1)} %get-tuple-element.32), channel_id=1, source_target_pairs={{0,1},{1,0},{2,3},{3,2},{4,5},{5,4},{6,7},{7,6},{8,9},{9,8},{10,11... | collective-permute-start | bytes 786440 | tf_op jit(solution)/shard_map/ppermute | solution.py:24
  47.7 1.2 %collective-permute-start.10 = (f32[64,4,256]{2,1,0:T(4,128)S(1)}, f32[64,4,256]{2,1,0:T(4,128)S(1)}, u32[]{:S(2)}, u32[]{:S(2)}) collective-permute-start(f32[64,4,256]{2,1,0:T(4,128)S(1)} %get-tuple-element.33), channel_id=1, source_target_pairs={{1,2},{2,1},{3,4},{4,3},{5,6},{6,5},{9,10},{10,9},{11,12},{12,11},... | collective-permute-start | bytes 786440 | tf_op jit(solution)/shard_map/ppermute | solution.py:23
  55.7 4.2 %collective-permute-start.12 = (f32[56,256]{1,0:T(8,128)S(1)}, f32[56,256]{1,0:T(8,128)S(1)}, u32[]{:S(2)}, u32[]{:S(2)}) collective-permute-start(f32[56,256]{1,0:T(8,128)S(1)} %pad_maximum_fusion.5), channel_id=1, source_target_pairs={{0,16},{8,24},{16,0},{24,8},{1,17},{9,25},{17,1},{25,9},{2,18},{10... | collective-permute-start | bytes 172040 | tf_op jit(solution)/shard_map/ppermute | solution.py:39
  57.3 5.1 %collective-permute-start.13 = (f32[56,256]{1,0:T(8,128)S(1)}, f32[56,256]{1,0:T(8,128)S(1)}, u32[]{:S(2)}, u32[]{:S(2)}) collective-permute-start(f32[56,256]{1,0:T(8,128)S(1)} %pad_maximum_fusion.5), channel_id=1, source_target_pairs={{0,24},{8,16},{16,8},{24,0},{1,25},{9,17},{17,9},{25,1},{2,26},{10... | collective-permute-start | bytes 172040 | tf_op jit(solution)/shard_map/ppermute | solution.py:39
  57.9 4.5 %collective-permute-start.11 = (f32[56,256]{1,0:T(8,128)S(1)}, f32[56,256]{1,0:T(8,128)S(1)}, u32[]{:S(2)}, u32[]{:S(2)}) collective-permute-start(f32[56,256]{1,0:T(8,128)S(1)} %pad_maximum_fusion.5), channel_id=1, source_target_pairs={{0,8},{8,0},{16,24},{24,16},{1,9},{9,1},{17,25},{25,17},{2,10},{10... | collective-permute-start | bytes 172040 | tf_op jit(solution)/shard_map/ppermute | solution.py:39
  62.5 8.2 %collective-permute-start.16 = (f32[16,256]{1,0:T(8,128)S(1)}, f32[16,256]{1,0:T(8,128)S(1)}, u32[]{:S(2)}, u32[]{:S(2)}) collective-permute-start(f32[16,256]{1,0:T(8,128)S(1)} %pad_maximum_fusion.6), channel_id=1, source_target_pairs={{0,1},{1,0},{2,3},{3,2},{4,5},{5,4},{6,7},{7,6},{8,9},{9,8},{10,11... | collective-permute-start | bytes 49160 | tf_op jit(solution)/shard_map/ppermute | solution.py:49
  68.5 1.0 %copy-start.4 = (f32[64,16,256]{2,1,0:T(8,128)}, f32[64,16,256]{2,1,0:T(8,128)S(1)}, u32[]{:S(2)}) copy-start(f32[64,16,256]{2,1,0:T(8,128)S(1)} %fusion.3) | copy-start | bytes 3145732
  69.5 17.6 %copy-start.5 = (f32[64,16,256]{2,1,0:T(8,128)S(1)}, f32[64,16,256]{2,1,0:T(8,128)}, u32[]{:S(2)}) copy-start(f32[64,16,256]{2,1,0:T(8,128)} %copy-done.4) | copy-start | bytes 3145732
  69.5 17.5 %collective-permute-start.14 = (f32[64,4,256]{2,1,0:T(4,128)S(1)}, f32[64,4,256]{2,1,0:T(4,128)S(1)}, u32[]{:S(2)}, u32[]{:S(2)}) collective-permute-start(f32[64,4,256]{2,1,0:T(4,128)S(1)} %get-tuple-element.30), channel_id=1, source_target_pairs={{0,1},{1,0},{2,3},{3,2},{4,5},{5,4},{6,7},{7,6},{8,9},{9,8},{10,11... | collective-permute-start | bytes 786440 | tf_op jit(solution)/shard_map/ppermute | solution.py:24
  69.6 17.4 %collective-permute-start.15 = (f32[64,4,256]{2,1,0:T(4,128)S(1)}, f32[64,4,256]{2,1,0:T(4,128)S(1)}, u32[]{:S(2)}, u32[]{:S(2)}) collective-permute-start(f32[64,4,256]{2,1,0:T(4,128)S(1)} %get-tuple-element.31), channel_id=1, source_target_pairs={{1,2},{2,1},{3,4},{4,3},{5,6},{6,5},{9,10},{10,9},{11,12},{12,11},... | collective-permute-start | bytes 786440 | tf_op jit(solution)/shard_map/ppermute | solution.py:23
  70.7 9.1 %collective-permute-start.17 = (f32[16,256]{1,0:T(8,128)S(1)}, f32[16,256]{1,0:T(8,128)S(1)}, u32[]{:S(2)}, u32[]{:S(2)}) collective-permute-start(f32[16,256]{1,0:T(8,128)S(1)} %fusion.126), channel_id=1, source_target_pairs={{0,2},{1,3},{2,0},{3,1},{4,6},{5,7},{6,4},{7,5},{8,10},{9,11},{10,... | collective-permute-start | bytes 49160 | tf_op jit(solution)/shard_map/ppermute | solution.py:49
  79.9 4.7 %collective-permute-start.18 = (f32[16,256]{1,0:T(8,128)S(1)}, f32[16,256]{1,0:T(8,128)S(1)}, u32[]{:S(2)}, u32[]{:S(2)}) collective-permute-start(f32[16,256]{1,0:T(8,128)S(1)} %add.415), channel_id=1, source_target_pairs={{0,4},{1,5},{2,6},{3,7},{4,0},{5,1},{6,2},{7,3},{8,12},{9,13},{10,... | collective-permute-start | bytes 49160 | tf_op jit(solution)/shard_map/ppermute | solution.py:49

commit v2 on v0

v2 whole, which is shorter than its diff:
```python
import jax
import jax.numpy as jnp
from jax import lax
from jax.experimental import pallas as pl
from jax.experimental.pallas import tpu as pltpu
from jax.sharding import PartitionSpec as P

SWEEPS = 4
SUB = 8
CHUNKS = 4
VMEM_BYTES = 67043328
SPARE = 3072
LANES = 128
PACK = 1
GROUP = 8


def pairs_inner(count):
    return [(i, i ^ 1) for i in range(count) if (i ^ 1) < count]


def pairs_outer(count):
    partner = [(i, i + 1 if i % 2 else i - 1) for i in range(count)]
    return [(i, j) for i, j in partner if 0 <= j < count]


def swap(inner, outer):
    count = lax.axis_size("tile")
    far = lax.ppermute(outer, "tile", pairs_outer(count))
    near = lax.ppermute(inner, "tile", pairs_inner(count))
    return near, far


def others(value, axis, stride=1):
    count = lax.axis_size(axis)
    power = count & (count - 1) == 0
    return [
        lax.ppermute(
            value, axis, [(i, i ^ step if power else (i + step) % count) for i in range(count)]
        )
        for step in range(stride, count, stride)
    ]


def order(width, back):
    wide = PACK * width
    cols, each = wide // LANES, LANES // PACK
    a = jnp.arange(wide, dtype=jnp.int32)
    lane, vector = a % LANES, a // LANES
    source = (lane // each) * width + cols * (lane % each) + vector
    if back:
        return (source[:, None] == a[None, :]).astype(jnp.bfloat16)
    return (a[:, None] == source[None, :]).astype(jnp.bfloat16)


def order_matrix(width):
    wide = PACK * width
    cols, each = wide // LANES, LANES // PACK
    a = lax.broadcasted_iota(jnp.int32, (wide, wide), 1)
    lane, vector = a % LANES, a // LANES
    source = (lane // each) * width + cols * (lane % each) + vector
    return jnp.where(lax.broadcasted_iota(jnp.int32, (wide, wide), 0) == source, 1.0, 0.0).astype(
        jnp.bfloat16
    )


def reordered(x, matrix):
    out = None
    for part in range(3):
        piece = x.astype(jnp.bfloat16)
        term = jnp.dot(piece, matrix, preferred_element_type=jnp.float32)
        out = term if out is None else out + term
        x = x - piece.astype(jnp.float32)
    return out


def columns(c):
    return pl.ds(c * LANES, LANES)


def sides(values, lane):
    last, each = len(values) - 1, LANES // PACK
    right = jnp.where(lane % each == each - 1, 0.0, pltpu.roll(values[0], LANES - 1, 1))
    left = jnp.where(lane % each == 0, 0.0, pltpu.roll(values[last], 1, 1))
    around = [left] + list(values) + [right]
    return [around[c] + around[c + 2] for c in range(last + 1)]


def below_of(x):
    return x[1:] + [pltpu.roll(x[0], SUB - 1, 0)]


def above_of(x):
    return [pltpu.roll(x[-1], 1, 0)] + x[:-1]


def forward(x, coef, lane):
    cols, tiles = len(x), len(x[0])
    lateral = [sides([x[c][t] for c in range(cols)], lane) for t in range(tiles)]
    out = []
    for c in range(cols):
        below, above = below_of(x[c]), above_of(x[c])
        out.append(
            [
                coef[0, c, t] * x[c][t]
                + coef[1, c, t] * below[t]
                + coef[2, c, t] * above[t]
                + coef[3, c, t] * lateral[t][c]
                for t in range(tiles)
            ]
        )
    return out


def adjoint(x, coef, lane):
    cols, tiles = len(x), len(x[0])
    lateral = [
        sides([coef[3, c, t] * x[c][t] for c in range(cols)], lane) for t in range(tiles)
    ]
    out = []
    for c in range(cols):
        below = below_of([coef[2, c, t] * x[c][t] for t in range(tiles)])
        above = above_of([coef[1, c, t] * x[c][t] for t in range(tiles)])
        out.append(
            [
                coef[0, c, t] * x[c][t] + below[t] + above[t] + lateral[t][c]
                for t in range(tiles)
            ]
        )
    return out


def sweeps(step, rows_ref, g, coef, lane, cols, tiles):
    x = [
        [rows_ref[g, c, pl.ds(t, SUB, stride=tiles), :] for t in range(tiles)]
        for c in range(cols)
    ]
    for _ in range(SWEEPS):
        x = step(x, coef, lane)
    for c in range(cols):
        for t in range(tiles):
            rows_ref[g, c, pl.ds(t, SUB, stride=tiles), :] = x[c][t]


def lane_of():
    return lax.broadcasted_iota(jnp.int32, (SUB, LANES), 1)


def sub_of():
    return lax.broadcasted_iota(jnp.int32, (SUB, LANES), 0)


def is_odd():
    return lax.axis_index("tile") % 2 == 1


def call(kernel, outs, scratch, operands, near=None, flops=1, limit=24 * 2**20):
    near = len(operands) if near is None else len(operands) + near
    nbytes = sum(x.size * x.dtype.itemsize for x in operands)
    return pl.pallas_call(
        kernel,
        out_shape=outs,
        in_specs=[
            pl.BlockSpec(memory_space=pltpu.VMEM if k < near else pl.ANY)
            for k in range(len(operands))
        ],
        out_specs=[pl.BlockSpec(memory_space=pltpu.VMEM)] * len(outs),
        scratch_shapes=scratch,
        compiler_params=pltpu.CompilerParams(vmem_limit_bytes=limit),
        cost_estimate=pl.CostEstimate(flops=flops, bytes_accessed=nbytes, transcendentals=0),
    )(*operands)


def f32(*shape):
    return jax.ShapeDtypeStruct(shape, jnp.float32)


def edge_kernel(members, control, diffusion, advection, upwind, near, far, fields, buf, number,
                stage, sems):
    _, rows, width = control.shape
    chunk = members // CHUNKS
    copies = [
        pltpu.make_async_copy(
            control.at[pl.ds(i * chunk, chunk)], buf.at[pl.ds(i * chunk, chunk)], sems.at[i]
        )
        for i in range(CHUNKS)
    ] + [
        pltpu.make_async_copy(diffusion, fields.at[0], sems.at[CHUNKS]),
        pltpu.make_async_copy(advection, fields.at[1], sems.at[CHUNKS + 1]),
        pltpu.make_async_copy(upwind, number, sems.at[CHUNKS + 2]),
    ]
    for copy in copies[CHUNKS:] + copies[:CHUNKS]:
        copy.start()
    odd, turn = is_odd(), order_matrix(width)
    sub = lax.broadcasted_iota(jnp.int32, (SUB, width), 0)
    last = pl.ds(rows - SUB, SUB)
    for copy in copies[CHUNKS:]:
        copy.wait()
    fields[2] = number[...].astype(jnp.float32)
    for q in range(3):
        top, end = fields[q, pl.ds(0, SUB), :], fields[q, last, :]
        at = pl.ds(members // PACK * SWEEPS + q * SUB, SUB)
        for b in range(PACK):
            cs = pl.ds(b * width, width)
            stage[0, at, cs] = jnp.where(odd, top, end)
            stage[1, at, cs] = jnp.where(odd, end, top)
    pairs = chunk // (2 * PACK)
    for k in range(members // (2 * PACK)):
        if k % pairs == 0:
            copies[k // pairs].wait()
        at = pl.ds(k * SUB, SUB)
        for b in range(PACK):
            first, second = 2 * PACK * k + b, 2 * PACK * k + PACK + b
            cs = pl.ds(b * width, width)
            x, y = buf[first, pl.ds(0, SUB), :], buf[second, pl.ds(0, SUB), :]
            top = jnp.where(sub < SWEEPS, x, pltpu.roll(y, SWEEPS, 0))
            x, y = buf[first, last, :], buf[second, last, :]
            end = jnp.where(sub < SWEEPS, pltpu.roll(x, SWEEPS, 0), y)
            stage[0, at, cs] = jnp.where(odd, top, end)
            stage[1, at, cs] = jnp.where(odd, end, top)
    near[...] = reordered(stage[0], turn)
    far[...] = reordered(stage[1], turn)


def side_by_side(parts):
    return jnp.concatenate(
        [jnp.concatenate(parts[i : i + PACK], 1) for i in range(0, len(parts), PACK)], 0
    )


def order_kernel(times, members, control, fields, pert, matrix, control_out, fields_out, pert_out):
    _, rows, width = control.shape
    turn = matrix[...]
    chunk = 2 * GROUP * PACK

    def group(step, carry):
        out = pl.ds(step * 2 * GROUP, 2 * GROUP)
        block = side_by_side([control[step * chunk + k] for k in range(chunk)])
        control_out[out] = reordered(block, turn).reshape((2 * GROUP,) + control_out.shape[1:])
        block = side_by_side(
            [pert[t, step * chunk + k] for t in range(times) for k in range(chunk)]
        )
        turned = jnp.dot(block, turn, preferred_element_type=jnp.float32).astype(jnp.bfloat16)
        turned = turned.reshape((times, 2 * GROUP) + pert_out.shape[2:])
        for t in range(times):
            pert_out[t, out] = turned[t]
        return carry

    lax.fori_loop(0, members // chunk, group, 0)
    plane_kernel(fields, matrix, fields_out)


def plane_kernel(*refs):
    count = len(refs) // 2
    turn = refs[count][...]
    for ref, out in zip(refs[:count], refs[count + 1 :]):
        block = ref[...].reshape(ref.shape[0] * ref.shape[1], ref.shape[2])
        out[...] = reordered(jnp.concatenate([block] * PACK, 1), turn).reshape(out.shape)


def restore_packs(first, count, field, turn, out):
    rows, width = out.shape[1:]
    block = field[pl.ds(first, count)].reshape(count * rows, PACK * width)
    block = reordered(block, turn)
    for k in range(count):
        for b in range(PACK):
            out[(first + k) * PACK + b] = block[
                k * rows : (k + 1) * rows, b * width : (b + 1) * width
            ]


def restore_kernel(packs, field, matrix, out, token):
    turn = matrix[...]
    token[...] = jnp.zeros_like(token)

    def group(step, carry):
        restore_packs(step * 4 * GROUP, 4 * GROUP, field, turn, out)
        return carry

    lax.fori_loop(0, packs // (4 * GROUP), group, 0)


def coefficients_into(fields, halo_low, halo_high, base, out3, out4, ring, dims):
    cols, own = dims
    sub = sub_of()
    fields3, fields4 = [], []
    for q in range(3):
        for c in range(cols):
            for i in range(own):
                ring[0, c, pl.ds(i * SUB, SUB), :] = fields[q, pl.ds(i * SUB, SUB), columns(c)]
            high = halo_high(base + q * SUB, c)
            low = halo_low(base + q * SUB, c)
            ring[0, c, pl.ds(own * SUB, SUB), :] = high
            ring[0, c, pl.ds((own + 1) * SUB, SUB), :] = low
            n = own + 2
            fields4.append([ring[0, c, pl.ds(t, SUB, stride=n), :] for t in range(n)])
            ring[0, c, pl.ds(own * SUB, SUB), :] = jnp.where(sub < SWEEPS, high, low)
            n = own + 1
            fields3.append([ring[0, c, pl.ds(t, SUB, stride=n), :] for t in range(n)])
    for fields, out in ((fields3, out3), (fields4, out4)):
        for c in range(cols):
            for t in range(len(fields[0])):
                kappa, advect, upper = (fields[q * cols + c][t] for q in range(3))
                toward = advect * upper
                out[0, c, t] = 1.0 - 4.0 * kappa - advect
                out[1, c, t] = kappa + toward
                out[2, c, t] = kappa + (advect - toward)
                out[3, c, t] = kappa


def project_member(pert, m, rows_ref, g, total, dims):
    cols, own = dims
    out = [[list(col) for col in per_time] for per_time in total]
    for c in range(cols):
        field = [rows_ref[g, c, pl.ds(i * SUB, SUB), :] for i in range(own)]
        for t in range(len(total)):
            weight = pert[t, m, :, columns(c)].astype(jnp.float32)
            for i in range(own):
                out[t][c][i] = total[t][c][i] + weight[i * SUB : (i + 1) * SUB] * field[i]
    return out


def zeros(times, dims):
    cols, own = dims
    zero = jnp.zeros((SUB, LANES), jnp.float32)
    return [[[zero] * own for _ in range(cols)] for _ in range(times)]


def write_sums(ref, total, dims, lane):
    cols, own = dims
    half = LANES // PACK
    for t, per_time in enumerate(total):
        for c in range(0, cols, PACK):
            for i in range(own):
                if PACK == 1:
                    ref[pl.ds((t * own + i) * SUB, SUB), columns(c)] = per_time[c][i]
                    continue
                x, y = (per_time[c + b][i] for b in range(PACK))
                x, y = x + pltpu.roll(x, half, 1), y + pltpu.roll(y, half, 1)
                ref[pl.ds((t * own + i) * SUB, SUB), columns(c // PACK)] = jnp.where(
                    lane < half, x, y
                )


def first_kernel(dims, times, members, control, near, far, fields, pert, sums, out3,
                 out4, halo, ring):
    cols, own = dims
    lane, sub, odd = lane_of(), sub_of(), is_odd()

    def high_of(start, c):
        rows = pl.ds(start, SUB)
        return jnp.where(odd, far[rows, columns(c)], near[rows, columns(c)])

    def low_of(start, c):
        rows = pl.ds(start, SUB)
        return jnp.where(odd, near[rows, columns(c)], far[rows, columns(c)])

    coefficients_into(
        fields, low_of, high_of, members * SWEEPS, out3, out4, ring, dims
    )

    def group(step, total):
        for pair in range(GROUP // 2):
            first = step * GROUP + 2 * pair
            start = pl.multiple_of(first * SWEEPS, SUB)
            for c in range(cols):
                high, low = high_of(start, c), low_of(start, c)
                edges = (
                    jnp.where(sub < SWEEPS, high, pltpu.roll(low, SWEEPS, 0)),
                    jnp.where(sub < SWEEPS, pltpu.roll(high, SWEEPS, 0), low),
                )
                for k in range(2):
                    g = 2 * pair + k
                    for i in range(own):
                        rows = pl.ds(i * SUB, SUB)
                        ring[g, c, rows, :] = control[first + k, rows, columns(c)]
                    ring[g, c, pl.ds(own * SUB, SUB), :] = edges[k]
                    halo[first + k, :, columns(c)] = edges[k]
        for g in range(GROUP):
            sweeps(forward, ring, g, out3, lane, cols, own + 1)
            total = project_member(pert, step * GROUP + g, ring, g, total, dims)
        return total

    total = lax.fori_loop(0, members // GROUP, group, zeros(times, dims))
    write_sums(sums, total, dims, lane)


def pull_member(pert, m, weights, c, own):
    out = None
    for t in range(len(weights)):
        value = pert[t, m, :, columns(c)].astype(jnp.float32)
        terms = [value[i * SUB : (i + 1) * SUB] * weights[t][c][i] for i in range(own)]
        out = terms if out is None else [a + b for a, b in zip(out, terms)]
    return out


def gathered(parts, rows, c):
    out = parts[0][rows, columns(c)]
    for part in parts[1:]:
        out = out + part[rows, columns(c)]
    return out


def totals_of(parts, t, i, dims, lane):
    cols, own = dims
    half = LANES // PACK
    out = []
    for c in range(cols // PACK):
        x = gathered(parts, pl.ds((t * own + i) * SUB, SUB), c)
        if PACK == 1:
            out.append(x)
            continue
        y = pltpu.roll(x, half, 1)
        out += [jnp.where(lane < half, x, y), jnp.where(lane < half, y, x)]
    return out


def second_kernel(dims, times, members, count, *refs):
    cols, own = dims
    parts, (innovation, weight, pert, near, far, rest) = refs[:count], refs[count:]
    odd, lane = is_odd(), lane_of()
    weights = []
    for t in range(times):
        weights.append([[None] * own for _ in range(cols)])
        for i in range(own):
            rows = pl.ds(i * SUB, SUB)
            total = totals_of(parts, t, i, dims, lane)
            for c in range(cols):
                weights[t][c][i] = weight[t, rows, columns(c)] * (
                    total[c] - innovation[t, rows, columns(c)]
                )

    def group(step, carry):
        for g in range(GROUP):
            m = step * GROUP + g
            for c in range(cols):
                tiles = pull_member(pert, m, weights, c, own)
                near[m, :, columns(c)] = jnp.where(odd, tiles[0], tiles[-1])
                far[m, :, columns(c)] = jnp.where(odd, tiles[-1], tiles[0])
                for i in range(1, own - 1):
                    rest[m, pl.ds((i - 1) * SUB, SUB), columns(c)] = tiles[i]
        return carry

    lax.fori_loop(0, members // GROUP, group, 0)


def third_kernel(dims, times, members, control, halo, near, far, rest, from_near, from_far,
                 coef3, coef4, pert, gradient, sums, ring, ring3):
    cols, own = dims
    lane, sub, odd = lane_of(), sub_of(), is_odd()
    index = lax.axis_index("tile")
    inside = jnp.where(
        sub < SWEEPS,
        jnp.where(index < lax.axis_size("tile") - 1, 1.0, 0.0),
        jnp.where(index > 0, 1.0, 0.0),
    )

    def group(step, carry):
        total, square = carry
        for g in range(GROUP):
            m = step * GROUP + g
            for c in range(cols):
                cs = columns(c)
                a, b = near[m, :, cs], far[m, :, cs]
                ring[g, c, pl.ds(0, SUB), :] = jnp.where(odd, a, b)
                ring[g, c, pl.ds((own - 1) * SUB, SUB), :] = jnp.where(odd, b, a)
                for i in range(1, own - 1):
                    ring[g, c, pl.ds(i * SUB, SUB), :] = rest[m, pl.ds((i - 1) * SUB, SUB), cs]
                a, b = from_near[m, :, cs], from_far[m, :, cs]
                ring[g, c, pl.ds(own * SUB, SUB), :] = jnp.where(odd, b, a)
                ring[g, c, pl.ds((own + 1) * SUB, SUB), :] = jnp.where(odd, a, b)
        for g in range(GROUP):
            m = step * GROUP + g
            sweeps(adjoint, ring, g, coef4, lane, cols, own + 2)
            for c in range(cols):
                cs = columns(c)
                for i in range(own):
                    rows = pl.ds(i * SUB, SUB)
                    value = control[m, rows, cs] + ring[g, c, rows, :]
                    gradient[m, rows, cs] = value
                    ring3[g, c, rows, :] = value
                    square = square + value * value
                edge = jnp.where(
                    sub < SWEEPS,
                    ring[g, c, pl.ds(own * SUB, SUB), :],
                    ring[g, c, pl.ds((own + 1) * SUB, SUB), :],
                )
                ring3[g, c, pl.ds(own * SUB, SUB), :] = inside * (halo[m, :, cs] + edge)
            sweeps(forward, ring3, g, coef3, lane, cols, own + 1)
            total = project_member(pert, m, ring3, g, total, dims)
        return total, square

    total, square = lax.fori_loop(
        0,
        members // GROUP,
        group,
        (zeros(times, dims), jnp.zeros((SUB, LANES), jnp.float32)),
    )
    write_sums(sums, total, dims, lane)
    sums[pl.ds(times * own * SUB, SUB), :] = jnp.zeros((SUB, sums.shape[1]), jnp.float32)
    sums[pl.ds(times * own * SUB, SUB), columns(0)] = square


def fourth_kernel(dims, times, members, count, *refs):
    cols, own = dims
    parts, (weight, pert, _, field, near, far) = refs[:count], refs[count:]
    odd, sub, lane = is_odd(), sub_of(), lane_of()
    weights = []
    curve = jnp.zeros((SUB, LANES), jnp.float32)
    for t in range(times):
        weights.append([[None] * own for _ in range(cols)])
        for i in range(own):
            total = totals_of(parts, t, i, dims, lane)
            for c in range(cols):
                weights[t][c][i] = weight[t, pl.ds(i * SUB, SUB), columns(c)] * total[c]
                curve = curve + total[c] * weights[t][c][i]
    square = gathered(parts, pl.ds(times * own * SUB, SUB), 0)
    base = members * SWEEPS
    near[pl.ds(base, 2 * SUB), :] = jnp.zeros((2 * SUB, near.shape[1]), jnp.float32)
    near[pl.ds(base, SUB), columns(0)] = square
    near[pl.ds(base + SUB, SUB), columns(0)] = curve * (1.0 / PACK)

    def group(step, carry):
        for pair in range(GROUP // 2):
            first = step * GROUP + 2 * pair
            start = pl.multiple_of(first * SWEEPS, SUB)
            for c in range(cols):
                cs = columns(c)
                both = []
                for k in range(2):
                    tiles = pull_member(pert, first + k, weights, c, own)
                    for i in range(own):
                        field[first + k, pl.ds(i * SUB, SUB), cs] = tiles[i]
                    both.append(tiles)
                top = jnp.where(sub < SWEEPS, both[0][0], pltpu.roll(both[1][0], SWEEPS, 0))
                end = jnp.where(sub < SWEEPS, pltpu.roll(both[0][-1], SWEEPS, 0), both[1][-1])
                near[pl.ds(start, SUB), cs] = jnp.where(odd, top, end)
                far[pl.ds(start, SUB), cs] = jnp.where(odd, end, top)
        return carry

    lax.fori_loop(0, members // GROUP, group, 0)


def fifth_kernel(dims, members, field, near, far, coef3, gradient, matrix, *refs):
    scalars, (product, length, ring, turned) = refs[:-4], refs[-4:]
    cols, own = dims
    lane, sub, odd = lane_of(), sub_of(), is_odd()
    turn = matrix[...]

    def group(step):
        for pair in range(GROUP // 2):
            first = step * GROUP + 2 * pair
            start = first * SWEEPS
            rows8 = pl.ds(start if isinstance(step, int) else pl.multiple_of(start, SUB), SUB)
            for c in range(cols):
                cs = columns(c)
                a, b = near[rows8, cs], far[rows8, cs]
                high, low = jnp.where(odd, b, a), jnp.where(odd, a, b)
                edges = (
                    jnp.where(sub < SWEEPS, high, pltpu.roll(low, SWEEPS, 0)),
                    jnp.where(sub < SWEEPS, pltpu.roll(high, SWEEPS, 0), low),
                )
                for k in range(2):
                    g = 2 * pair + k
                    for i in range(own):
                        rows = pl.ds(i * SUB, SUB)
                        ring[g, c, rows, :] = field[first + k, rows, cs]
                    ring[g, c, pl.ds(own * SUB, SUB), :] = edges[k]
        for g in range(GROUP):
            m = step * GROUP + g
            sweeps(adjoint, ring, g, coef3, lane, cols, own + 1)
            for c in range(cols):
                for i in range(own):
                    rows = pl.ds(i * SUB, SUB)
                    turned[m, rows, columns(c)] = (
                        gradient[m, rows, columns(c)] + ring[g, c, rows, :]
                    )

    def both(step, carry):
        restore_packs((step - 1) * GROUP, GROUP, turned, turn, product)
        group(step)
        return carry

    total = sum((ref[...] for ref in scalars[1:]), scalars[0][...])
    square = jnp.sum(total[:SUB], keepdims=True)
    length[...] = square / (square + jnp.sum(total[SUB:], keepdims=True))
    group(0)
    lax.fori_loop(1, members // GROUP, both, 0)
    restore_packs(members - GROUP, GROUP, turned, turn, product)


def bind(kernel, *static):
    def bound(*refs):
        kernel(*static, *refs)

    return bound


def shards(perturbations, control, innovation, obs_weight, diffusion, advection, upwind):
    times, members, rows, width = perturbations.shape
    packs, wide = members // PACK, PACK * width
    cols, own = wide // LANES, rows // SUB
    dims = (cols, own)

    turn, back = order(width, False), order(width, True)
    edge = f32(packs * SWEEPS + 3 * SUB, wide)
    planes = f32(3, rows, width)
    near, far, fields = call(
        bind(edge_kernel, members),
        [edge, edge, planes],
        [
            pltpu.VMEM(control.shape, jnp.float32),
            pltpu.VMEM((rows, width), jnp.int32),
            pltpu.VMEM((2,) + edge.shape, jnp.float32),
            pltpu.SemaphoreType.DMA((CHUNKS + 3,)),
        ],
        [control, diffusion, advection, upwind],
        near=-4,
        limit=VMEM_BYTES - 4 * (2 * edge.size + planes.size + SPARE),
    )
    near, far = swap(near, far)
    packed = f32(packs, rows, wide)
    per_time = f32(times, rows, wide)
    gradient_shape = f32(*control.shape)
    control, fields, perturbations = call(
        bind(order_kernel, times, members),
        [packed, f32(3, rows, wide), jax.ShapeDtypeStruct((times,) + packed.shape, jnp.bfloat16)],
        [],
        [control, fields, perturbations, turn],
        flops=2_000_000_000,
    )
    innovation, obs_weight = call(
        plane_kernel, [per_time, per_time], [], [innovation, obs_weight, turn], flops=200_000_000
    )

    def ring_of(n):
        return pltpu.VMEM((GROUP, cols, n * SUB, LANES), jnp.float32)

    sums, coef3, coef4, halo = call(
        bind(first_kernel, dims, times, packs),
        [
            f32(times * rows, width),
            f32(4, cols, own + 1, SUB, LANES),
            f32(4, cols, own + 2, SUB, LANES),
            f32(packs, SUB, wide),
        ],
        [ring_of(own + 2)],
        [control, near, far, fields, perturbations],
        flops=4_000_000_000,
    )
    parts = [sums] + others(sums, "mem")
    edges = f32(packs, SUB, wide)
    near, far, rest = call(
        bind(second_kernel, dims, times, packs, len(parts)),
        [edges, edges, f32(packs, max(own - 2, 1) * SUB, wide)],
        [],
        parts + [innovation, obs_weight, perturbations],
    )
    from_near, from_far = swap(near, far)
    gradient, sums = call(
        bind(third_kernel, dims, times, packs),
        [packed, f32(times * rows + SUB, width)],
        [ring_of(own + 2), ring_of(own + 1)],
        [control, halo, near, far, rest, from_near, from_far, coef3, coef4, perturbations],
        flops=8_000_000_000,
    )
    parts = [sums] + others(sums, "mem")
    restored, token = call(
        bind(restore_kernel, packs),
        [gradient_shape, f32(SUB, LANES)],
        [],
        [gradient, back],
        flops=1_000_000_000,
    )
    field, near, far = call(
        bind(fourth_kernel, dims, times, packs, len(parts)),
        [packed, f32(packs * SWEEPS + 2 * SUB, wide), f32(packs * SWEEPS, wide)],
        [],
        parts + [obs_weight, perturbations, token],
    )
    from_near, from_far = swap(near, far)
    one = near[packs * SWEEPS :, :LANES] + from_near[packs * SWEEPS :, :LANES]
    scalars = [one] + others(one, "tile", 2)
    product, length = call(
        bind(fifth_kernel, dims, packs),
        [gradient_shape, f32(1, 1)],
        [ring_of(own + 1), pltpu.VMEM(gradient.shape, jnp.float32)],
        [field, from_near, from_far, coef3, gradient, back] + scalars,
        flops=4_000_000_000,
    )
    return restored, product, length[0, 0]


def solution(mesh):
    return jax.shard_map(
        shards,
        mesh=mesh,
        in_specs=(
            P(None, "mem", "tile", None),
            P("mem", "tile", None),
            P(None, "tile", None),
            P(None, "tile", None),
            P("tile", None),
            P("tile", None),
            P("tile", None),
        ),
        out_specs=(P("mem", "tile", None), P("mem", "tile", None), P()),
        check_vma=False,
    )
```

time: 156 us -> 63 us (0.40)
  blocking collectives: 75.7 us -> 0 us
  other arithmetic: 30.8 us -> 0.11 us
  Pallas kernels: 0 us -> 20.9 us
  between operations: 4.95 us -> 0.77 us
  local copies, waits for them, and re-layouts: 7.32 us -> 3.44 us
  waiting for transfers between devices: 8.78 us -> 10.6 us
    psum x3 -> x0, blocking collectives: 75.7 us -> none  [the longest x1 44.5 us: shards(): lax.psum((jnp.sum(gradient * gradient), curvature_term), ('mem', 'tile'))]
    pallas_call x0 -> x9, Pallas kernels: none -> 20.9 us  [call(): pl.pallas_call(kernel, out_shape=outs, in_specs=[pl.BlockSpec(memory_spac...]
    mul x21 -> x0, other arithmetic: 20 us -> none  [the longest x8 11.2 us: localise(): forward_core(extended, kappa_wide[first_row:last_row], advect_wide[first_...]
    slice x32 -> x0, local copies, waits for them, and re-layouts: 4.25 us -> none  [the longest x4 1.57 us: extended_2(): lax.slice_in_dim(block, block.shape[dim] - width, None, axis=dim)]
    reduce_sum x6 -> x0, other arithmetic: 3.76 us -> none  [the longest x1 1.76 us: shards(): jnp.sum(gradient * gradient)]
    concatenate x5 -> x0, other arithmetic: 3.31 us -> none  [extended_2(): block = jnp.concatenate([low, block, high], axis=dim)]
    add x1 -> x2, other arithmetic: 2.05 us -> 0.01 us  [the longest x1 0.01 us: order(): source = lane // each * width + cols * (lane % each) + vector]
    ppermute x10 -> x15, waiting for transfers between devices: 8.78 us -> 10.6 us  [the longest x9 9.19 us: others(): lax.ppermute(value, axis, [(i, i ^ step if power else (i + step) % count)...]
  transfers between devices with their start and end apart: 10 -> 15, of which waited for: 3 -> 8; matrix products, arithmetic and copies ran while one was open for 2% -> 0% of each run, Pallas kernels for 0% -> 6%
where the time goes in v2:
time: 63 us; the launch traced here: 62.7 us
  starting transfers between devices  26.9 us (43%)
  Pallas kernels  20.9 us (33%)
  waiting for transfers between devices  10.6 us (17%)
  local copies, waits for them, and re-layouts  3.44 us (5%)
  between operations  0.77 us (1%)
    pallas_call x9, Pallas kernels, call(): pl.pallas_call(kernel, out_shape=outs, in_specs=[pl.BlockSpec(memory_spac...  20.9 us
    ppermute x9, starting transfers between devices, others(): lax.ppermute(value, axis, [(i, i ^ step if power else (i + step) % count)...  15.1 us
    ppermute x3, starting transfers between devices, swap(): near = lax.ppermute(inner, 'tile', pairs_inner(count))  9.82 us
    ppermute x9, waiting for transfers between devices, others(): lax.ppermute(value, axis, [(i, i ^ step if power else (i + step) % count)...  9.19 us
    unnamed x10, local copies, waits for them, and re-layouts  3.44 us
    ppermute x3, starting transfers between devices, swap(): far = lax.ppermute(outer, 'tile', pairs_outer(count))  2.01 us
    ppermute x3, waiting for transfers between devices, swap(): near = lax.ppermute(inner, 'tile', pairs_inner(count))  1.39 us
  transfers between devices with their start and end apart: 15, of which 8 were waited for; matrix products, arithmetic and copies ran while one was open for 0% of the time, Pallas kernels for 6%

profile of v2, /device:TPU:0, one launch (start us, length us, event | category | flops | bytes accessed | tf_op | source)
XLA Modules:
  0.0 62.7 jit_solution(17981523992124865321)
XLA Ops:
  0.6 2.5 %shard_map.94 = (f32[280,256]{1,0:T(8,128)}, f32[280,256]{1,0:T(8,128)}, f32[3,16,256]{2,1,0:T(8,128)}) custom-call(f32[64,16,256]{2,1,0:T(8,128)} %refs_0_.4, f32[16,256]{1,0:T(8,128)} %refs_1_.2, f32[16,256]{1,0:T(8,128)} %refs_2_.2, s32[16,256]{1,0:T(8,128)} %refs_3_.1), custom_call_target="tpu_custom_call" | custom-call | flops 1 | bytes 1097728 | tf_op jit(solution)/shard_map/pallas_call | solution.py:160
  3.1 0.6 collective-permute-start
  3.7 0.7 %collective-permute-start.1 = (f32[280,256]{1,0:T(8,128)}, f32[280,256]{1,0:T(8,128)S(1)}, u32[]{:S(2)}, u32[]{:S(2)}) collective-permute-start(f32[280,256]{1,0:T(8,128)} %get-tuple-element.30), channel_id=1, source_target_pairs={{1,2},{2,1},{3,4},{4,3},{5,6},{6,5},{9,10},{10,9},{11,12},{12,11},... | collective-permute-start | bytes 860168 | tf_op jit(solution)/shard_map/ppermute | solution.py:29
  4.5 1.2 %copy-done = f32[64,16,256]{2,1,0:T(8,128)S(1)} copy-done((f32[64,16,256]{2,1,0:T(8,128)S(1)}, f32[64,16,256]{2,1,0:T(8,128)}, u32[]{:S(2)}) %copy-start) | copy-done | bytes 1048600
  5.7 1.4 %copy-done.1 = bf16[3,64,16,256]{3,2,1,0:T(8,128)(2,1)S(1)} copy-done((bf16[3,64,16,256]{3,2,1,0:T(8,128)(2,1)S(1)}, bf16[3,64,16,256]{3,2,1,0:T(8,128)(2,1)}, u32[]{:S(2)}) %copy-start.1) | copy-done | bytes 1572888
  7.1 0.8 %copy-done.4 = f32[3,16,256]{2,1,0:T(8,128)S(1)} copy-done((f32[3,16,256]{2,1,0:T(8,128)S(1)}, f32[3,16,256]{2,1,0:T(8,128)}, u32[]{:S(2)}) %copy-start.4) | copy-done | bytes 49176
  7.9 1.7 %shard_map.95 = (f32[64,16,256]{2,1,0:T(8,128)S(1)}, f32[3,16,256]{2,1,0:T(8,128)S(1)}, bf16[3,64,16,256]{3,2,1,0:T(8,128)(2,1)S(1)}) custom-call(f32[64,16,256]{2,1,0:T(8,128)S(1)} %copy-done, f32[3,16,256]{2,1,0:T(8,128)S(1)} %copy-done.4, bf16[3,64,16,256]{3,2,1,0:T(8,128)(2,1)S(1)} %copy-done.1, bf16[256,256]{1,0:T(8,128)(2,1)S(1)} %get-tuple-element.52.refs_3_.refs_2_), custom_call_target="tpu_custom_call" | custom-call | flops 2000000000 | bytes 2801664 | tf_op jit(solution)/shard_map/pallas_call | solution.py:160
  9.7 3.1 %shard_map.96 = (f32[48,256]{1,0:T(8,128)S(1)}, f32[4,2,3,8,128]{4,3,2,1,0:T(8,128)S(1)}, f32[4,2,4,8,128]{4,3,2,1,0:T(8,128)S(1)}, f32[64,8,256]{2,1,0:T(8,128)S(1)}) custom-call(f32[64,16,256]{2,1,0:T(8,128)S(1)} %get-tuple-element.28.refs_0_, f32[280,256]{1,0:T(8,128)S(1)} %collective-permute-done.refs_1_, f32[280,256]{1,0:T(8,128)S(1)} %collective-permute-done.1.refs_2_, ...), custom_call_target="tpu_custom_call" | custom-call | flops 4000000000 | bytes 3244032 | tf_op jit(solution)/shard_map/pallas_call | solution.py:160
  12.8 3.5 %collective-permute-start.4 = (f32[48,256]{1,0:T(8,128)S(1)}, f32[48,256]{1,0:T(8,128)S(1)}, u32[]{:S(2)}, u32[]{:S(2)}) collective-permute-start(f32[48,256]{1,0:T(8,128)S(1)} %get-tuple-element.34.refs_0_), channel_id=1, source_target_pairs={{0,24},{8,16},{16,8},{24,0},{1,25},{9,17},{17,9},{25,1},{2,26},{10... | collective-permute-start | bytes 147464 | tf_op jit(solution)/shard_map/ppermute | solution.py:38
  16.3 0.5 collective-permute-start.3
  17.2 1.2 %collective-permute-done.4.refs_3_ = f32[48,256]{1,0:T(8,128)S(1)} collective-permute-done((f32[48,256]{1,0:T(8,128)S(1)}, f32[48,256]{1,0:T(8,128)S(1)}, u32[]{:S(2)}, u32[]{:S(2)}) %collective-permute-start.4) | collective-permute-done | bytes 49184 | tf_op jit(solution)/shard_map/ppermute | solution.py:38
  18.4 2.5 %collective-permute-done.3.refs_2_ = f32[48,256]{1,0:T(8,128)S(1)} collective-permute-done((f32[48,256]{1,0:T(8,128)S(1)}, f32[48,256]{1,0:T(8,128)S(1)}, u32[]{:S(2)}, u32[]{:S(2)}) %collective-permute-start.3) | collective-permute-done | bytes 49184 | tf_op jit(solution)/shard_map/ppermute | solution.py:38
  21.0 0.5 collective-permute-done.2.refs_1_
  21.4 0.4 shard_map.98
  21.8 0.8 %collective-permute-start.5 = (f32[64,8,256]{2,1,0:T(8,128)S(1)}, f32[64,8,256]{2,1,0:T(8,128)S(1)}, u32[]{:S(2)}, u32[]{:S(2)}) collective-permute-start(f32[64,8,256]{2,1,0:T(8,128)S(1)} %get-tuple-element.37.refs_2_), channel_id=1, source_target_pairs={{0,1},{1,0},{2,3},{3,2},{4,5},{5,4},{6,7},{7,6},{8,9},{9,8},{10,11... | collective-permute-start | bytes 1572872 | tf_op jit(solution)/shard_map/ppermute | solution.py:30
  22.6 0.7 %collective-permute-start.6 = (f32[64,8,256]{2,1,0:T(8,128)S(1)}, f32[64,8,256]{2,1,0:T(8,128)S(1)}, u32[]{:S(2)}, u32[]{:S(2)}) collective-permute-start(f32[64,8,256]{2,1,0:T(8,128)S(1)} %get-tuple-element.38.refs_3_), channel_id=1, source_target_pairs={{1,2},{2,1},{3,4},{4,3},{5,6},{6,5},{9,10},{10,9},{11,12},{12,11},... | collective-permute-start | bytes 1572872 | tf_op jit(solution)/shard_map/ppermute | solution.py:29
  23.3 0.8 %collective-permute-done.5.refs_5_ = f32[64,8,256]{2,1,0:T(8,128)S(1)} collective-permute-done((f32[64,8,256]{2,1,0:T(8,128)S(1)}, f32[64,8,256]{2,1,0:T(8,128)S(1)}, u32[]{:S(2)}, u32[]{:S(2)}) %collective-permute-start.5) | collective-permute-done | bytes 524320 | tf_op jit(solution)/shard_map/ppermute | solution.py:30
  24.1 6.5 %shard_map.99 = (f32[64,16,256]{2,1,0:T(8,128)S(1)}, f32[56,256]{1,0:T(8,128)S(1)}) custom-call(f32[64,16,256]{2,1,0:T(8,128)S(1)} %get-tuple-element.28.refs_0_, f32[64,8,256]{2,1,0:T(8,128)S(1)} %get-tuple-element.33.refs_1_, f32[64,8,256]{2,1,0:T(8,128)S(1)} %get-tuple-element.37.refs_2_, f32[64,8,256]{2,1,0:T(8,128)S(1)} %get-tuple-element.38.refs_3_, ...), custom_call_target="tpu_custom_call" | custom-call | flops 8000000000 | bytes 5996544 | tf_op jit(solution)/shard_map/pallas_call | solution.py:160
  30.6 1.6 %collective-permute-start.9 = (f32[56,256]{1,0:T(8,128)S(1)}, f32[56,256]{1,0:T(8,128)S(1)}, u32[]{:S(2)}, u32[]{:S(2)}) collective-permute-start(f32[56,256]{1,0:T(8,128)S(1)} %get-tuple-element.44.refs_0_), channel_id=1, source_target_pairs={{0,24},{8,16},{16,8},{24,0},{1,25},{9,17},{17,9},{25,1},{2,26},{10... | collective-permute-start | bytes 172040 | tf_op jit(solution)/shard_map/ppermute | solution.py:38
  32.2 0.6 collective-permute-start.8
  32.8 1.4 %collective-permute-start.7 = (f32[56,256]{1,0:T(8,128)S(1)}, f32[56,256]{1,0:T(8,128)S(1)}, u32[]{:S(2)}, u32[]{:S(2)}) collective-permute-start(f32[56,256]{1,0:T(8,128)S(1)} %get-tuple-element.44.refs_0_), channel_id=1, source_target_pairs={{0,8},{8,0},{16,24},{24,16},{1,9},{9,1},{17,25},{25,17},{2,10},{10... | collective-permute-start | bytes 172040 | tf_op jit(solution)/shard_map/ppermute | solution.py:38
  34.2 1.8 %shard_map.100 = (f32[64,16,256]{2,1,0:T(8,128)}, f32[8,128]{1,0:T(8,128)S(1)}) custom-call(f32[64,16,256]{2,1,0:T(8,128)S(1)} %get-tuple-element.42.refs_0_.refs_4_, bf16[256,256]{1,0:T(8,128)(2,1)S(1)} %get-tuple-element.51.refs_1_.refs_5_), custom_call_target="tpu_custom_call" | custom-call | flops 1000000000 | bytes 1179648 | tf_op jit(solution)/shard_map/pallas_call | solution.py:160
  36.0 0.4 collective-permute-done.8.refs_2_
  36.4 0.6 collective-permute-done.7.refs_1_
  37.0 0.4 shard_map.101
  37.4 8.5 %collective-permute-start.10 = (f32[272,256]{1,0:T(8,128)S(1)}, f32[272,256]{1,0:T(8,128)S(1)}, u32[]{:S(2)}, u32[]{:S(2)}) collective-permute-start(f32[272,256]{1,0:T(8,128)S(1)} %get-tuple-element.47), channel_id=1, source_target_pairs={{0,1},{1,0},{2,3},{3,2},{4,5},{5,4},{6,7},{7,6},{8,9},{9,8},{10,11... | collective-permute-start | bytes 835592 | tf_op jit(solution)/shard_map/ppermute | solution.py:30
  45.8 0.7 %collective-permute-start.11 = (f32[256,256]{1,0:T(8,128)S(1)}, f32[256,256]{1,0:T(8,128)S(1)}, u32[]{:S(2)}, u32[]{:S(2)}) collective-permute-start(f32[256,256]{1,0:T(8,128)S(1)} %get-tuple-element.48), channel_id=1, source_target_pairs={{1,2},{2,1},{3,4},{4,3},{5,6},{6,5},{9,10},{10,9},{11,12},{12,11},... | collective-permute-start | bytes 786440 | tf_op jit(solution)/shard_map/ppermute | solution.py:29
  46.5 0.5 collective-permute-done.10.refs_1_
  47.0 6.7 %collective-permute-start.14 = (f32[16,128]{1,0:T(8,128)S(1)}, f32[16,128]{1,0:T(8,128)S(1)}, u32[]{:S(2)}, u32[]{:S(2)}) collective-permute-start(f32[16,128]{1,0:T(8,128)S(1)} %slice_add_fusion.refs_6_), channel_id=1, source_target_pairs={{0,6},{1,7},{2,4},{3,5},{4,2},{5,3},{6,0},{7,1},{8,14},{9,15},{10,... | collective-permute-start | bytes 24584 | tf_op jit(solution)/shard_map/ppermute | solution.py:38
  53.7 0.6 %collective-permute-start.12 = (f32[16,128]{1,0:T(8,128)S(1)}, f32[16,128]{1,0:T(8,128)S(1)}, u32[]{:S(2)}, u32[]{:S(2)}) collective-permute-start(f32[16,128]{1,0:T(8,128)S(1)} %slice_add_fusion.refs_6_), channel_id=1, source_target_pairs={{0,2},{1,3},{2,0},{3,1},{4,6},{5,7},{6,4},{7,5},{8,10},{9,11},{10,... | collective-permute-start | bytes 24584 | tf_op jit(solution)/shard_map/ppermute | solution.py:38
  54.4 4.0 %collective-permute-done.14.refs_9_ = f32[16,128]{1,0:T(8,128)S(1)} collective-permute-done((f32[16,128]{1,0:T(8,128)S(1)}, f32[16,128]{1,0:T(8,128)S(1)}, u32[]{:S(2)}, u32[]{:S(2)}) %collective-permute-start.14) | collective-permute-done | bytes 8224 | tf_op jit(solution)/shard_map/ppermute | solution.py:38
  58.4 4.3 %shard_map.102 = (f32[64,16,256]{2,1,0:T(8,128)}, f32[1,1]{1,0:T(1,128)}) custom-call(f32[64,16,256]{2,1,0:T(8,128)S(1)} %get-tuple-element.46.refs_0_, f32[272,256]{1,0:T(8,128)S(1)} %collective-permute-done.10.refs_1_, f32[256,256]{1,0:T(8,128)S(1)} %collective-permute-done.11.refs_2_, f32[4,2,3,8,128]{4,3,2,1,0:T(8,128)S(1)} %get-tuple-element.40.refs_7_.refs_3_, ...), custom_call_target="tpu_custom_call" | custom-call | flops 4000000000 | bytes 2899968 | tf_op jit(solution)/shard_map/pallas_call | solution.py:160
  (20 shorter events, 0.5 us)
Async XLA Ops:
  3.1 6.5 %collective-permute-start = (f32[280,256]{1,0:T(8,128)}, f32[280,256]{1,0:T(8,128)S(1)}, u32[]{:S(2)}, u32[]{:S(2)}) collective-permute-start(f32[280,256]{1,0:T(8,128)} %get-tuple-element.29), channel_id=1, source_target_pairs={{0,1},{1,0},{2,3},{3,2},{4,5},{5,4},{6,7},{7,6},{8,9},{9,8},{10,11... | collective-permute-start | bytes 860168 | tf_op jit(solution)/shard_map/ppermute | solution.py:30
  3.7 5.9 %collective-permute-start.1 = (f32[280,256]{1,0:T(8,128)}, f32[280,256]{1,0:T(8,128)S(1)}, u32[]{:S(2)}, u32[]{:S(2)}) collective-permute-start(f32[280,256]{1,0:T(8,128)} %get-tuple-element.30), channel_id=1, source_target_pairs={{1,2},{2,1},{3,4},{4,3},{5,6},{6,5},{9,10},{10,9},{11,12},{12,11},... | collective-permute-start | bytes 860168 | tf_op jit(solution)/shard_map/ppermute | solution.py:29
  4.5 1.2 %copy-start = (f32[64,16,256]{2,1,0:T(8,128)S(1)}, f32[64,16,256]{2,1,0:T(8,128)}, u32[]{:S(2)}) copy-start(f32[64,16,256]{2,1,0:T(8,128)} %refs_0_.4) | copy-start | bytes 3145732
  5.7 1.4 %copy-start.1 = (bf16[3,64,16,256]{3,2,1,0:T(8,128)(2,1)S(1)}, bf16[3,64,16,256]{3,2,1,0:T(8,128)(2,1)}, u32[]{:S(2)}) copy-start(bf16[3,64,16,256]{3,2,1,0:T(8,128)(2,1)} %refs_2_.3) | copy-start | bytes 4718596
  7.1 0.8 %copy-start.4 = (f32[3,16,256]{2,1,0:T(8,128)S(1)}, f32[3,16,256]{2,1,0:T(8,128)}, u32[]{:S(2)}) copy-start(f32[3,16,256]{2,1,0:T(8,128)} %get-tuple-element.27.refs_1_) | copy-start | bytes 147460
  9.6 7.3 %copy-start.2 = (f32[3,16,256]{2,1,0:T(8,128)S(1)}, f32[3,16,256]{2,1,0:T(8,128)}, u32[]{:S(2)}) copy-start(f32[3,16,256]{2,1,0:T(8,128)} %refs_0_.5) | copy-start | bytes 147460
  9.7 7.3 %copy-start.3 = (f32[3,16,256]{2,1,0:T(8,128)S(1)}, f32[3,16,256]{2,1,0:T(8,128)}, u32[]{:S(2)}) copy-start(f32[3,16,256]{2,1,0:T(8,128)} %refs_1_.3) | copy-start | bytes 147460
  12.8 5.6 %collective-permute-start.4 = (f32[48,256]{1,0:T(8,128)S(1)}, f32[48,256]{1,0:T(8,128)S(1)}, u32[]{:S(2)}, u32[]{:S(2)}) collective-permute-start(f32[48,256]{1,0:T(8,128)S(1)} %get-tuple-element.34.refs_0_), channel_id=1, source_target_pairs={{0,24},{8,16},{16,8},{24,0},{1,25},{9,17},{17,9},{25,1},{2,26},{10... | collective-permute-start | bytes 147464 | tf_op jit(solution)/shard_map/ppermute | solution.py:38
  16.3 4.6 %collective-permute-start.3 = (f32[48,256]{1,0:T(8,128)S(1)}, f32[48,256]{1,0:T(8,128)S(1)}, u32[]{:S(2)}, u32[]{:S(2)}) collective-permute-start(f32[48,256]{1,0:T(8,128)S(1)} %get-tuple-element.34.refs_0_), channel_id=1, source_target_pairs={{0,16},{8,24},{16,0},{24,8},{1,17},{9,25},{17,1},{25,9},{2,18},{10... | collective-permute-start | bytes 147464 | tf_op jit(solution)/shard_map/ppermute | solution.py:38
  16.8 4.6 %collective-permute-start.2 = (f32[48,256]{1,0:T(8,128)S(1)}, f32[48,256]{1,0:T(8,128)S(1)}, u32[]{:S(2)}, u32[]{:S(2)}) collective-permute-start(f32[48,256]{1,0:T(8,128)S(1)} %get-tuple-element.34.refs_0_), channel_id=1, source_target_pairs={{0,8},{8,0},{16,24},{24,16},{1,9},{9,1},{17,25},{25,17},{2,10},{10... | collective-permute-start | bytes 147464 | tf_op jit(solution)/shard_map/ppermute | solution.py:38
  21.8 2.3 %collective-permute-start.5 = (f32[64,8,256]{2,1,0:T(8,128)S(1)}, f32[64,8,256]{2,1,0:T(8,128)S(1)}, u32[]{:S(2)}, u32[]{:S(2)}) collective-permute-start(f32[64,8,256]{2,1,0:T(8,128)S(1)} %get-tuple-element.37.refs_2_), channel_id=1, source_target_pairs={{0,1},{1,0},{2,3},{3,2},{4,5},{5,4},{6,7},{7,6},{8,9},{9,8},{10,11... | collective-permute-start | bytes 1572872 | tf_op jit(solution)/shard_map/ppermute | solution.py:30
  22.6 1.5 %collective-permute-start.6 = (f32[64,8,256]{2,1,0:T(8,128)S(1)}, f32[64,8,256]{2,1,0:T(8,128)S(1)}, u32[]{:S(2)}, u32[]{:S(2)}) collective-permute-start(f32[64,8,256]{2,1,0:T(8,128)S(1)} %get-tuple-element.38.refs_3_), channel_id=1, source_target_pairs={{1,2},{2,1},{3,4},{4,3},{5,6},{6,5},{9,10},{10,9},{11,12},{12,11},... | collective-permute-start | bytes 1572872 | tf_op jit(solution)/shard_map/ppermute | solution.py:29
  30.6 5.3 %collective-permute-start.9 = (f32[56,256]{1,0:T(8,128)S(1)}, f32[56,256]{1,0:T(8,128)S(1)}, u32[]{:S(2)}, u32[]{:S(2)}) collective-permute-start(f32[56,256]{1,0:T(8,128)S(1)} %get-tuple-element.44.refs_0_), channel_id=1, source_target_pairs={{0,24},{8,16},{16,8},{24,0},{1,25},{9,17},{17,9},{25,1},{2,26},{10... | collective-permute-start | bytes 172040 | tf_op jit(solution)/shard_map/ppermute | solution.py:38
  32.2 4.2 %collective-permute-start.8 = (f32[56,256]{1,0:T(8,128)S(1)}, f32[56,256]{1,0:T(8,128)S(1)}, u32[]{:S(2)}, u32[]{:S(2)}) collective-permute-start(f32[56,256]{1,0:T(8,128)S(1)} %get-tuple-element.44.refs_0_), channel_id=1, source_target_pairs={{0,16},{8,24},{16,0},{24,8},{1,17},{9,25},{17,1},{25,9},{2,18},{10... | collective-permute-start | bytes 172040 | tf_op jit(solution)/shard_map/ppermute | solution.py:38
  32.8 4.2 %collective-permute-start.7 = (f32[56,256]{1,0:T(8,128)S(1)}, f32[56,256]{1,0:T(8,128)S(1)}, u32[]{:S(2)}, u32[]{:S(2)}) collective-permute-start(f32[56,256]{1,0:T(8,128)S(1)} %get-tuple-element.44.refs_0_), channel_id=1, source_target_pairs={{0,8},{8,0},{16,24},{24,16},{1,9},{9,1},{17,25},{25,17},{2,10},{10... | collective-permute-start | bytes 172040 | tf_op jit(solution)/shard_map/ppermute | solution.py:38
  37.4 9.7 %collective-permute-start.10 = (f32[272,256]{1,0:T(8,128)S(1)}, f32[272,256]{1,0:T(8,128)S(1)}, u32[]{:S(2)}, u32[]{:S(2)}) collective-permute-start(f32[272,256]{1,0:T(8,128)S(1)} %get-tuple-element.47), channel_id=1, source_target_pairs={{0,1},{1,0},{2,3},{3,2},{4,5},{5,4},{6,7},{7,6},{8,9},{9,8},{10,11... | collective-permute-start | bytes 835592 | tf_op jit(solution)/shard_map/ppermute | solution.py:30
  45.8 8.6 %collective-permute-start.11 = (f32[256,256]{1,0:T(8,128)S(1)}, f32[256,256]{1,0:T(8,128)S(1)}, u32[]{:S(2)}, u32[]{:S(2)}) collective-permute-start(f32[256,256]{1,0:T(8,128)S(1)} %get-tuple-element.48), channel_id=1, source_target_pairs={{1,2},{2,1},{3,4},{4,3},{5,6},{6,5},{9,10},{10,9},{11,12},{12,11},... | collective-permute-start | bytes 786440 | tf_op jit(solution)/shard_map/ppermute | solution.py:29
  47.0 11.4 %collective-permute-start.14 = (f32[16,128]{1,0:T(8,128)S(1)}, f32[16,128]{1,0:T(8,128)S(1)}, u32[]{:S(2)}, u32[]{:S(2)}) collective-permute-start(f32[16,128]{1,0:T(8,128)S(1)} %slice_add_fusion.refs_6_), channel_id=1, source_target_pairs={{0,6},{1,7},{2,4},{3,5},{4,2},{5,3},{6,0},{7,1},{8,14},{9,15},{10,... | collective-permute-start | bytes 24584 | tf_op jit(solution)/shard_map/ppermute | solution.py:38
  53.7 4.6 %collective-permute-start.13 = (f32[16,128]{1,0:T(8,128)S(1)}, f32[16,128]{1,0:T(8,128)S(1)}, u32[]{:S(2)}, u32[]{:S(2)}) collective-permute-start(f32[16,128]{1,0:T(8,128)S(1)} %slice_add_fusion.refs_6_), channel_id=1, source_target_pairs={{0,4},{1,5},{2,6},{3,7},{4,0},{5,1},{6,2},{7,3},{8,12},{9,13},{10,... | collective-permute-start | bytes 24584 | tf_op jit(solution)/shard_map/ppermute | solution.py:38
  53.7 4.6 %collective-permute-start.12 = (f32[16,128]{1,0:T(8,128)S(1)}, f32[16,128]{1,0:T(8,128)S(1)}, u32[]{:S(2)}, u32[]{:S(2)}) collective-permute-start(f32[16,128]{1,0:T(8,128)S(1)} %slice_add_fusion.refs_6_), channel_id=1, source_target_pairs={{0,2},{1,3},{2,0},{3,1},{4,6},{5,7},{6,4},{7,5},{8,10},{9,11},{10,... | collective-permute-start | bytes 24584 | tf_op jit(solution)/shard_map/ppermute | solution.py:38

commit v3 on v2

--- a/solution.py
+++ b/solution.py
@@ -8,6 +8,7 @@
 SWEEPS = 4
 SUB = 8
 CHUNKS = 4
+UNROLL = 7
 VMEM_BYTES = 67043328
 SPARE = 3072
 LANES = 128
@@ -65,13 +66,11 @@
 
 
 def reordered(x, matrix):
-    out = None
-    for part in range(3):
-        piece = x.astype(jnp.bfloat16)
-        term = jnp.dot(piece, matrix, preferred_element_type=jnp.float32)
-        out = term if out is None else out + term
-        x = x - piece.astype(jnp.float32)
-    return out
+    high = x.astype(jnp.bfloat16)
+    low = (x - high.astype(jnp.float32)).astype(jnp.bfloat16)
+    return jnp.dot(high, matrix, preferred_element_type=jnp.float32) + jnp.dot(
+        low, matrix, preferred_element_type=jnp.float32
+    )
 
 
 def columns(c):
@@ -240,7 +239,7 @@
         block = side_by_side(
             [pert[t, step * chunk + k] for t in range(times) for k in range(chunk)]
         )
-        turned = jnp.dot(block, turn, preferred_element_type=jnp.float32).astype(jnp.bfloat16)
+        turned = jnp.dot(block, turn, preferred_element_type=jnp.float32)
         turned = turned.reshape((times, 2 * GROUP) + pert_out.shape[2:])
         for t in range(times):
             pert_out[t, out] = turned[t]
@@ -272,40 +271,29 @@
 def restore_kernel(packs, field, matrix, out, token):
     turn = matrix[...]
     token[...] = jnp.zeros_like(token)
-
-    def group(step, carry):
-        restore_packs(step * 4 * GROUP, 4 * GROUP, field, turn, out)
-        return carry
-
-    lax.fori_loop(0, packs // (4 * GROUP), group, 0)
-
-
-def coefficients_into(fields, halo_low, halo_high, base, out3, out4, ring, dims):
-    cols, own = dims
-    sub = sub_of()
-    fields3, fields4 = [], []
+    for step in range(packs // GROUP):
+        restore_packs(step * GROUP, GROUP, field, turn, out)
+
+
+def coefficients_into(fields, halo_low, halo_high, base, out, ring, dims):
+    cols, own = dims
+    sub, n = sub_of(), own + 1
+    strided = []
     for q in range(3):
         for c in range(cols):
             for i in range(own):
                 ring[0, c, pl.ds(i * SUB, SUB), :] = fields[q, pl.ds(i * SUB, SUB), columns(c)]
-            high = halo_high(base + q * SUB, c)
-            low = halo_low(base + q * SUB, c)
-            ring[0, c, pl.ds(own * SUB, SUB), :] = high
-            ring[0, c, pl.ds((own + 1) * SUB, SUB), :] = low
-            n = own + 2
-            fields4.append([ring[0, c, pl.ds(t, SUB, stride=n), :] for t in range(n)])
+            high, low = halo_high(base + q * SUB, c), halo_low(base + q * SUB, c)
             ring[0, c, pl.ds(own * SUB, SUB), :] = jnp.where(sub < SWEEPS, high, low)
-            n = own + 1
-            fields3.append([ring[0, c, pl.ds(t, SUB, stride=n), :] for t in range(n)])
-    for fields, out in ((fields3, out3), (fields4, out4)):
-        for c in range(cols):
-            for t in range(len(fields[0])):
-                kappa, advect, upper = (fields[q * cols + c][t] for q in range(3))
-                toward = advect * upper
-                out[0, c, t] = 1.0 - 4.0 * kappa - advect
-                out[1, c, t] = kappa + toward
-                out[2, c, t] = kappa + (advect - toward)
-                out[3, c, t] = kappa
+            strided.append([ring[0, c, pl.ds(t, SUB, stride=n), :] for t in range(n)])
+    for c in range(cols):
+        for t in range(n):
+            kappa, advect, upper = (strided[q * cols + c][t] for q in range(3))
+            toward = advect * upper
+            out[0, c, t] = 1.0 - 4.0 * kappa - advect
+            out[1, c, t] = kappa + toward
+            out[2, c, t] = kappa + (advect - toward)
+            out[3, c, t] = kappa
 
 
 def project_member(pert, m, rows_ref, g, total, dims):
@@ -314,7 +302,7 @@
     for c in range(cols):
         field = [rows_ref[g, c, pl.ds(i * SUB, SUB), :] for i in range(own)]
         for t in range(len(total)):
-            weight = pert[t, m, :, columns(c)].astype(jnp.float32)
+            weight = pert[t, m, :, columns(c)]
             for i in range(own):
                 out[t][c][i] = total[t][c][i] + weight[i * SUB : (i + 1) * SUB] * field[i]
     return out
@@ -343,7 +331,7 @@
 
 
 def first_kernel(dims, times, members, control, near, far, fields, pert, sums, out3,
-                 out4, halo, ring):
+                 halo, ring):
     cols, own = dims
     lane, sub, odd = lane_of(), sub_of(), is_odd()
 
@@ -356,7 +344,7 @@
         return jnp.where(odd, near[rows, columns(c)], far[rows, columns(c)])
 
     coefficients_into(
-        fields, low_of, high_of, members * SWEEPS, out3, out4, ring, dims
+        fields, low_of, high_of, members * SWEEPS, out3, ring, dims
     )
 
     def group(step, total):
@@ -388,7 +376,7 @@
 def pull_member(pert, m, weights, c, own):
     out = None
     for t in range(len(weights)):
-        value = pert[t, m, :, columns(c)].astype(jnp.float32)
+        value = pert[t, m, :, columns(c)]
         terms = [value[i * SUB : (i + 1) * SUB] * weights[t][c][i] for i in range(own)]
         out = terms if out is None else [a + b for a, b in zip(out, terms)]
     return out
@@ -415,10 +403,24 @@
     return out
 
 
+def pulled_sweeps(step, weights, pert, ring, coef3, lane, dims):
+    cols, own = dims
+    for g in range(GROUP):
+        for c in range(cols):
+            tiles = pull_member(pert, step * GROUP + g, weights, c, own)
+            for i in range(own):
+                ring[g, c, pl.ds(i * SUB, SUB), :] = tiles[i]
+            ring[g, c, pl.ds(own * SUB, SUB), :] = jnp.zeros((SUB, LANES), jnp.float32)
+        sweeps(adjoint, ring, g, coef3, lane, cols, own + 1)
+
+
 def second_kernel(dims, times, members, count, *refs):
     cols, own = dims
-    parts, (innovation, weight, pert, near, far, rest) = refs[:count], refs[count:]
-    odd, lane = is_odd(), lane_of()
+    parts, (innovation, weight, pert, coef3, near, far, field, spill, ring) = (
+        refs[:count],
+        refs[count:],
+    )
+    odd, lane, sub = is_odd(), lane_of(), sub_of()
     weights = []
     for t in range(times):
         weights.append([[None] * own for _ in range(cols)])
@@ -431,21 +433,26 @@
                 )
 
     def group(step, carry):
+        pulled_sweeps(step, weights, pert, ring, coef3, lane, dims)
         for g in range(GROUP):
             m = step * GROUP + g
             for c in range(cols):
-                tiles = pull_member(pert, m, weights, c, own)
-                near[m, :, columns(c)] = jnp.where(odd, tiles[0], tiles[-1])
-                far[m, :, columns(c)] = jnp.where(odd, tiles[-1], tiles[0])
-                for i in range(1, own - 1):
-                    rest[m, pl.ds((i - 1) * SUB, SUB), columns(c)] = tiles[i]
+                cs = columns(c)
+                tiles = [ring[g, c, pl.ds(i * SUB, SUB), :] for i in range(own + 1)]
+                for i in range(own):
+                    field[m, pl.ds(i * SUB, SUB), cs] = tiles[i]
+                spill[m, :, cs] = tiles[own]
+                low = jnp.where(sub < SWEEPS, tiles[0], tiles[own])
+                high = jnp.where(sub < SWEEPS, tiles[own], tiles[own - 1])
+                near[m, :, cs] = jnp.where(odd, low, high)
+                far[m, :, cs] = jnp.where(odd, high, low)
         return carry
 
     lax.fori_loop(0, members // GROUP, group, 0)
 
 
-def third_kernel(dims, times, members, control, halo, near, far, rest, from_near, from_far,
-                 coef3, coef4, pert, gradient, sums, ring, ring3):
+def third_kernel(dims, times, members, control, halo, field, spill, from_near, from_far, coef3,
+                 pert, gradient, sums, ring):
     cols, own = dims
     lane, sub, odd = lane_of(), sub_of(), is_odd()
     index = lax.axis_index("tile")
@@ -461,33 +468,23 @@
             m = step * GROUP + g
             for c in range(cols):
                 cs = columns(c)
-                a, b = near[m, :, cs], far[m, :, cs]
-                ring[g, c, pl.ds(0, SUB), :] = jnp.where(odd, a, b)
-                ring[g, c, pl.ds((own - 1) * SUB, SUB), :] = jnp.where(odd, b, a)
-                for i in range(1, own - 1):
-                    ring[g, c, pl.ds(i * SUB, SUB), :] = rest[m, pl.ds((i - 1) * SUB, SUB), cs]
                 a, b = from_near[m, :, cs], from_far[m, :, cs]
-                ring[g, c, pl.ds(own * SUB, SUB), :] = jnp.where(odd, b, a)
-                ring[g, c, pl.ds((own + 1) * SUB, SUB), :] = jnp.where(odd, a, b)
-        for g in range(GROUP):
-            m = step * GROUP + g
-            sweeps(adjoint, ring, g, coef4, lane, cols, own + 2)
-            for c in range(cols):
-                cs = columns(c)
+                high, low = jnp.where(odd, b, a), jnp.where(odd, a, b)
                 for i in range(own):
                     rows = pl.ds(i * SUB, SUB)
-                    value = control[m, rows, cs] + ring[g, c, rows, :]
+                    value = control[m, rows, cs] + field[m, rows, cs]
+                    if i == 0:
+                        value = value + jnp.where(sub < SWEEPS, low, 0.0)
+                    if i == own - 1:
+                        value = value + jnp.where(sub < SWEEPS, 0.0, high)
                     gradient[m, rows, cs] = value
-                    ring3[g, c, rows, :] = value
+                    ring[g, c, rows, :] = value
                     square = square + value * value
-                edge = jnp.where(
-                    sub < SWEEPS,
-                    ring[g, c, pl.ds(own * SUB, SUB), :],
-                    ring[g, c, pl.ds((own + 1) * SUB, SUB), :],
-                )
-                ring3[g, c, pl.ds(own * SUB, SUB), :] = inside * (halo[m, :, cs] + edge)
-            sweeps(forward, ring3, g, coef3, lane, cols, own + 1)
-            total = project_member(pert, m, ring3, g, total, dims)
+                edge = jnp.where(sub < SWEEPS, high, low) + spill[m, :, cs]
+                ring[g, c, pl.ds(own * SUB, SUB), :] = inside * (halo[m, :, cs] + edge)
+        for g in range(GROUP):
+            sweeps(forward, ring, g, coef3, lane, cols, own + 1)
+            total = project_member(pert, step * GROUP + g, ring, g, total, dims)
         return total, square
 
     total, square = lax.fori_loop(
@@ -503,7 +500,7 @@
 
 def fourth_kernel(dims, times, members, count, *refs):
     cols, own = dims
-    parts, (weight, pert, _, field, near, far) = refs[:count], refs[count:]
+    parts, (weight, pert, _, coef3, gradient, field, near, far, ring) = refs[:count], refs[count:]
     odd, sub, lane = is_odd(), sub_of(), lane_of()
     weights = []
     curve = jnp.zeros((SUB, LANES), jnp.float32)
@@ -521,30 +518,32 @@
     near[pl.ds(base + SUB, SUB), columns(0)] = curve * (1.0 / PACK)
 
     def group(step, carry):
+        pulled_sweeps(step, weights, pert, ring, coef3, lane, dims)
         for pair in range(GROUP // 2):
             first = step * GROUP + 2 * pair
             start = pl.multiple_of(first * SWEEPS, SUB)
             for c in range(cols):
                 cs = columns(c)
-                both = []
                 for k in range(2):
-                    tiles = pull_member(pert, first + k, weights, c, own)
                     for i in range(own):
-                        field[first + k, pl.ds(i * SUB, SUB), cs] = tiles[i]
-                    both.append(tiles)
-                top = jnp.where(sub < SWEEPS, both[0][0], pltpu.roll(both[1][0], SWEEPS, 0))
-                end = jnp.where(sub < SWEEPS, pltpu.roll(both[0][-1], SWEEPS, 0), both[1][-1])
-                near[pl.ds(start, SUB), cs] = jnp.where(odd, top, end)
-                far[pl.ds(start, SUB), cs] = jnp.where(odd, end, top)
+                        rows = pl.ds(i * SUB, SUB)
+                        field[first + k, rows, cs] = (
+                            gradient[first + k, rows, cs] + ring[2 * pair + k, c, rows, :]
+                        )
+                x, y = (ring[2 * pair + k, c, pl.ds(own * SUB, SUB), :] for k in range(2))
+                high = jnp.where(sub < SWEEPS, x, pltpu.roll(y, SWEEPS, 0))
+                low = jnp.where(sub < SWEEPS, pltpu.roll(x, SWEEPS, 0), y)
+                near[pl.ds(start, SUB), cs] = jnp.where(odd, low, high)
+                far[pl.ds(start, SUB), cs] = jnp.where(odd, high, low)
         return carry
 
     lax.fori_loop(0, members // GROUP, group, 0)
 
 
-def fifth_kernel(dims, members, field, near, far, coef3, gradient, matrix, *refs):
-    scalars, (product, length, ring, turned) = refs[:-4], refs[-4:]
-    cols, own = dims
-    lane, sub, odd = lane_of(), sub_of(), is_odd()
+def fifth_kernel(dims, members, field, near, far, matrix, product, token, whole):
+    token[...] = jnp.zeros_like(token)
+    cols, own = dims
+    sub, odd = sub_of(), is_odd()
     turn = matrix[...]
 
     def group(step):
@@ -556,37 +555,36 @@
                 cs = columns(c)
                 a, b = near[rows8, cs], far[rows8, cs]
                 high, low = jnp.where(odd, b, a), jnp.where(odd, a, b)
-                edges = (
-                    jnp.where(sub < SWEEPS, high, pltpu.roll(low, SWEEPS, 0)),
-                    jnp.where(sub < SWEEPS, pltpu.roll(high, SWEEPS, 0), low),
-                )
+                lows = (low, pltpu.roll(low, SWEEPS, 0))
+                highs = (pltpu.roll(high, SWEEPS, 0), high)
                 for k in range(2):
-                    g = 2 * pair + k
                     for i in range(own):
                         rows = pl.ds(i * SUB, SUB)
-                        ring[g, c, rows, :] = field[first + k, rows, cs]
-                    ring[g, c, pl.ds(own * SUB, SUB), :] = edges[k]
-        for g in range(GROUP):
-            m = step * GROUP + g
-            sweeps(adjoint, ring, g, coef3, lane, cols, own + 1)
-            for c in range(cols):
-                for i in range(own):
-                    rows = pl.ds(i * SUB, SUB)
-                    turned[m, rows, columns(c)] = (
-                        gradient[m, rows, columns(c)] + ring[g, c, rows, :]
-                    )
+                        value = field[first + k, rows, cs]
+                        if i == 0:
+                            value = value + jnp.where(sub < SWEEPS, lows[k], 0.0)
+                        if i == own - 1:
+                            value = value + jnp.where(sub < SWEEPS, 0.0, highs[k])
+                        whole[first + k, rows, cs] = value
 
     def both(step, carry):
-        restore_packs((step - 1) * GROUP, GROUP, turned, turn, product)
+        restore_packs((step - 1) * GROUP, GROUP, whole, turn, product)
         group(step)
         return carry
 
+    group(0)
+    lax.fori_loop(1, members // GROUP, both, 0, unroll=UNROLL)
+    restore_packs(members - GROUP, GROUP, whole, turn, product)
+
+
+def length_kernel(*refs):
+    scalars, length = refs[:-2], refs[-1]
     total = sum((ref[...] for ref in scalars[1:]), scalars[0][...])
-    square = jnp.sum(total[:SUB], keepdims=True)
-    length[...] = square / (square + jnp.sum(total[SUB:], keepdims=True))
-    group(0)
-    lax.fori_loop(1, members // GROUP, both, 0)
-    restore_packs(members - GROUP, GROUP, turned, turn, product)
+    square, curve = (
+        jnp.sum(jnp.sum(x, axis=0, keepdims=True), axis=1, keepdims=True)
+        for x in (total[:SUB], total[SUB:])
+    )
+    length[...] = square / (square + curve)
 
 
 def bind(kernel, *static):
@@ -624,7 +622,7 @@
     gradient_shape = f32(*control.shape)
     control, fields, perturbations = call(
         bind(order_kernel, times, members),
-        [packed, f32(3, rows, wide), jax.ShapeDtypeStruct((times,) + packed.shape, jnp.bfloat16)],
+        [packed, f32(3, rows, wide), f32(times, *packed.shape)],
         [],
         [control, fields, perturbations, turn],
         flops=2_000_000_000,
@@ -636,33 +634,32 @@
     def ring_of(n):
         return pltpu.VMEM((GROUP, cols, n * SUB, LANES), jnp.float32)
 
-    sums, coef3, coef4, halo = call(
+    sums, coef3, halo = call(
         bind(first_kernel, dims, times, packs),
         [
             f32(times * rows, width),
             f32(4, cols, own + 1, SUB, LANES),
-            f32(4, cols, own + 2, SUB, LANES),
             f32(packs, SUB, wide),
         ],
-        [ring_of(own + 2)],
+        [ring_of(own + 1)],
         [control, near, far, fields, perturbations],
         flops=4_000_000_000,
     )
     parts = [sums] + others(sums, "mem")
     edges = f32(packs, SUB, wide)
-    near, far, rest = call(
+    near, far, field, spill = call(
         bind(second_kernel, dims, times, packs, len(parts)),
-        [edges, edges, f32(packs, max(own - 2, 1) * SUB, wide)],
-        [],
-        parts + [innovation, obs_weight, perturbations],
+        [edges, edges, packed, edges],
+        [ring_of(own + 1)],
+        parts + [innovation, obs_weight, perturbations, coef3],
     )
     from_near, from_far = swap(near, far)
     gradient, sums = call(
         bind(third_kernel, dims, times, packs),
         [packed, f32(times * rows + SUB, width)],
-        [ring_of(own + 2), ring_of(own + 1)],
-        [control, halo, near, far, rest, from_near, from_far, coef3, coef4, perturbations],
-        flops=8_000_000_000,
+        [ring_of(own + 1)],
+        [control, halo, field, spill, from_near, from_far, coef3, perturbations],
+        flops=4_000_000_000,
     )
     parts = [sums] + others(sums, "mem")
     restored, token = call(
@@ -675,19 +672,20 @@
     field, near, far = call(
         bind(fourth_kernel, dims, times, packs, len(parts)),
         [packed, f32(packs * SWEEPS + 2 * SUB, wide), f32(packs * SWEEPS, wide)],
-        [],
-        parts + [obs_weight, perturbations, token],
+        [ring_of(own + 1)],
+        parts + [obs_weight, perturbations, token, coef3, gradient],
     )
     from_near, from_far = swap(near, far)
     one = near[packs * SWEEPS :, :LANES] + from_near[packs * SWEEPS :, :LANES]
     scalars = [one] + others(one, "tile", 2)
-    product, length = call(
+    product, token = call(
         bind(fifth_kernel, dims, packs),
-        [gradient_shape, f32(1, 1)],
-        [ring_of(own + 1), pltpu.VMEM(gradient.shape, jnp.float32)],
-        [field, from_near, from_far, coef3, gradient, back] + scalars,
-        flops=4_000_000_000,
-    )
+        [gradient_shape, f32(SUB, LANES)],
+        [pltpu.VMEM(gradient.shape, jnp.float32)],
+        [field, from_near, from_far, back],
+        flops=1_000_000_000,
+    )
+    (length,) = call(length_kernel, [f32(1, 1)], [], scalars + [token])
     return restored, product, length[0, 0]
 
 

time: 63 us -> 61.4 us (0.975)
  waiting for transfers between devices: 10.6 us -> 9.5 us
  Pallas kernels: 20.9 us -> 20.2 us
    ppermute x9, waiting for transfers between devices: 9.19 us -> 8.13 us  [others(): lax.ppermute(value, axis, [(i, i ^ step if power else (i + step) % count)...]
    pallas_call x9 -> x10, Pallas kernels: 20.9 us -> 20.2 us  [call(): pl.pallas_call(kernel, out_shape=outs, in_specs=[pl.BlockSpec(memory_spac...]
  transfers between devices with their start and end apart: 15 -> 15, of which waited for: 8 -> 9; matrix products, arithmetic and copies ran while one was open for 0% -> 0% of each run, Pallas kernels for 6% -> 7%
where the time goes in v3:
time: 61.4 us; the launch traced here: 61.1 us
  starting transfers between devices  27.1 us (44%)
  Pallas kernels  20.2 us (33%)
  waiting for transfers between devices  9.5 us (15%)
  local copies, waits for them, and re-layouts  3.44 us (6%)
  between operations  0.77 us (1%)
    pallas_call x10, Pallas kernels, call(): pl.pallas_call(kernel, out_shape=outs, in_specs=[pl.BlockSpec(memory_spac...  20.2 us
    ppermute x9, starting transfers between devices, others(): lax.ppermute(value, axis, [(i, i ^ step if power else (i + step) % count)...  15 us
    ppermute x3, starting transfers between devices, swap(): near = lax.ppermute(inner, 'tile', pairs_inner(count))  10.1 us
    ppermute x9, waiting for transfers between devices, others(): lax.ppermute(value, axis, [(i, i ^ step if power else (i + step) % count)...  8.13 us
    unnamed x10, local copies, waits for them, and re-layouts  3.44 us
    ppermute x3, starting transfers between devices, swap(): far = lax.ppermute(outer, 'tile', pairs_outer(count))  2.01 us
    ppermute x3, waiting for transfers between devices, swap(): near = lax.ppermute(inner, 'tile', pairs_inner(count))  1.36 us
  transfers between devices with their start and end apart: 15, of which 9 were waited for; matrix products, arithmetic and copies ran while one was open for 0% of the time, Pallas kernels for 7%

profile of v3, /device:TPU:0, one launch (start us, length us, event | category | flops | bytes accessed | tf_op | source)
XLA Modules:
  0.0 61.1 jit_solution(3011937224010125960)
XLA Ops:
  0.6 2.4 %shard_map.94 = (f32[280,256]{1,0:T(8,128)}, f32[280,256]{1,0:T(8,128)}, f32[3,16,256]{2,1,0:T(8,128)}) custom-call(f32[64,16,256]{2,1,0:T(8,128)} %refs_0_.4, f32[16,256]{1,0:T(8,128)} %refs_1_.2, f32[16,256]{1,0:T(8,128)} %refs_2_.2, s32[16,256]{1,0:T(8,128)} %refs_3_.1), custom_call_target="tpu_custom_call" | custom-call | flops 1 | bytes 1097728 | tf_op jit(solution)/shard_map/pallas_call | solution.py:159
  3.1 0.6 collective-permute-start
  3.6 0.7 %collective-permute-start.1 = (f32[280,256]{1,0:T(8,128)}, f32[280,256]{1,0:T(8,128)S(1)}, u32[]{:S(2)}, u32[]{:S(2)}) collective-permute-start(f32[280,256]{1,0:T(8,128)} %get-tuple-element.30), channel_id=1, source_target_pairs={{1,2},{2,1},{3,4},{4,3},{5,6},{6,5},{9,10},{10,9},{11,12},{12,11},... | collective-permute-start | bytes 860168 | tf_op jit(solution)/shard_map/ppermute | solution.py:30
  4.4 1.2 %copy-done = f32[64,16,256]{2,1,0:T(8,128)S(1)} copy-done((f32[64,16,256]{2,1,0:T(8,128)S(1)}, f32[64,16,256]{2,1,0:T(8,128)}, u32[]{:S(2)}) %copy-start) | copy-done | bytes 1048600
  5.6 1.4 %copy-done.1 = bf16[3,64,16,256]{3,2,1,0:T(8,128)(2,1)S(1)} copy-done((bf16[3,64,16,256]{3,2,1,0:T(8,128)(2,1)S(1)}, bf16[3,64,16,256]{3,2,1,0:T(8,128)(2,1)}, u32[]{:S(2)}) %copy-start.1) | copy-done | bytes 1572888
  7.0 0.8 %copy-done.4 = f32[3,16,256]{2,1,0:T(8,128)S(1)} copy-done((f32[3,16,256]{2,1,0:T(8,128)S(1)}, f32[3,16,256]{2,1,0:T(8,128)}, u32[]{:S(2)}) %copy-start.4) | copy-done | bytes 49176
  7.8 1.5 %shard_map.95 = (f32[64,16,256]{2,1,0:T(8,128)S(1)}, f32[3,16,256]{2,1,0:T(8,128)S(1)}, f32[3,64,16,256]{3,2,1,0:T(8,128)S(1)}) custom-call(f32[64,16,256]{2,1,0:T(8,128)S(1)} %copy-done, f32[3,16,256]{2,1,0:T(8,128)S(1)} %copy-done.4, bf16[3,64,16,256]{3,2,1,0:T(8,128)(2,1)S(1)} %copy-done.1, bf16[256,256]{1,0:T(8,128)(2,1)S(1)} %get-tuple-element.52.refs_3_.refs_2_), custom_call_target="tpu_custom_call" | custom-call | flops 2000000000 | bytes 2801664 | tf_op jit(solution)/shard_map/pallas_call | solution.py:159
  9.4 3.2 %shard_map.96 = (f32[48,256]{1,0:T(8,128)S(1)}, f32[4,2,3,8,128]{4,3,2,1,0:T(8,128)S(1)}, f32[64,8,256]{2,1,0:T(8,128)S(1)}) custom-call(f32[64,16,256]{2,1,0:T(8,128)S(1)} %get-tuple-element.28.refs_0_, f32[280,256]{1,0:T(8,128)S(1)} %collective-permute-done.refs_1_, f32[280,256]{1,0:T(8,128)S(1)} %collective-permute-done.1.refs_2_, ...), custom_call_target="tpu_custom_call" | custom-call | flops 4000000000 | bytes 4816896 | tf_op jit(solution)/shard_map/pallas_call | solution.py:159
  12.6 3.5 %collective-permute-start.4 = (f32[48,256]{1,0:T(8,128)S(1)}, f32[48,256]{1,0:T(8,128)S(1)}, u32[]{:S(2)}, u32[]{:S(2)}) collective-permute-start(f32[48,256]{1,0:T(8,128)S(1)} %get-tuple-element.34.refs_0_), channel_id=1, source_target_pairs={{0,24},{8,16},{16,8},{24,0},{1,25},{9,17},{17,9},{25,1},{2,26},{10... | collective-permute-start | bytes 147464 | tf_op jit(solution)/shard_map/ppermute | solution.py:39
  16.1 0.5 collective-permute-start.3
  17.0 1.2 %collective-permute-done.4.refs_3_ = f32[48,256]{1,0:T(8,128)S(1)} collective-permute-done((f32[48,256]{1,0:T(8,128)S(1)}, f32[48,256]{1,0:T(8,128)S(1)}, u32[]{:S(2)}, u32[]{:S(2)}) %collective-permute-start.4) | collective-permute-done | bytes 49184 | tf_op jit(solution)/shard_map/ppermute | solution.py:39
  18.2 2.5 %collective-permute-done.3.refs_2_ = f32[48,256]{1,0:T(8,128)S(1)} collective-permute-done((f32[48,256]{1,0:T(8,128)S(1)}, f32[48,256]{1,0:T(8,128)S(1)}, u32[]{:S(2)}, u32[]{:S(2)}) %collective-permute-start.3) | collective-permute-done | bytes 49184 | tf_op jit(solution)/shard_map/ppermute | solution.py:39
  21.2 3.1 %shard_map.98 = (f32[64,8,256]{2,1,0:T(8,128)S(1)}, f32[64,8,256]{2,1,0:T(8,128)S(1)}, f32[64,16,256]{2,1,0:T(8,128)S(1)}, f32[64,8,256]{2,1,0:T(8,128)S(1)}) custom-call(f32[48,256]{1,0:T(8,128)S(1)} %get-tuple-element.34.refs_0_, f32[48,256]{1,0:T(8,128)S(1)} %collective-permute-done.2.refs_1_, f32[48,256]{1,0:T(8,128)S(1)} %collective-permute-done.3.refs_2_, ...), custom_call_target="tpu_custom_call" | custom-call | flops 1 | bytes 3538944 | tf_op jit(solution)/shard_map/pallas_call | solution.py:159
  24.3 0.8 %collective-permute-start.5 = (f32[64,8,256]{2,1,0:T(8,128)S(1)}, f32[64,8,256]{2,1,0:T(8,128)S(1)}, u32[]{:S(2)}, u32[]{:S(2)}) collective-permute-start(f32[64,8,256]{2,1,0:T(8,128)S(1)} %get-tuple-element.40), channel_id=1, source_target_pairs={{0,1},{1,0},{2,3},{3,2},{4,5},{5,4},{6,7},{7,6},{8,9},{9,8},{10,11... | collective-permute-start | bytes 1572872 | tf_op jit(solution)/shard_map/ppermute | solution.py:31
  25.1 0.7 %collective-permute-start.6 = (f32[64,8,256]{2,1,0:T(8,128)S(1)}, f32[64,8,256]{2,1,0:T(8,128)S(1)}, u32[]{:S(2)}, u32[]{:S(2)}) collective-permute-start(f32[64,8,256]{2,1,0:T(8,128)S(1)} %get-tuple-element.41), channel_id=1, source_target_pairs={{1,2},{2,1},{3,4},{4,3},{5,6},{6,5},{9,10},{10,9},{11,12},{12,11},... | collective-permute-start | bytes 1572872 | tf_op jit(solution)/shard_map/ppermute | solution.py:30
  25.8 0.8 %collective-permute-done.5.refs_4_ = f32[64,8,256]{2,1,0:T(8,128)S(1)} collective-permute-done((f32[64,8,256]{2,1,0:T(8,128)S(1)}, f32[64,8,256]{2,1,0:T(8,128)S(1)}, u32[]{:S(2)}, u32[]{:S(2)}) %collective-permute-start.5) | collective-permute-done | bytes 524320 | tf_op jit(solution)/shard_map/ppermute | solution.py:31
  26.6 3.2 %shard_map.99 = (f32[64,16,256]{2,1,0:T(8,128)S(1)}, f32[56,256]{1,0:T(8,128)S(1)}) custom-call(f32[64,16,256]{2,1,0:T(8,128)S(1)} %get-tuple-element.28.refs_0_, f32[64,8,256]{2,1,0:T(8,128)S(1)} %get-tuple-element.33.refs_1_, f32[64,16,256]{2,1,0:T(8,128)S(1)} %get-tuple-element.38.refs_2_, f32[64,8,256]{2,1,0:T(8,128)S(1)} %get-tuple-element.39.refs_3_, ...), custom_call_target="tpu_custom_call" | custom-call | flops 4000000000 | bytes 7438336 | tf_op jit(solution)/shard_map/pallas_call | solution.py:159
  29.8 1.6 %collective-permute-start.9 = (f32[56,256]{1,0:T(8,128)S(1)}, f32[56,256]{1,0:T(8,128)S(1)}, u32[]{:S(2)}, u32[]{:S(2)}) collective-permute-start(f32[56,256]{1,0:T(8,128)S(1)} %get-tuple-element.44.refs_0_), channel_id=1, source_target_pairs={{0,24},{8,16},{16,8},{24,0},{1,25},{9,17},{17,9},{25,1},{2,26},{10... | collective-permute-start | bytes 172040 | tf_op jit(solution)/shard_map/ppermute | solution.py:39
  31.4 0.6 collective-permute-start.8
  32.0 1.4 %collective-permute-start.7 = (f32[56,256]{1,0:T(8,128)S(1)}, f32[56,256]{1,0:T(8,128)S(1)}, u32[]{:S(2)}, u32[]{:S(2)}) collective-permute-start(f32[56,256]{1,0:T(8,128)S(1)} %get-tuple-element.44.refs_0_), channel_id=1, source_target_pairs={{0,8},{8,0},{16,24},{24,16},{1,9},{9,1},{17,25},{25,17},{2,10},{10... | collective-permute-start | bytes 172040 | tf_op jit(solution)/shard_map/ppermute | solution.py:39
  33.4 1.4 %shard_map.100 = (f32[64,16,256]{2,1,0:T(8,128)}, f32[8,128]{1,0:T(8,128)S(1)}) custom-call(f32[64,16,256]{2,1,0:T(8,128)S(1)} %get-tuple-element.42.refs_0_.refs_8_, bf16[256,256]{1,0:T(8,128)(2,1)S(1)} %get-tuple-element.51.refs_1_.refs_3_), custom_call_target="tpu_custom_call" | custom-call | flops 1000000000 | bytes 1179648 | tf_op jit(solution)/shard_map/pallas_call | solution.py:159
  35.0 0.6 %collective-permute-done.8.refs_2_ = f32[56,256]{1,0:T(8,128)S(1)} collective-permute-done((f32[56,256]{1,0:T(8,128)S(1)}, f32[56,256]{1,0:T(8,128)S(1)}, u32[]{:S(2)}, u32[]{:S(2)}) %collective-permute-start.8) | collective-permute-done | bytes 57376 | tf_op jit(solution)/shard_map/ppermute | solution.py:39
  35.6 0.6 collective-permute-done.7.refs_1_
  36.2 3.1 %shard_map.101 = (f32[64,16,256]{2,1,0:T(8,128)S(1)}, f32[272,256]{1,0:T(8,128)S(1)}, f32[256,256]{1,0:T(8,128)S(1)}) custom-call(f32[56,256]{1,0:T(8,128)S(1)} %get-tuple-element.44.refs_0_, f32[56,256]{1,0:T(8,128)S(1)} %collective-permute-done.7.refs_1_, f32[56,256]{1,0:T(8,128)S(1)} %collective-permute-done.8.refs_2_, ...), custom_call_target="tpu_custom_call" | custom-call | flops 1 | bytes 4575232 | tf_op jit(solution)/shard_map/pallas_call | solution.py:159
  39.3 8.8 %collective-permute-start.10 = (f32[272,256]{1,0:T(8,128)S(1)}, f32[272,256]{1,0:T(8,128)S(1)}, u32[]{:S(2)}, u32[]{:S(2)}) collective-permute-start(f32[272,256]{1,0:T(8,128)S(1)} %get-tuple-element.47), channel_id=1, source_target_pairs={{0,1},{1,0},{2,3},{3,2},{4,5},{5,4},{6,7},{7,6},{8,9},{9,8},{10,11... | collective-permute-start | bytes 835592 | tf_op jit(solution)/shard_map/ppermute | solution.py:31
  48.0 0.7 %collective-permute-start.11 = (f32[256,256]{1,0:T(8,128)S(1)}, f32[256,256]{1,0:T(8,128)S(1)}, u32[]{:S(2)}, u32[]{:S(2)}) collective-permute-start(f32[256,256]{1,0:T(8,128)S(1)} %get-tuple-element.48), channel_id=1, source_target_pairs={{1,2},{2,1},{3,4},{4,3},{5,6},{6,5},{9,10},{10,9},{11,12},{12,11},... | collective-permute-start | bytes 786440 | tf_op jit(solution)/shard_map/ppermute | solution.py:30
  48.7 0.5 collective-permute-done.10.refs_1_
  49.2 6.6 %collective-permute-start.14 = (f32[16,128]{1,0:T(8,128)S(1)}, f32[16,128]{1,0:T(8,128)S(1)}, u32[]{:S(2)}, u32[]{:S(2)}) collective-permute-start(f32[16,128]{1,0:T(8,128)S(1)} %slice_add_fusion.refs_0_), channel_id=1, source_target_pairs={{0,6},{1,7},{2,4},{3,5},{4,2},{5,3},{6,0},{7,1},{8,14},{9,15},{10,... | collective-permute-start | bytes 24584 | tf_op jit(solution)/shard_map/ppermute | solution.py:39
  55.9 0.6 %collective-permute-start.12 = (f32[16,128]{1,0:T(8,128)S(1)}, f32[16,128]{1,0:T(8,128)S(1)}, u32[]{:S(2)}, u32[]{:S(2)}) collective-permute-start(f32[16,128]{1,0:T(8,128)S(1)} %slice_add_fusion.refs_0_), channel_id=1, source_target_pairs={{0,2},{1,3},{2,0},{3,1},{4,6},{5,7},{6,4},{7,5},{8,10},{9,11},{10,... | collective-permute-start | bytes 24584 | tf_op jit(solution)/shard_map/ppermute | solution.py:39
  56.5 1.5 %shard_map.102 = (f32[64,16,256]{2,1,0:T(8,128)}, f32[8,128]{1,0:T(8,128)S(1)}) custom-call(f32[64,16,256]{2,1,0:T(8,128)S(1)} %get-tuple-element.46.refs_0_, f32[272,256]{1,0:T(8,128)S(1)} %collective-permute-done.10.refs_1_, f32[256,256]{1,0:T(8,128)S(1)} %collective-permute-done.11.refs_2_, bf16[256,256]{1,0:T(8,128)(2,1)S(1)} %get-tuple-element.51.refs_1_.refs_3_), custom_call_target="tpu_custom_call" | custom-call | flops 1000000000 | bytes 1720320 | tf_op jit(solution)/shard_map/pallas_call | solution.py:159
  57.9 2.5 %collective-permute-done.14.refs_3_ = f32[16,128]{1,0:T(8,128)S(1)} collective-permute-done((f32[16,128]{1,0:T(8,128)S(1)}, f32[16,128]{1,0:T(8,128)S(1)}, u32[]{:S(2)}, u32[]{:S(2)}) %collective-permute-start.14) | collective-permute-done | bytes 8224 | tf_op jit(solution)/shard_map/ppermute | solution.py:39
  60.5 0.6 shard_map.103
  (21 shorter events, 1.1 us)
Async XLA Ops:
  3.1 6.3 %collective-permute-start = (f32[280,256]{1,0:T(8,128)}, f32[280,256]{1,0:T(8,128)S(1)}, u32[]{:S(2)}, u32[]{:S(2)}) collective-permute-start(f32[280,256]{1,0:T(8,128)} %get-tuple-element.29), channel_id=1, source_target_pairs={{0,1},{1,0},{2,3},{3,2},{4,5},{5,4},{6,7},{7,6},{8,9},{9,8},{10,11... | collective-permute-start | bytes 860168 | tf_op jit(solution)/shard_map/ppermute | solution.py:31
  3.6 5.8 %collective-permute-start.1 = (f32[280,256]{1,0:T(8,128)}, f32[280,256]{1,0:T(8,128)S(1)}, u32[]{:S(2)}, u32[]{:S(2)}) collective-permute-start(f32[280,256]{1,0:T(8,128)} %get-tuple-element.30), channel_id=1, source_target_pairs={{1,2},{2,1},{3,4},{4,3},{5,6},{6,5},{9,10},{10,9},{11,12},{12,11},... | collective-permute-start | bytes 860168 | tf_op jit(solution)/shard_map/ppermute | solution.py:30
  4.4 1.2 %copy-start = (f32[64,16,256]{2,1,0:T(8,128)S(1)}, f32[64,16,256]{2,1,0:T(8,128)}, u32[]{:S(2)}) copy-start(f32[64,16,256]{2,1,0:T(8,128)} %refs_0_.4) | copy-start | bytes 3145732
  5.6 1.4 %copy-start.1 = (bf16[3,64,16,256]{3,2,1,0:T(8,128)(2,1)S(1)}, bf16[3,64,16,256]{3,2,1,0:T(8,128)(2,1)}, u32[]{:S(2)}) copy-start(bf16[3,64,16,256]{3,2,1,0:T(8,128)(2,1)} %refs_2_.3) | copy-start | bytes 4718596
  7.0 0.8 %copy-start.4 = (f32[3,16,256]{2,1,0:T(8,128)S(1)}, f32[3,16,256]{2,1,0:T(8,128)}, u32[]{:S(2)}) copy-start(f32[3,16,256]{2,1,0:T(8,128)} %get-tuple-element.27.refs_1_) | copy-start | bytes 147460
  9.4 7.4 %copy-start.2 = (f32[3,16,256]{2,1,0:T(8,128)S(1)}, f32[3,16,256]{2,1,0:T(8,128)}, u32[]{:S(2)}) copy-start(f32[3,16,256]{2,1,0:T(8,128)} %refs_0_.5) | copy-start | bytes 147460
  9.4 7.4 %copy-start.3 = (f32[3,16,256]{2,1,0:T(8,128)S(1)}, f32[3,16,256]{2,1,0:T(8,128)}, u32[]{:S(2)}) copy-start(f32[3,16,256]{2,1,0:T(8,128)} %refs_1_.3) | copy-start | bytes 147460
  12.6 5.6 %collective-permute-start.4 = (f32[48,256]{1,0:T(8,128)S(1)}, f32[48,256]{1,0:T(8,128)S(1)}, u32[]{:S(2)}, u32[]{:S(2)}) collective-permute-start(f32[48,256]{1,0:T(8,128)S(1)} %get-tuple-element.34.refs_0_), channel_id=1, source_target_pairs={{0,24},{8,16},{16,8},{24,0},{1,25},{9,17},{17,9},{25,1},{2,26},{10... | collective-permute-start | bytes 147464 | tf_op jit(solution)/shard_map/ppermute | solution.py:39
  16.1 4.6 %collective-permute-start.3 = (f32[48,256]{1,0:T(8,128)S(1)}, f32[48,256]{1,0:T(8,128)S(1)}, u32[]{:S(2)}, u32[]{:S(2)}) collective-permute-start(f32[48,256]{1,0:T(8,128)S(1)} %get-tuple-element.34.refs_0_), channel_id=1, source_target_pairs={{0,16},{8,24},{16,0},{24,8},{1,17},{9,25},{17,1},{25,9},{2,18},{10... | collective-permute-start | bytes 147464 | tf_op jit(solution)/shard_map/ppermute | solution.py:39
  16.6 4.6 %collective-permute-start.2 = (f32[48,256]{1,0:T(8,128)S(1)}, f32[48,256]{1,0:T(8,128)S(1)}, u32[]{:S(2)}, u32[]{:S(2)}) collective-permute-start(f32[48,256]{1,0:T(8,128)S(1)} %get-tuple-element.34.refs_0_), channel_id=1, source_target_pairs={{0,8},{8,0},{16,24},{24,16},{1,9},{9,1},{17,25},{25,17},{2,10},{10... | collective-permute-start | bytes 147464 | tf_op jit(solution)/shard_map/ppermute | solution.py:39
  24.3 2.3 %collective-permute-start.5 = (f32[64,8,256]{2,1,0:T(8,128)S(1)}, f32[64,8,256]{2,1,0:T(8,128)S(1)}, u32[]{:S(2)}, u32[]{:S(2)}) collective-permute-start(f32[64,8,256]{2,1,0:T(8,128)S(1)} %get-tuple-element.40), channel_id=1, source_target_pairs={{0,1},{1,0},{2,3},{3,2},{4,5},{5,4},{6,7},{7,6},{8,9},{9,8},{10,11... | collective-permute-start | bytes 1572872 | tf_op jit(solution)/shard_map/ppermute | solution.py:31
  25.1 1.5 %collective-permute-start.6 = (f32[64,8,256]{2,1,0:T(8,128)S(1)}, f32[64,8,256]{2,1,0:T(8,128)S(1)}, u32[]{:S(2)}, u32[]{:S(2)}) collective-permute-start(f32[64,8,256]{2,1,0:T(8,128)S(1)} %get-tuple-element.41), channel_id=1, source_target_pairs={{1,2},{2,1},{3,4},{4,3},{5,6},{6,5},{9,10},{10,9},{11,12},{12,11},... | collective-permute-start | bytes 1572872 | tf_op jit(solution)/shard_map/ppermute | solution.py:30
  29.8 5.1 %collective-permute-start.9 = (f32[56,256]{1,0:T(8,128)S(1)}, f32[56,256]{1,0:T(8,128)S(1)}, u32[]{:S(2)}, u32[]{:S(2)}) collective-permute-start(f32[56,256]{1,0:T(8,128)S(1)} %get-tuple-element.44.refs_0_), channel_id=1, source_target_pairs={{0,24},{8,16},{16,8},{24,0},{1,25},{9,17},{17,9},{25,1},{2,26},{10... | collective-permute-start | bytes 172040 | tf_op jit(solution)/shard_map/ppermute | solution.py:39
  31.4 4.2 %collective-permute-start.8 = (f32[56,256]{1,0:T(8,128)S(1)}, f32[56,256]{1,0:T(8,128)S(1)}, u32[]{:S(2)}, u32[]{:S(2)}) collective-permute-start(f32[56,256]{1,0:T(8,128)S(1)} %get-tuple-element.44.refs_0_), channel_id=1, source_target_pairs={{0,16},{8,24},{16,0},{24,8},{1,17},{9,25},{17,1},{25,9},{2,18},{10... | collective-permute-start | bytes 172040 | tf_op jit(solution)/shard_map/ppermute | solution.py:39
  32.0 4.2 %collective-permute-start.7 = (f32[56,256]{1,0:T(8,128)S(1)}, f32[56,256]{1,0:T(8,128)S(1)}, u32[]{:S(2)}, u32[]{:S(2)}) collective-permute-start(f32[56,256]{1,0:T(8,128)S(1)} %get-tuple-element.44.refs_0_), channel_id=1, source_target_pairs={{0,8},{8,0},{16,24},{24,16},{1,9},{9,1},{17,25},{25,17},{2,10},{10... | collective-permute-start | bytes 172040 | tf_op jit(solution)/shard_map/ppermute | solution.py:39
  39.3 9.9 %collective-permute-start.10 = (f32[272,256]{1,0:T(8,128)S(1)}, f32[272,256]{1,0:T(8,128)S(1)}, u32[]{:S(2)}, u32[]{:S(2)}) collective-permute-start(f32[272,256]{1,0:T(8,128)S(1)} %get-tuple-element.47), channel_id=1, source_target_pairs={{0,1},{1,0},{2,3},{3,2},{4,5},{5,4},{6,7},{7,6},{8,9},{9,8},{10,11... | collective-permute-start | bytes 835592 | tf_op jit(solution)/shard_map/ppermute | solution.py:31
  48.0 8.5 %collective-permute-start.11 = (f32[256,256]{1,0:T(8,128)S(1)}, f32[256,256]{1,0:T(8,128)S(1)}, u32[]{:S(2)}, u32[]{:S(2)}) collective-permute-start(f32[256,256]{1,0:T(8,128)S(1)} %get-tuple-element.48), channel_id=1, source_target_pairs={{1,2},{2,1},{3,4},{4,3},{5,6},{6,5},{9,10},{10,9},{11,12},{12,11},... | collective-permute-start | bytes 786440 | tf_op jit(solution)/shard_map/ppermute | solution.py:30
  49.2 11.3 %collective-permute-start.14 = (f32[16,128]{1,0:T(8,128)S(1)}, f32[16,128]{1,0:T(8,128)S(1)}, u32[]{:S(2)}, u32[]{:S(2)}) collective-permute-start(f32[16,128]{1,0:T(8,128)S(1)} %slice_add_fusion.refs_0_), channel_id=1, source_target_pairs={{0,6},{1,7},{2,4},{3,5},{4,2},{5,3},{6,0},{7,1},{8,14},{9,15},{10,... | collective-permute-start | bytes 24584 | tf_op jit(solution)/shard_map/ppermute | solution.py:39
  55.8 4.6 %collective-permute-start.13 = (f32[16,128]{1,0:T(8,128)S(1)}, f32[16,128]{1,0:T(8,128)S(1)}, u32[]{:S(2)}, u32[]{:S(2)}) collective-permute-start(f32[16,128]{1,0:T(8,128)S(1)} %slice_add_fusion.refs_0_), channel_id=1, source_target_pairs={{0,4},{1,5},{2,6},{3,7},{4,0},{5,1},{6,2},{7,3},{8,12},{9,13},{10,... | collective-permute-start | bytes 24584 | tf_op jit(solution)/shard_map/ppermute | solution.py:39
  55.9 4.6 %collective-permute-start.12 = (f32[16,128]{1,0:T(8,128)S(1)}, f32[16,128]{1,0:T(8,128)S(1)}, u32[]{:S(2)}, u32[]{:S(2)}) collective-permute-start(f32[16,128]{1,0:T(8,128)S(1)} %slice_add_fusion.refs_0_), channel_id=1, source_target_pairs={{0,2},{1,3},{2,0},{3,1},{4,6},{5,7},{6,4},{7,5},{8,10},{9,11},{10,... | collective-permute-start | bytes 24584 | tf_op jit(solution)/shard_map/ppermute | solution.py:39

commit v4 on v3

--- a/solution.py
+++ b/solution.py
@@ -1,3 +1,4 @@
+import functools
 import jax
 import jax.numpy as jnp
 from jax import lax
@@ -9,6 +10,7 @@
 SUB = 8
 CHUNKS = 4
 UNROLL = 7
+PIECES = 2
 VMEM_BYTES = 67043328
 SPARE = 3072
 LANES = 128
@@ -39,7 +41,7 @@
         lax.ppermute(
             value, axis, [(i, i ^ step if power else (i + step) % count) for i in range(count)]
         )
-        for step in range(stride, count, stride)
+        for step in reversed(range(stride, count, stride))
     ]
 
 
@@ -257,22 +259,25 @@
         out[...] = reordered(jnp.concatenate([block] * PACK, 1), turn).reshape(out.shape)
 
 
-def restore_packs(first, count, field, turn, out):
+def restore_packs(first, count, field, turn, out, offset=0):
     rows, width = out.shape[1:]
     block = field[pl.ds(first, count)].reshape(count * rows, PACK * width)
     block = reordered(block, turn)
     for k in range(count):
         for b in range(PACK):
-            out[(first + k) * PACK + b] = block[
+            out[(offset + first + k) * PACK + b] = block[
                 k * rows : (k + 1) * rows, b * width : (b + 1) * width
             ]
 
 
-def restore_kernel(packs, field, matrix, out, token):
+def restore_kernel(packs, matrix, *refs):
+    fields, (out, token) = refs[:-2], refs[-2:]
     turn = matrix[...]
     token[...] = jnp.zeros_like(token)
-    for step in range(packs // GROUP):
-        restore_packs(step * GROUP, GROUP, field, turn, out)
+    part = packs // len(fields)
+    for k, field in enumerate(fields):
+        for step in range(part // GROUP):
+            restore_packs(step * GROUP, GROUP, field, turn, out, k * part)
 
 
 def coefficients_into(fields, halo_low, halo_high, base, out, ring, dims):
@@ -403,18 +408,18 @@
     return out
 
 
-def pulled_sweeps(step, weights, pert, ring, coef3, lane, dims):
+def pulled_sweeps(start, weights, pert, ring, coef3, lane, dims):
     cols, own = dims
     for g in range(GROUP):
         for c in range(cols):
-            tiles = pull_member(pert, step * GROUP + g, weights, c, own)
+            tiles = pull_member(pert, start + g, weights, c, own)
             for i in range(own):
                 ring[g, c, pl.ds(i * SUB, SUB), :] = tiles[i]
             ring[g, c, pl.ds(own * SUB, SUB), :] = jnp.zeros((SUB, LANES), jnp.float32)
         sweeps(adjoint, ring, g, coef3, lane, cols, own + 1)
 
 
-def second_kernel(dims, times, members, count, *refs):
+def second_kernel(dims, times, members, offset, count, *refs):
     cols, own = dims
     parts, (innovation, weight, pert, coef3, near, far, field, spill, ring) = (
         refs[:count],
@@ -433,7 +438,7 @@
                 )
 
     def group(step, carry):
-        pulled_sweeps(step, weights, pert, ring, coef3, lane, dims)
+        pulled_sweeps(offset + step * GROUP, weights, pert, ring, coef3, lane, dims)
         for g in range(GROUP):
             m = step * GROUP + g
             for c in range(cols):
@@ -451,8 +456,9 @@
     lax.fori_loop(0, members // GROUP, group, 0)
 
 
-def third_kernel(dims, times, members, control, halo, field, spill, from_near, from_far, coef3,
-                 pert, gradient, sums, ring):
+def third_kernel(dims, times, members, offset, control, halo, field, spill, from_near, from_far,
+                 coef3, pert, *refs):
+    gradient, sums, ring = refs[-3:]
     cols, own = dims
     lane, sub, odd = lane_of(), sub_of(), is_odd()
     index = lax.axis_index("tile")
@@ -472,7 +478,7 @@
                 high, low = jnp.where(odd, b, a), jnp.where(odd, a, b)
                 for i in range(own):
                     rows = pl.ds(i * SUB, SUB)
-                    value = control[m, rows, cs] + field[m, rows, cs]
+                    value = control[offset + m, rows, cs] + field[m, rows, cs]
                     if i == 0:
                         value = value + jnp.where(sub < SWEEPS, low, 0.0)
                     if i == own - 1:
@@ -481,10 +487,10 @@
                     ring[g, c, rows, :] = value
                     square = square + value * value
                 edge = jnp.where(sub < SWEEPS, high, low) + spill[m, :, cs]
-                ring[g, c, pl.ds(own * SUB, SUB), :] = inside * (halo[m, :, cs] + edge)
+                ring[g, c, pl.ds(own * SUB, SUB), :] = inside * (halo[offset + m, :, cs] + edge)
         for g in range(GROUP):
             sweeps(forward, ring, g, coef3, lane, cols, own + 1)
-            total = project_member(pert, step * GROUP + g, ring, g, total, dims)
+            total = project_member(pert, offset + step * GROUP + g, ring, g, total, dims)
         return total, square
 
     total, square = lax.fori_loop(
@@ -496,11 +502,18 @@
     write_sums(sums, total, dims, lane)
     sums[pl.ds(times * own * SUB, SUB), :] = jnp.zeros((SUB, sums.shape[1]), jnp.float32)
     sums[pl.ds(times * own * SUB, SUB), columns(0)] = square
+    for before in refs[:-3]:
+        sums[...] = sums[...] + before[...]
+
+
+def tie_kernel(value, _, out):
+    out[...] = value[...]
 
 
 def fourth_kernel(dims, times, members, count, *refs):
     cols, own = dims
-    parts, (weight, pert, _, coef3, gradient, field, near, far, ring) = refs[:count], refs[count:]
+    parts, (weight, pert, _, coef3, *refs) = refs[:count], refs[count:]
+    gradients, (field, near, far, ring) = refs[:-4], refs[-4:]
     odd, sub, lane = is_odd(), sub_of(), lane_of()
     weights = []
     curve = jnp.zeros((SUB, LANES), jnp.float32)
@@ -517,10 +530,11 @@
     near[pl.ds(base, SUB), columns(0)] = square
     near[pl.ds(base + SUB, SUB), columns(0)] = curve * (1.0 / PACK)
 
-    def group(step, carry):
-        pulled_sweeps(step, weights, pert, ring, coef3, lane, dims)
+    def group(offset, gradient, step, carry):
+        pulled_sweeps(offset + step * GROUP, weights, pert, ring, coef3, lane, dims)
         for pair in range(GROUP // 2):
-            first = step * GROUP + 2 * pair
+            here = step * GROUP + 2 * pair
+            first = offset + here
             start = pl.multiple_of(first * SWEEPS, SUB)
             for c in range(cols):
                 cs = columns(c)
@@ -528,7 +542,7 @@
                     for i in range(own):
                         rows = pl.ds(i * SUB, SUB)
                         field[first + k, rows, cs] = (
-                            gradient[first + k, rows, cs] + ring[2 * pair + k, c, rows, :]
+                            gradient[here + k, rows, cs] + ring[2 * pair + k, c, rows, :]
                         )
                 x, y = (ring[2 * pair + k, c, pl.ds(own * SUB, SUB), :] for k in range(2))
                 high = jnp.where(sub < SWEEPS, x, pltpu.roll(y, SWEEPS, 0))
@@ -537,7 +551,9 @@
                 far[pl.ds(start, SUB), cs] = jnp.where(odd, high, low)
         return carry
 
-    lax.fori_loop(0, members // GROUP, group, 0)
+    part = members // len(gradients)
+    for k, gradient in enumerate(gradients):
+        lax.fori_loop(0, part // GROUP, functools.partial(group, k * part, gradient), 0)
 
 
 def fifth_kernel(dims, members, field, near, far, matrix, product, token, whole):
@@ -646,34 +662,44 @@
         flops=4_000_000_000,
     )
     parts = [sums] + others(sums, "mem")
-    edges = f32(packs, SUB, wide)
-    near, far, field, spill = call(
-        bind(second_kernel, dims, times, packs, len(parts)),
-        [edges, edges, packed, edges],
-        [ring_of(own + 1)],
-        parts + [innovation, obs_weight, perturbations, coef3],
-    )
-    from_near, from_far = swap(near, far)
-    gradient, sums = call(
-        bind(third_kernel, dims, times, packs),
-        [packed, f32(times * rows + SUB, width)],
-        [ring_of(own + 1)],
-        [control, halo, field, spill, from_near, from_far, coef3, perturbations],
-        flops=4_000_000_000,
-    )
+    half = packs // PIECES
+    pieces = []
+    for k in range(PIECES):
+        edges, some = f32(half, SUB, wide), f32(half, rows, wide)
+        near, far, field, spill = call(
+            bind(second_kernel, dims, times, half, k * half, len(parts)),
+            [edges, edges, some, edges],
+            [ring_of(own + 1)],
+            parts + [innovation, obs_weight, perturbations, coef3],
+            flops=2_000_000_000,
+        )
+        if k:
+            (near,) = call(tie_kernel, [edges], [], [near, pieces[-1][3]])
+        pieces.append([field, spill] + list(swap(near, far)))
+    gradients, before = [], []
+    for k in range(PIECES):
+        gradient, sums = call(
+            bind(third_kernel, dims, times, half, k * half),
+            [some, f32(times * rows + SUB, width)],
+            [ring_of(own + 1)],
+            [control, halo] + pieces[k] + [coef3, perturbations] + before,
+            flops=2_000_000_000,
+        )
+        gradients.append(gradient)
+        before = [sums]
     parts = [sums] + others(sums, "mem")
     restored, token = call(
         bind(restore_kernel, packs),
         [gradient_shape, f32(SUB, LANES)],
         [],
-        [gradient, back],
+        [back] + gradients,
         flops=1_000_000_000,
     )
     field, near, far = call(
         bind(fourth_kernel, dims, times, packs, len(parts)),
         [packed, f32(packs * SWEEPS + 2 * SUB, wide), f32(packs * SWEEPS, wide)],
         [ring_of(own + 1)],
-        parts + [obs_weight, perturbations, token, coef3, gradient],
+        parts + [obs_weight, perturbations, token, coef3] + gradients,
     )
     from_near, from_far = swap(near, far)
     one = near[packs * SWEEPS :, :LANES] + from_near[packs * SWEEPS :, :LANES]
@@ -681,7 +707,7 @@
     product, token = call(
         bind(fifth_kernel, dims, packs),
         [gradient_shape, f32(SUB, LANES)],
-        [pltpu.VMEM(gradient.shape, jnp.float32)],
+        [pltpu.VMEM(packed.shape, jnp.float32)],
         [field, from_near, from_far, back],
         flops=1_000_000_000,
     )

time: 61.4 us -> 59.9 us (0.976)
    ppermute x3 -> x4, starting transfers between devices: 10.1 us -> 9.24 us  [swap(): near = lax.ppermute(inner, 'tile', pairs_inner(count))]
    ppermute x3 -> x4, waiting for transfers between devices: 1.36 us -> 0.52 us  [swap(): near = lax.ppermute(inner, 'tile', pairs_inner(count))]
    ppermute x3 -> x4, starting transfers between devices: 2.01 us -> 2.69 us  [swap(): far = lax.ppermute(outer, 'tile', pairs_outer(count))]
    pallas_call x10 -> x13, Pallas kernels: 20.2 us -> 19.7 us  [call(): pl.pallas_call(kernel, out_shape=outs, in_specs=[pl.BlockSpec(memory_spac...]
  transfers between devices with their start and end apart: 15 -> 17, of which waited for: 9 -> 8; matrix products, arithmetic and copies ran while one was open for 0% -> 0% of each run, Pallas kernels for 7% -> 13%
where the time goes in v4:
time: 59.9 us; the launch traced here: 59.6 us
  starting transfers between devices  26.5 us (44%)
  Pallas kernels  19.7 us (33%)
  waiting for transfers between devices  9.01 us (15%)
  local copies, waits for them, and re-layouts  3.44 us (6%)
  between operations  0.82 us (1%)
    pallas_call x13, Pallas kernels, call(): pl.pallas_call(kernel, out_shape=outs, in_specs=[pl.BlockSpec(memory_spac...  19.7 us
    ppermute x9, starting transfers between devices, others(): lax.ppermute(value, axis, [(i, i ^ step if power else (i + step) % count)...  14.6 us
    ppermute x4, starting transfers between devices, swap(): near = lax.ppermute(inner, 'tile', pairs_inner(count))  9.24 us
    ppermute x9, waiting for transfers between devices, others(): lax.ppermute(value, axis, [(i, i ^ step if power else (i + step) % count)...  8.48 us
    unnamed x10, local copies, waits for them, and re-layouts  3.44 us
    ppermute x4, starting transfers between devices, swap(): far = lax.ppermute(outer, 'tile', pairs_outer(count))  2.69 us
  transfers between devices with their start and end apart: 17, of which 8 were waited for; matrix products, arithmetic and copies ran while one was open for 0% of the time, Pallas kernels for 13%

profile of v4, /device:TPU:0, one launch (start us, length us, event | category | flops | bytes accessed | tf_op | source)
XLA Modules:
  0.0 59.6 jit_solution(12593212325636682562)
XLA Ops:
  0.6 2.4 %shard_map.94 = (f32[280,256]{1,0:T(8,128)}, f32[280,256]{1,0:T(8,128)}, f32[3,16,256]{2,1,0:T(8,128)}) custom-call(f32[64,16,256]{2,1,0:T(8,128)} %refs_0_.4, f32[16,256]{1,0:T(8,128)} %refs_1_.2, f32[16,256]{1,0:T(8,128)} %refs_2_.2, s32[16,256]{1,0:T(8,128)} %refs_3_.1), custom_call_target="tpu_custom_call" | custom-call | flops 1 | bytes 1097728 | tf_op jit(solution)/shard_map/pallas_call | solution.py:161
  3.6 0.7 %collective-permute-start.1 = (f32[280,256]{1,0:T(8,128)}, f32[280,256]{1,0:T(8,128)S(1)}, u32[]{:S(2)}, u32[]{:S(2)}) collective-permute-start(f32[280,256]{1,0:T(8,128)} %get-tuple-element.36), channel_id=1, source_target_pairs={{1,2},{2,1},{3,4},{4,3},{5,6},{6,5},{9,10},{10,9},{11,12},{12,11},... | collective-permute-start | bytes 860168 | tf_op jit(solution)/shard_map/ppermute | solution.py:32
  4.4 1.2 %copy-done = f32[64,16,256]{2,1,0:T(8,128)S(1)} copy-done((f32[64,16,256]{2,1,0:T(8,128)S(1)}, f32[64,16,256]{2,1,0:T(8,128)}, u32[]{:S(2)}) %copy-start) | copy-done | bytes 1048600
  5.6 1.4 %copy-done.1 = bf16[3,64,16,256]{3,2,1,0:T(8,128)(2,1)S(1)} copy-done((bf16[3,64,16,256]{3,2,1,0:T(8,128)(2,1)S(1)}, bf16[3,64,16,256]{3,2,1,0:T(8,128)(2,1)}, u32[]{:S(2)}) %copy-start.1) | copy-done | bytes 1572888
  7.0 0.8 %copy-done.4 = f32[3,16,256]{2,1,0:T(8,128)S(1)} copy-done((f32[3,16,256]{2,1,0:T(8,128)S(1)}, f32[3,16,256]{2,1,0:T(8,128)}, u32[]{:S(2)}) %copy-start.4) | copy-done | bytes 49176
  7.8 1.5 %shard_map.95 = (f32[64,16,256]{2,1,0:T(8,128)S(1)}, f32[3,16,256]{2,1,0:T(8,128)S(1)}, f32[3,64,16,256]{3,2,1,0:T(8,128)S(1)}) custom-call(f32[64,16,256]{2,1,0:T(8,128)S(1)} %copy-done, f32[3,16,256]{2,1,0:T(8,128)S(1)} %copy-done.4, bf16[3,64,16,256]{3,2,1,0:T(8,128)(2,1)S(1)} %copy-done.1, bf16[256,256]{1,0:T(8,128)(2,1)S(1)} %get-tuple-element.63.refs_3_.refs_2_), custom_call_target="tpu_custom_call" | custom-call | flops 2000000000 | bytes 2801664 | tf_op jit(solution)/shard_map/pallas_call | solution.py:161
  9.4 3.0 %shard_map.96 = (f32[48,256]{1,0:T(8,128)S(1)}, f32[4,2,3,8,128]{4,3,2,1,0:T(8,128)S(1)}, f32[64,8,256]{2,1,0:T(8,128)S(1)}) custom-call(f32[64,16,256]{2,1,0:T(8,128)S(1)} %get-tuple-element.34.refs_0_, f32[280,256]{1,0:T(8,128)S(1)} %collective-permute-done.refs_1_, f32[280,256]{1,0:T(8,128)S(1)} %collective-permute-done.1.refs_2_, ...), custom_call_target="tpu_custom_call" | custom-call | flops 4000000000 | bytes 4816896 | tf_op jit(solution)/shard_map/pallas_call | solution.py:161
  12.4 3.5 %collective-permute-start.2 = (f32[48,256]{1,0:T(8,128)S(1)}, f32[48,256]{1,0:T(8,128)S(1)}, u32[]{:S(2)}, u32[]{:S(2)}) collective-permute-start(f32[48,256]{1,0:T(8,128)S(1)} %get-tuple-element.40.refs_0_), channel_id=1, source_target_pairs={{0,24},{8,16},{16,8},{24,0},{1,25},{9,17},{17,9},{25,1},{2,26},{10... | collective-permute-start | bytes 147464 | tf_op jit(solution)/shard_map/ppermute | solution.py:41
  16.7 1.2 %collective-permute-done.2.refs_1_ = f32[48,256]{1,0:T(8,128)S(1)} collective-permute-done((f32[48,256]{1,0:T(8,128)S(1)}, f32[48,256]{1,0:T(8,128)S(1)}, u32[]{:S(2)}, u32[]{:S(2)}) %collective-permute-start.2) | collective-permute-done | bytes 49184 | tf_op jit(solution)/shard_map/ppermute | solution.py:41
  18.0 2.5 %collective-permute-done.3.refs_2_ = f32[48,256]{1,0:T(8,128)S(1)} collective-permute-done((f32[48,256]{1,0:T(8,128)S(1)}, f32[48,256]{1,0:T(8,128)S(1)}, u32[]{:S(2)}, u32[]{:S(2)}) %collective-permute-start.3) | collective-permute-done | bytes 49184 | tf_op jit(solution)/shard_map/ppermute | solution.py:41
  21.0 1.5 %shard_map.98 = (f32[32,8,256]{2,1,0:T(8,128)S(1)}, f32[32,8,256]{2,1,0:T(8,128)S(1)}, f32[32,16,256]{2,1,0:T(8,128)S(1)}, f32[32,8,256]{2,1,0:T(8,128)S(1)}) custom-call(f32[48,256]{1,0:T(8,128)S(1)} %get-tuple-element.40.refs_0_, f32[48,256]{1,0:T(8,128)S(1)} %collective-permute-done.2.refs_1_, f32[48,256]{1,0:T(8,128)S(1)} %collective-permute-done.3.refs_2_, ...), custom_call_target="tpu_custom_call" | custom-call | flops 2000000000 | bytes 3538944 | tf_op jit(solution)/shard_map/pallas_call | solution.py:161
  22.5 0.7 %collective-permute-start.6 = (f32[32,8,256]{2,1,0:T(8,128)S(1)}, f32[32,8,256]{2,1,0:T(8,128)S(1)}, u32[]{:S(2)}, u32[]{:S(2)}) collective-permute-start(f32[32,8,256]{2,1,0:T(8,128)S(1)} %get-tuple-element.47), channel_id=1, source_target_pairs={{1,2},{2,1},{3,4},{4,3},{5,6},{6,5},{9,10},{10,9},{11,12},{12,11},... | collective-permute-start | bytes 786440 | tf_op jit(solution)/shard_map/ppermute | solution.py:32
  23.2 4.9 %collective-permute-start.5 = (f32[32,8,256]{2,1,0:T(8,128)S(1)}, f32[32,8,256]{2,1,0:T(8,128)S(1)}, u32[]{:S(2)}, u32[]{:S(2)}) collective-permute-start(f32[32,8,256]{2,1,0:T(8,128)S(1)} %get-tuple-element.46), channel_id=1, source_target_pairs={{0,1},{1,0},{2,3},{3,2},{4,5},{5,4},{6,7},{7,6},{8,9},{9,8},{10,11... | collective-permute-start | bytes 786440 | tf_op jit(solution)/shard_map/ppermute | solution.py:33
  28.1 1.5 %shard_map.100 = (f32[32,8,256]{2,1,0:T(8,128)S(1)}, f32[32,8,256]{2,1,0:T(8,128)S(1)}, f32[32,16,256]{2,1,0:T(8,128)S(1)}, f32[32,8,256]{2,1,0:T(8,128)S(1)}) custom-call(f32[48,256]{1,0:T(8,128)S(1)} %get-tuple-element.40.refs_0_, f32[48,256]{1,0:T(8,128)S(1)} %collective-permute-done.2.refs_1_, f32[48,256]{1,0:T(8,128)S(1)} %collective-permute-done.3.refs_2_, ...), custom_call_target="tpu_custom_call" | custom-call | flops 2000000000 | bytes 3538944 | tf_op jit(solution)/shard_map/pallas_call | solution.py:161
  29.6 0.7 %collective-permute-start.8 = (f32[32,8,256]{2,1,0:T(8,128)S(1)}, f32[32,8,256]{2,1,0:T(8,128)S(1)}, u32[]{:S(2)}, u32[]{:S(2)}) collective-permute-start(f32[32,8,256]{2,1,0:T(8,128)S(1)} %get-tuple-element.52), channel_id=1, source_target_pairs={{1,2},{2,1},{3,4},{4,3},{5,6},{6,5},{9,10},{10,9},{11,12},{12,11},... | collective-permute-start | bytes 786440 | tf_op jit(solution)/shard_map/ppermute | solution.py:32
  30.3 3.0 %collective-permute-start.7 = (f32[32,8,256]{2,1,0:T(8,128)S(1)}, f32[32,8,256]{2,1,0:T(8,128)S(1)}, u32[]{:S(2)}, u32[]{:S(2)}) collective-permute-start(f32[32,8,256]{2,1,0:T(8,128)S(1)} %shard_map.101), channel_id=1, source_target_pairs={{0,1},{1,0},{2,3},{3,2},{4,5},{5,4},{6,7},{7,6},{8,9},{9,8},{10,11... | collective-permute-start | bytes 786440 | tf_op jit(solution)/shard_map/ppermute | solution.py:33
  33.3 1.5 %shard_map.99 = (f32[32,16,256]{2,1,0:T(8,128)S(1)}, f32[56,256]{1,0:T(8,128)S(1)}) custom-call(f32[64,16,256]{2,1,0:T(8,128)S(1)} %get-tuple-element.34.refs_0_, f32[64,8,256]{2,1,0:T(8,128)S(1)} %get-tuple-element.39.refs_1_, f32[32,16,256]{2,1,0:T(8,128)S(1)} %get-tuple-element.44.refs_2_, f32[32,8,256]{2,1,0:T(8,128)S(1)} %get-tuple-element.45.refs_3_, ...), custom_call_target="tpu_custom_call" | custom-call | flops 2000000000 | bytes 6127616 | tf_op jit(solution)/shard_map/pallas_call | solution.py:161
  34.8 1.5 %shard_map.102 = (f32[32,16,256]{2,1,0:T(8,128)S(1)}, f32[56,256]{1,0:T(8,128)S(1)}) custom-call(f32[64,16,256]{2,1,0:T(8,128)S(1)} %get-tuple-element.34.refs_0_, f32[64,8,256]{2,1,0:T(8,128)S(1)} %get-tuple-element.39.refs_1_, f32[32,16,256]{2,1,0:T(8,128)S(1)} %get-tuple-element.49.refs_2_, f32[32,8,256]{2,1,0:T(8,128)S(1)} %get-tuple-element.50.refs_3_, ...), custom_call_target="tpu_custom_call" | custom-call | flops 2000000000 | bytes 6184960 | tf_op jit(solution)/shard_map/pallas_call | solution.py:161
  36.4 1.6 %collective-permute-start.9 = (f32[56,256]{1,0:T(8,128)S(1)}, f32[56,256]{1,0:T(8,128)S(1)}, u32[]{:S(2)}, u32[]{:S(2)}) collective-permute-start(f32[56,256]{1,0:T(8,128)S(1)} %get-tuple-element.56.refs_0_), channel_id=1, source_target_pairs={{0,24},{8,16},{16,8},{24,0},{1,25},{9,17},{17,9},{25,1},{2,26},{10... | collective-permute-start | bytes 172040 | tf_op jit(solution)/shard_map/ppermute | solution.py:41
  37.9 0.6 %collective-permute-start.10 = (f32[56,256]{1,0:T(8,128)S(1)}, f32[56,256]{1,0:T(8,128)S(1)}, u32[]{:S(2)}, u32[]{:S(2)}) collective-permute-start(f32[56,256]{1,0:T(8,128)S(1)} %get-tuple-element.56.refs_0_), channel_id=1, source_target_pairs={{0,16},{8,24},{16,0},{24,8},{1,17},{9,25},{17,1},{25,9},{2,18},{10... | collective-permute-start | bytes 172040 | tf_op jit(solution)/shard_map/ppermute | solution.py:41
  38.5 1.4 %collective-permute-start.11 = (f32[56,256]{1,0:T(8,128)S(1)}, f32[56,256]{1,0:T(8,128)S(1)}, u32[]{:S(2)}, u32[]{:S(2)}) collective-permute-start(f32[56,256]{1,0:T(8,128)S(1)} %get-tuple-element.56.refs_0_), channel_id=1, source_target_pairs={{0,8},{8,0},{16,24},{24,16},{1,9},{9,1},{17,25},{25,17},{2,10},{10... | collective-permute-start | bytes 172040 | tf_op jit(solution)/shard_map/ppermute | solution.py:41
  39.9 1.4 %shard_map.103 = (f32[64,16,256]{2,1,0:T(8,128)}, f32[8,128]{1,0:T(8,128)S(1)}) custom-call(bf16[256,256]{1,0:T(8,128)(2,1)S(1)} %get-tuple-element.64.refs_0_.refs_3_, f32[32,16,256]{2,1,0:T(8,128)S(1)} %get-tuple-element.48.refs_1_.refs_8_, f32[32,16,256]{2,1,0:T(8,128)S(1)} %get-tuple-element.54.refs_2_.refs_9_), custom_call_target="tpu_custom_call" | custom-call | flops 1000000000 | bytes 1179648 | tf_op jit(solution)/shard_map/pallas_call | solution.py:161
  41.5 0.6 %collective-permute-done.10.refs_2_ = f32[56,256]{1,0:T(8,128)S(1)} collective-permute-done((f32[56,256]{1,0:T(8,128)S(1)}, f32[56,256]{1,0:T(8,128)S(1)}, u32[]{:S(2)}, u32[]{:S(2)}) %collective-permute-start.10) | collective-permute-done | bytes 57376 | tf_op jit(solution)/shard_map/ppermute | solution.py:41
  42.1 0.9 %collective-permute-done.11.refs_3_ = f32[56,256]{1,0:T(8,128)S(1)} collective-permute-done((f32[56,256]{1,0:T(8,128)S(1)}, f32[56,256]{1,0:T(8,128)S(1)}, u32[]{:S(2)}, u32[]{:S(2)}) %collective-permute-start.11) | collective-permute-done | bytes 57376 | tf_op jit(solution)/shard_map/ppermute | solution.py:41
  43.0 3.0 %shard_map.104 = (f32[64,16,256]{2,1,0:T(8,128)S(1)}, f32[272,256]{1,0:T(8,128)S(1)}, f32[256,256]{1,0:T(8,128)S(1)}) custom-call(f32[56,256]{1,0:T(8,128)S(1)} %get-tuple-element.56.refs_0_, f32[56,256]{1,0:T(8,128)S(1)} %collective-permute-done.9.refs_1_, f32[56,256]{1,0:T(8,128)S(1)} %collective-permute-done.10.refs_2_, ...), custom_call_target="tpu_custom_call" | custom-call | flops 1 | bytes 4575232 | tf_op jit(solution)/shard_map/pallas_call | solution.py:161
  46.1 0.8 %collective-permute-start.12 = (f32[272,256]{1,0:T(8,128)S(1)}, f32[272,256]{1,0:T(8,128)S(1)}, u32[]{:S(2)}, u32[]{:S(2)}) collective-permute-start(f32[272,256]{1,0:T(8,128)S(1)} %get-tuple-element.59), channel_id=1, source_target_pairs={{0,1},{1,0},{2,3},{3,2},{4,5},{5,4},{6,7},{7,6},{8,9},{9,8},{10,11... | collective-permute-start | bytes 835592 | tf_op jit(solution)/shard_map/ppermute | solution.py:33
  46.9 0.7 %collective-permute-start.13 = (f32[256,256]{1,0:T(8,128)S(1)}, f32[256,256]{1,0:T(8,128)S(1)}, u32[]{:S(2)}, u32[]{:S(2)}) collective-permute-start(f32[256,256]{1,0:T(8,128)S(1)} %get-tuple-element.60), channel_id=1, source_target_pairs={{1,2},{2,1},{3,4},{4,3},{5,6},{6,5},{9,10},{10,9},{11,12},{12,11},... | collective-permute-start | bytes 786440 | tf_op jit(solution)/shard_map/ppermute | solution.py:32
  48.1 6.2 %collective-permute-start.14 = (f32[16,128]{1,0:T(8,128)S(1)}, f32[16,128]{1,0:T(8,128)S(1)}, u32[]{:S(2)}, u32[]{:S(2)}) collective-permute-start(f32[16,128]{1,0:T(8,128)S(1)} %slice_add_fusion.refs_0_), channel_id=1, source_target_pairs={{0,6},{1,7},{2,4},{3,5},{4,2},{5,3},{6,0},{7,1},{8,14},{9,15},{10,... | collective-permute-start | bytes 24584 | tf_op jit(solution)/shard_map/ppermute | solution.py:41
  54.3 0.6 %collective-permute-start.16 = (f32[16,128]{1,0:T(8,128)S(1)}, f32[16,128]{1,0:T(8,128)S(1)}, u32[]{:S(2)}, u32[]{:S(2)}) collective-permute-start(f32[16,128]{1,0:T(8,128)S(1)} %slice_add_fusion.refs_0_), channel_id=1, source_target_pairs={{0,2},{1,3},{2,0},{3,1},{4,6},{5,7},{6,4},{7,5},{8,10},{9,11},{10,... | collective-permute-start | bytes 24584 | tf_op jit(solution)/shard_map/ppermute | solution.py:41
  54.9 1.4 %shard_map.105 = (f32[64,16,256]{2,1,0:T(8,128)}, f32[8,128]{1,0:T(8,128)S(1)}) custom-call(f32[64,16,256]{2,1,0:T(8,128)S(1)} %get-tuple-element.58.refs_0_, f32[272,256]{1,0:T(8,128)S(1)} %collective-permute-done.12.refs_1_, f32[256,256]{1,0:T(8,128)S(1)} %collective-permute-done.13.refs_2_, bf16[256,256]{1,0:T(8,128)(2,1)S(1)} %get-tuple-element.64.refs_0_.refs_3_), custom_call_target="tpu_custom_call" | custom-call | flops 1000000000 | bytes 1720320 | tf_op jit(solution)/shard_map/pallas_call | solution.py:161
  56.4 2.6 %collective-permute-done.14.refs_1_ = f32[16,128]{1,0:T(8,128)S(1)} collective-permute-done((f32[16,128]{1,0:T(8,128)S(1)}, f32[16,128]{1,0:T(8,128)S(1)}, u32[]{:S(2)}, u32[]{:S(2)}) %collective-permute-start.14) | collective-permute-done | bytes 8224 | tf_op jit(solution)/shard_map/ppermute | solution.py:41
  58.9 0.6 %shard_map.106 = f32[1,1]{1,0:T(1,128)} custom-call(f32[16,128]{1,0:T(8,128)S(1)} %slice_add_fusion.refs_0_, f32[16,128]{1,0:T(8,128)S(1)} %collective-permute-done.14.refs_1_, f32[16,128]{1,0:T(8,128)S(1)} %collective-permute-done.15.refs_2_, f32[16,128]{1,0:T(8,128)S(1)} %collective-permute-done.16.refs_3_, f32[8,128]{1,0:T(8,128)S(1)} %get-tuple-element.62.refs_4_), custom_call_target="tpu_custom_call" | custom-call | flops 1 | bytes 36864 | tf_op jit(solution)/shard_map/pallas_call | solution.py:161
  (28 shorter events, 2.7 us)
Async XLA Ops:
  3.1 6.3 %collective-permute-start = (f32[280,256]{1,0:T(8,128)}, f32[280,256]{1,0:T(8,128)S(1)}, u32[]{:S(2)}, u32[]{:S(2)}) collective-permute-start(f32[280,256]{1,0:T(8,128)} %get-tuple-element.35), channel_id=1, source_target_pairs={{0,1},{1,0},{2,3},{3,2},{4,5},{5,4},{6,7},{7,6},{8,9},{9,8},{10,11... | collective-permute-start | bytes 860168 | tf_op jit(solution)/shard_map/ppermute | solution.py:33
  3.6 5.8 %collective-permute-start.1 = (f32[280,256]{1,0:T(8,128)}, f32[280,256]{1,0:T(8,128)S(1)}, u32[]{:S(2)}, u32[]{:S(2)}) collective-permute-start(f32[280,256]{1,0:T(8,128)} %get-tuple-element.36), channel_id=1, source_target_pairs={{1,2},{2,1},{3,4},{4,3},{5,6},{6,5},{9,10},{10,9},{11,12},{12,11},... | collective-permute-start | bytes 860168 | tf_op jit(solution)/shard_map/ppermute | solution.py:32
  4.4 1.2 %copy-start = (f32[64,16,256]{2,1,0:T(8,128)S(1)}, f32[64,16,256]{2,1,0:T(8,128)}, u32[]{:S(2)}) copy-start(f32[64,16,256]{2,1,0:T(8,128)} %refs_0_.4) | copy-start | bytes 3145732
  5.6 1.4 %copy-start.1 = (bf16[3,64,16,256]{3,2,1,0:T(8,128)(2,1)S(1)}, bf16[3,64,16,256]{3,2,1,0:T(8,128)(2,1)}, u32[]{:S(2)}) copy-start(bf16[3,64,16,256]{3,2,1,0:T(8,128)(2,1)} %refs_2_.3) | copy-start | bytes 4718596
  7.0 0.8 %copy-start.4 = (f32[3,16,256]{2,1,0:T(8,128)S(1)}, f32[3,16,256]{2,1,0:T(8,128)}, u32[]{:S(2)}) copy-start(f32[3,16,256]{2,1,0:T(8,128)} %get-tuple-element.33.refs_1_) | copy-start | bytes 147460
  9.4 7.2 %copy-start.2 = (f32[3,16,256]{2,1,0:T(8,128)S(1)}, f32[3,16,256]{2,1,0:T(8,128)}, u32[]{:S(2)}) copy-start(f32[3,16,256]{2,1,0:T(8,128)} %refs_0_.5) | copy-start | bytes 147460
  9.4 7.2 %copy-start.3 = (f32[3,16,256]{2,1,0:T(8,128)S(1)}, f32[3,16,256]{2,1,0:T(8,128)}, u32[]{:S(2)}) copy-start(f32[3,16,256]{2,1,0:T(8,128)} %refs_1_.3) | copy-start | bytes 147460
  12.4 5.6 %collective-permute-start.2 = (f32[48,256]{1,0:T(8,128)S(1)}, f32[48,256]{1,0:T(8,128)S(1)}, u32[]{:S(2)}, u32[]{:S(2)}) collective-permute-start(f32[48,256]{1,0:T(8,128)S(1)} %get-tuple-element.40.refs_0_), channel_id=1, source_target_pairs={{0,24},{8,16},{16,8},{24,0},{1,25},{9,17},{17,9},{25,1},{2,26},{10... | collective-permute-start | bytes 147464 | tf_op jit(solution)/shard_map/ppermute | solution.py:41
  15.9 4.6 %collective-permute-start.3 = (f32[48,256]{1,0:T(8,128)S(1)}, f32[48,256]{1,0:T(8,128)S(1)}, u32[]{:S(2)}, u32[]{:S(2)}) collective-permute-start(f32[48,256]{1,0:T(8,128)S(1)} %get-tuple-element.40.refs_0_), channel_id=1, source_target_pairs={{0,16},{8,24},{16,0},{24,8},{1,17},{9,25},{17,1},{25,9},{2,18},{10... | collective-permute-start | bytes 147464 | tf_op jit(solution)/shard_map/ppermute | solution.py:41
  16.4 4.6 %collective-permute-start.4 = (f32[48,256]{1,0:T(8,128)S(1)}, f32[48,256]{1,0:T(8,128)S(1)}, u32[]{:S(2)}, u32[]{:S(2)}) collective-permute-start(f32[48,256]{1,0:T(8,128)S(1)} %get-tuple-element.40.refs_0_), channel_id=1, source_target_pairs={{0,8},{8,0},{16,24},{24,16},{1,9},{9,1},{17,25},{25,17},{2,10},{10... | collective-permute-start | bytes 147464 | tf_op jit(solution)/shard_map/ppermute | solution.py:41
  22.5 7.8 %collective-permute-start.6 = (f32[32,8,256]{2,1,0:T(8,128)S(1)}, f32[32,8,256]{2,1,0:T(8,128)S(1)}, u32[]{:S(2)}, u32[]{:S(2)}) collective-permute-start(f32[32,8,256]{2,1,0:T(8,128)S(1)} %get-tuple-element.47), channel_id=1, source_target_pairs={{1,2},{2,1},{3,4},{4,3},{5,6},{6,5},{9,10},{10,9},{11,12},{12,11},... | collective-permute-start | bytes 786440 | tf_op jit(solution)/shard_map/ppermute | solution.py:32
  23.2 10.1 %collective-permute-start.5 = (f32[32,8,256]{2,1,0:T(8,128)S(1)}, f32[32,8,256]{2,1,0:T(8,128)S(1)}, u32[]{:S(2)}, u32[]{:S(2)}) collective-permute-start(f32[32,8,256]{2,1,0:T(8,128)S(1)} %get-tuple-element.46), channel_id=1, source_target_pairs={{0,1},{1,0},{2,3},{3,2},{4,5},{5,4},{6,7},{7,6},{8,9},{9,8},{10,11... | collective-permute-start | bytes 786440 | tf_op jit(solution)/shard_map/ppermute | solution.py:33
  29.6 5.2 %collective-permute-start.8 = (f32[32,8,256]{2,1,0:T(8,128)S(1)}, f32[32,8,256]{2,1,0:T(8,128)S(1)}, u32[]{:S(2)}, u32[]{:S(2)}) collective-permute-start(f32[32,8,256]{2,1,0:T(8,128)S(1)} %get-tuple-element.52), channel_id=1, source_target_pairs={{1,2},{2,1},{3,4},{4,3},{5,6},{6,5},{9,10},{10,9},{11,12},{12,11},... | collective-permute-start | bytes 786440 | tf_op jit(solution)/shard_map/ppermute | solution.py:32
  30.3 4.5 %collective-permute-start.7 = (f32[32,8,256]{2,1,0:T(8,128)S(1)}, f32[32,8,256]{2,1,0:T(8,128)S(1)}, u32[]{:S(2)}, u32[]{:S(2)}) collective-permute-start(f32[32,8,256]{2,1,0:T(8,128)S(1)} %shard_map.101), channel_id=1, source_target_pairs={{0,1},{1,0},{2,3},{3,2},{4,5},{5,4},{6,7},{7,6},{8,9},{9,8},{10,11... | collective-permute-start | bytes 786440 | tf_op jit(solution)/shard_map/ppermute | solution.py:33
  36.4 5.1 %collective-permute-start.9 = (f32[56,256]{1,0:T(8,128)S(1)}, f32[56,256]{1,0:T(8,128)S(1)}, u32[]{:S(2)}, u32[]{:S(2)}) collective-permute-start(f32[56,256]{1,0:T(8,128)S(1)} %get-tuple-element.56.refs_0_), channel_id=1, source_target_pairs={{0,24},{8,16},{16,8},{24,0},{1,25},{9,17},{17,9},{25,1},{2,26},{10... | collective-permute-start | bytes 172040 | tf_op jit(solution)/shard_map/ppermute | solution.py:41
  37.9 4.2 %collective-permute-start.10 = (f32[56,256]{1,0:T(8,128)S(1)}, f32[56,256]{1,0:T(8,128)S(1)}, u32[]{:S(2)}, u32[]{:S(2)}) collective-permute-start(f32[56,256]{1,0:T(8,128)S(1)} %get-tuple-element.56.refs_0_), channel_id=1, source_target_pairs={{0,16},{8,24},{16,0},{24,8},{1,17},{9,25},{17,1},{25,9},{2,18},{10... | collective-permute-start | bytes 172040 | tf_op jit(solution)/shard_map/ppermute | solution.py:41
  38.5 4.5 %collective-permute-start.11 = (f32[56,256]{1,0:T(8,128)S(1)}, f32[56,256]{1,0:T(8,128)S(1)}, u32[]{:S(2)}, u32[]{:S(2)}) collective-permute-start(f32[56,256]{1,0:T(8,128)S(1)} %get-tuple-element.56.refs_0_), channel_id=1, source_target_pairs={{0,8},{8,0},{16,24},{24,16},{1,9},{9,1},{17,25},{25,17},{2,10},{10... | collective-permute-start | bytes 172040 | tf_op jit(solution)/shard_map/ppermute | solution.py:41
  46.1 2.0 %collective-permute-start.12 = (f32[272,256]{1,0:T(8,128)S(1)}, f32[272,256]{1,0:T(8,128)S(1)}, u32[]{:S(2)}, u32[]{:S(2)}) collective-permute-start(f32[272,256]{1,0:T(8,128)S(1)} %get-tuple-element.59), channel_id=1, source_target_pairs={{0,1},{1,0},{2,3},{3,2},{4,5},{5,4},{6,7},{7,6},{8,9},{9,8},{10,11... | collective-permute-start | bytes 835592 | tf_op jit(solution)/shard_map/ppermute | solution.py:33
  46.9 8.1 %collective-permute-start.13 = (f32[256,256]{1,0:T(8,128)S(1)}, f32[256,256]{1,0:T(8,128)S(1)}, u32[]{:S(2)}, u32[]{:S(2)}) collective-permute-start(f32[256,256]{1,0:T(8,128)S(1)} %get-tuple-element.60), channel_id=1, source_target_pairs={{1,2},{2,1},{3,4},{4,3},{5,6},{6,5},{9,10},{10,9},{11,12},{12,11},... | collective-permute-start | bytes 786440 | tf_op jit(solution)/shard_map/ppermute | solution.py:32
  48.1 10.9 %collective-permute-start.14 = (f32[16,128]{1,0:T(8,128)S(1)}, f32[16,128]{1,0:T(8,128)S(1)}, u32[]{:S(2)}, u32[]{:S(2)}) collective-permute-start(f32[16,128]{1,0:T(8,128)S(1)} %slice_add_fusion.refs_0_), channel_id=1, source_target_pairs={{0,6},{1,7},{2,4},{3,5},{4,2},{5,3},{6,0},{7,1},{8,14},{9,15},{10,... | collective-permute-start | bytes 24584 | tf_op jit(solution)/shard_map/ppermute | solution.py:41
  54.3 4.6 %collective-permute-start.15 = (f32[16,128]{1,0:T(8,128)S(1)}, f32[16,128]{1,0:T(8,128)S(1)}, u32[]{:S(2)}, u32[]{:S(2)}) collective-permute-start(f32[16,128]{1,0:T(8,128)S(1)} %slice_add_fusion.refs_0_), channel_id=1, source_target_pairs={{0,4},{1,5},{2,6},{3,7},{4,0},{5,1},{6,2},{7,3},{8,12},{9,13},{10,... | collective-permute-start | bytes 24584 | tf_op jit(solution)/shard_map/ppermute | solution.py:41
  54.3 4.6 %collective-permute-start.16 = (f32[16,128]{1,0:T(8,128)S(1)}, f32[16,128]{1,0:T(8,128)S(1)}, u32[]{:S(2)}, u32[]{:S(2)}) collective-permute-start(f32[16,128]{1,0:T(8,128)S(1)} %slice_add_fusion.refs_0_), channel_id=1, source_target_pairs={{0,2},{1,3},{2,0},{3,1},{4,6},{5,7},{6,4},{7,5},{8,10},{9,11},{10,... | collective-permute-start | bytes 24584 | tf_op jit(solution)/shard_map/ppermute | solution.py:41
